TPU v7x, 128 devices: a whole 4x4x4 slice. The times are simulated.
128 devices in a mesh: rows: 2 (over core), cols: 8 (over z, x_lo), slabs: 8 (over y, x_hi).
Axes of the slice: x: 4 (x_hi: 2, x_lo: 2; x = x_hi * 2 + x_lo), y: 4, z: 4, core: 2. Of those that a mesh axis runs over, the one named last changes fastest.
Arguments:
- density: float32 [32, 768, 64, 128], P('rows', 'cols', 'slabs'), may hold values from 0.5 to 2
- flow_j: float32 [32, 768, 64, 128], P('rows', 'cols', 'slabs'), may hold values from -0.3 to 0.3
- flow_i: float32 [32, 768, 64, 128], P('rows', 'cols', 'slabs'), may hold values from -0.3 to 0.3
- flow_k: float32 [32, 768, 64, 128], P('rows', 'cols', 'slabs'), may hold values from -0.3 to 0.3
Outputs:
- anomaly: float32 [32, 768, 64, 128], P('rows', 'cols', 'slabs')
- density_end: float32 [32, 768, 64, 128], P('rows', 'cols', 'slabs')
All inputs are finite; a program needn't handle non-finite values.
Results may differ from a plain program's by a relative error of at most 0.00002.
Values sent between devices are 32-bit elements; how exact they have to be, the bound alone decides.
No kernel may reach another device: no remote copies, remote signals or barrier semaphores. Data moves between devices by JAX's collectives and lax.ppermute only.
A program may use at most 128 MiB of HBM per device.

v0:
```python
import jax
import jax.numpy as jnp
from jax import lax
from jax.sharding import PartitionSpec as P

STEPS = 6


def with_halo(value, sides, width):
    edges = {}
    for axis, dim in sides:
        size, length = (lax.axis_size(axis), value.shape[dim])
        up = [(i, (i + 1) % size) for i in range(size - 1)]
        last = lax.slice_in_dim(value, length - width, length, axis=dim)
        first = lax.slice_in_dim(value, 0, width, axis=dim)
        edges[dim] = (
            lax.ppermute(last, axis, up),
            lax.ppermute(first, axis, [(b, a) for a, b in up]),
        )
    done = []
    for _, dim in sides:
        low, high = edges[dim]
        around = [(width, width) if d in done else (0, 0) for d in range(value.ndim)]
        value = jnp.concatenate([jnp.pad(low, around), value, jnp.pad(high, around)], axis=dim)
        done.append(dim)
    return value


def inner_cells(values, dims):
    for dim in dims:
        values = lax.slice_in_dim(values, 1, values.shape[dim] - 1, axis=dim)
    return values


def side_cells(values, dim, start, dims):
    others = [other for other in dims if other != dim]
    values = inner_cells(values, others)
    return lax.slice_in_dim(values, start, start + values.shape[dim] - 2, axis=dim)


def advance(padded, flow_j, flow_i, flow_k):
    middle = inner_cells(padded, (0, 1, 2))
    lower = [side_cells(padded, dim, 0, (0, 1, 2)) for dim in (0, 1, 2)]
    upper = [side_cells(padded, dim, 2, (0, 1, 2)) for dim in (0, 1, 2)]
    slopes = [above - below for above, below in zip(upper, lower)]
    smooth_rate = 0.05
    spread = lower[0] + upper[0] + lower[1] + upper[1] + lower[2] + upper[2] - 6.0 * middle
    return (
        middle - flow_j * slopes[0] - flow_i * slopes[1] - flow_k * slopes[2] + smooth_rate * spread
    )


def body(density, flow_j, flow_i, flow_k):
    for step in range(STEPS):
        padded = with_halo(density, (("rows", 0), ("cols", 1), ("slabs", 2)), 1)
        density = advance(padded, flow_j, flow_i, flow_k)
    count = density.shape[2] * lax.axis_size("slabs")
    guess = 1.0
    moved = density - guess
    totals, squares = lax.psum(
        (jnp.sum(moved, axis=2, keepdims=True), jnp.sum(moved * moved, axis=2, keepdims=True)),
        "slabs",
    )
    line_mean = guess + totals / count
    centred = density - line_mean
    line_variance = squares / count - totals / count * (totals / count)
    anomaly = centred * lax.rsqrt(line_variance + 0.0001)
    return (anomaly, density)


def solution(mesh):
    placed = (
        P("rows", "cols", "slabs", None),
        P("rows", "cols", "slabs", None),
        P("rows", "cols", "slabs", None),
        P("rows", "cols", "slabs", None),
    )
    return jax.shard_map(
        body,
        mesh=mesh,
        in_specs=placed,
        out_specs=(P("rows", "cols", "slabs", None), P("rows", "cols", "slabs", None)),
        check_vma=False,
    )
```

profile of v0, /device:TPU:0, one launch (start us, length us, event | category | flops | bytes accessed | tf_op | source)
XLA Modules:
  0.0 556.2 jit_solution(4195282195116643130)
XLA Ops:
  15.9 4.6 collective-permute-start.3
  22.0 6.1 %collective-permute-start.5 = (f32[16,96,1,128]{3,1,2,0:T(8,128)S(1)}, f32[16,96,1,128]{3,1,2,0:T(8,128)S(1)}, u32[]{:S(2)}, u32[]{:S(2)}) collective-permute-start(f32[16,96,1,128]{3,1,2,0:T(8,128)S(1)} %get-tuple-element.39), channel_id=1, source_target_pairs={{0,1},{1,2},{2,3},{3,4},{4,5},{5,6},{6,7},{8,9},{9,10},{10,11},{11... | collective-permute-start | bytes 2359304 | tf_op jit(solution)/shard_map/ppermute | solution.py:17
  33.9 10.6 %collective-permute-done.4 = f32[16,96,1,128]{3,1,2,0:T(8,128)S(1)} collective-permute-done((f32[16,96,1,128]{3,1,2,0:T(8,128)S(1)}, f32[16,96,1,128]{3,1,2,0:T(8,128)S(1)}, u32[]{:S(2)}, u32[]{:S(2)}) %collective-permute-start.4) | collective-permute-done | bytes 786464 | tf_op jit(solution)/shard_map/ppermute | solution.py:18
  45.6 22.0 %multiply_add_fusion.5 = f32[16,96,8,128]{3,1,2,0:T(8,128)} fusion(f32[16,96,8,128]{3,1,2,0:T(8,128)} %copy-done, f32[16,96,1,128]{3,1,2,0:T(8,128)S(1)} %collective-permute-done.4, f32[18,1,8,128]{3,1,2,0:T(1,128)S(1)} %pad.74, f32[18,96,8,128]{3,1,2,0:T(8,128)} %constant_dynamic-update-slice_fusion, f32[18,1,8,128]{3,1,2,0:T(1,128)S(1)} %pad.75, ...), kind=kLoop, calls=%fused_computation.121 | loop fusion | flops 53477376 | bytes 41041920 | tf_op jit(solution)/shard_map/add | solution.py:49
  70.4 17.8 %collective-permute-start.11 = (f32[16,96,1,128]{3,1,2,0:T(8,128)S(1)}, f32[16,96,1,128]{3,1,2,0:T(8,128)S(1)}, u32[]{:S(2)}, u32[]{:S(2)}) collective-permute-start(f32[16,96,1,128]{3,1,2,0:T(8,128)S(1)} %get-tuple-element.33), channel_id=1, source_target_pairs={{0,1},{1,2},{2,3},{3,4},{4,5},{5,6},{6,7},{8,9},{9,10},{10,11},{11... | collective-permute-start | bytes 2359304 | tf_op jit(solution)/shard_map/ppermute | solution.py:17
  96.4 12.9 %collective-permute-done.8 = f32[16,1,8,128]{3,1,2,0:T(1,128)S(1)} collective-permute-done((f32[16,1,8,128]{3,1,2,0:T(1,128)S(1)}, f32[16,1,8,128]{3,1,2,0:T(1,128)S(1)}, u32[]{:S(2)}, u32[]{:S(2)}) %collective-permute-start.8) | collective-permute-done | bytes 65568 | tf_op jit(solution)/shard_map/ppermute | solution.py:18
  114.2 25.4 %multiply_add_fusion.4 = f32[16,96,8,128]{3,1,2,0:T(8,128)} fusion(f32[16,96,8,128]{3,1,2,0:T(8,128)} %multiply_add_fusion.5, f32[16,96,1,128]{3,1,2,0:T(8,128)S(1)} %collective-permute-done.10, f32[18,1,8,128]{3,1,2,0:T(1,128)S(1)} %pad.78, f32[1,96,8,128]{3,1,2,0:T(8,128)S(1)} %collective-permute-done.6, f32[1,96,8,128]{3,1,2,0:T(8,128)S(1)} %collective-permute-done.7, ...), kind=kLoop, calls=%fused_computation.120 | loop fusion | flops 66060288 | bytes 33964032 | tf_op jit(solution)/shard_map/add | solution.py:49
  142.3 17.8 %collective-permute-start.17 = (f32[16,96,1,128]{3,1,2,0:T(8,128)S(1)}, f32[16,96,1,128]{3,1,2,0:T(8,128)S(1)}, u32[]{:S(2)}, u32[]{:S(2)}) collective-permute-start(f32[16,96,1,128]{3,1,2,0:T(8,128)S(1)} %get-tuple-element.27), channel_id=1, source_target_pairs={{0,1},{1,2},{2,3},{3,4},{4,5},{5,6},{6,7},{8,9},{9,10},{10,11},{11... | collective-permute-start | bytes 2359304 | tf_op jit(solution)/shard_map/ppermute | solution.py:17
  168.3 11.0 %collective-permute-done.14 = f32[16,1,8,128]{3,1,2,0:T(1,128)S(1)} collective-permute-done((f32[16,1,8,128]{3,1,2,0:T(1,128)S(1)}, f32[16,1,8,128]{3,1,2,0:T(1,128)S(1)}, u32[]{:S(2)}, u32[]{:S(2)}) %collective-permute-start.14) | collective-permute-done | bytes 65568 | tf_op jit(solution)/shard_map/ppermute | solution.py:18
  179.3 5.5 collective-permute-start.15
  186.7 25.1 %multiply_add_fusion.3 = f32[16,96,8,128]{3,1,2,0:T(8,128)} fusion(f32[16,96,8,128]{3,1,2,0:T(8,128)} %multiply_add_fusion.4, f32[16,96,1,128]{3,1,2,0:T(8,128)S(1)} %collective-permute-done.16, f32[18,1,8,128]{3,1,2,0:T(1,128)S(1)} %pad.82, f32[1,96,8,128]{3,1,2,0:T(8,128)S(1)} %collective-permute-done.12, ...), kind=kLoop, calls=%fused_computation.119 | loop fusion | flops 66060288 | bytes 33964032 | tf_op jit(solution)/shard_map/add | solution.py:49
  214.6 17.8 %collective-permute-start.23 = (f32[16,96,1,128]{3,1,2,0:T(8,128)S(1)}, f32[16,96,1,128]{3,1,2,0:T(8,128)S(1)}, u32[]{:S(2)}, u32[]{:S(2)}) collective-permute-start(f32[16,96,1,128]{3,1,2,0:T(8,128)S(1)} %get-tuple-element.21), channel_id=1, source_target_pairs={{0,1},{1,2},{2,3},{3,4},{4,5},{5,6},{6,7},{8,9},{9,10},{10,11},{11... | collective-permute-start | bytes 2359304 | tf_op jit(solution)/shard_map/ppermute | solution.py:17
  240.6 8.0 %collective-permute-done.20 = f32[16,1,8,128]{3,1,2,0:T(1,128)S(1)} collective-permute-done((f32[16,1,8,128]{3,1,2,0:T(1,128)S(1)}, f32[16,1,8,128]{3,1,2,0:T(1,128)S(1)}, u32[]{:S(2)}, u32[]{:S(2)}) %collective-permute-start.20) | collective-permute-done | bytes 65568 | tf_op jit(solution)/shard_map/ppermute | solution.py:18
  254.7 25.4 %multiply_add_fusion.2 = f32[16,96,8,128]{3,1,2,0:T(8,128)} fusion(f32[16,96,8,128]{3,1,2,0:T(8,128)} %multiply_add_fusion.3, f32[16,96,1,128]{3,1,2,0:T(8,128)S(1)} %collective-permute-done.22, f32[18,1,8,128]{3,1,2,0:T(1,128)S(1)} %pad.86, f32[1,96,8,128]{3,1,2,0:T(8,128)S(1)} %collective-permute-done.18, ...), kind=kLoop, calls=%fused_computation.118 | loop fusion | flops 66060288 | bytes 33964032 | tf_op jit(solution)/shard_map/add | solution.py:49
  282.9 17.8 %collective-permute-start.29 = (f32[16,96,1,128]{3,1,2,0:T(8,128)S(1)}, f32[16,96,1,128]{3,1,2,0:T(8,128)S(1)}, u32[]{:S(2)}, u32[]{:S(2)}) collective-permute-start(f32[16,96,1,128]{3,1,2,0:T(8,128)S(1)} %get-tuple-element.15), channel_id=1, source_target_pairs={{0,1},{1,2},{2,3},{3,4},{4,5},{5,6},{6,7},{8,9},{9,10},{10,11},{11... | collective-permute-start | bytes 2359304 | tf_op jit(solution)/shard_map/ppermute | solution.py:17
  308.9 6.3 %collective-permute-done.26 = f32[16,1,8,128]{3,1,2,0:T(1,128)S(1)} collective-permute-done((f32[16,1,8,128]{3,1,2,0:T(1,128)S(1)}, f32[16,1,8,128]{3,1,2,0:T(1,128)S(1)}, u32[]{:S(2)}, u32[]{:S(2)}) %collective-permute-start.26) | collective-permute-done | bytes 65568 | tf_op jit(solution)/shard_map/ppermute | solution.py:18
  315.2 4.9 collective-permute-start.27
  322.0 25.1 %multiply_add_fusion.1 = f32[16,96,8,128]{3,1,2,0:T(8,128)} fusion(f32[16,96,8,128]{3,1,2,0:T(8,128)} %multiply_add_fusion.2, f32[16,96,1,128]{3,1,2,0:T(8,128)S(1)} %collective-permute-done.28, f32[18,1,8,128]{3,1,2,0:T(1,128)S(1)} %pad.90, f32[1,96,8,128]{3,1,2,0:T(8,128)S(1)} %collective-permute-done.24, ...), kind=kLoop, calls=%fused_computation.117 | loop fusion | flops 66060288 | bytes 33964032 | tf_op jit(solution)/shard_map/add | solution.py:49
  349.9 18.5 %collective-permute-start.35 = (f32[16,96,1,128]{3,1,2,0:T(8,128)S(1)}, f32[16,96,1,128]{3,1,2,0:T(8,128)S(1)}, u32[]{:S(2)}, u32[]{:S(2)}) collective-permute-start(f32[16,96,1,128]{3,1,2,0:T(8,128)S(1)} %get-tuple-element.10), channel_id=1, source_target_pairs={{0,1},{1,2},{2,3},{3,4},{4,5},{5,6},{6,7},{8,9},{9,10},{10,11},{11... | collective-permute-start | bytes 2359304 | tf_op jit(solution)/shard_map/ppermute | solution.py:17
  376.6 4.9 collective-permute-done.32
  389.3 29.2 %add_reduce_fusion = (f32[16,96,128]{2,1,0:T(8,128)}, f32[16,96,128]{2,1,0:T(8,128)}, f32[16,96,8,128]{3,1,2,0:T(8,128)}) fusion(f32[16,96,8,128]{3,1,2,0:T(8,128)} %multiply_add_fusion.1, f32[18,1,8,128]{3,1,2,0:T(1,128)S(1)} %pad.94, f32[1,96,8,128]{3,1,2,0:T(8,128)S(1)} %collective-permute-done.30, f32[1,96,8,128]{3,1,2,0:T(8,128)} %copy-done.2, ...), kind=kLoop, calls=%fused_computation.122 | loop fusion | flops 71958528 | bytes 35536896 | tf_op jit(solution)/shard_map/reduce_sum | solution.py:61
  418.5 10.4 %copy.36 = f32[16,96,8,128]{3,2,1,0:T(8,128)} copy(f32[16,96,8,128]{3,1,2,0:T(8,128)} %get-tuple-element.8) | data formatting | bytes 12582912
  428.9 107.5 %all-reduce.27.cloned.1.call-done = (f32[16,96,1,128]{3,1,0,2:T(8,128)}, f32[16,96,1,128]{3,1,0,2:T(8,128)}) async-done(((f32[16,96,1,128]{3,1,0,2:T(8,128)}, f32[16,96,1,128]{3,1,0,2:T(8,128)}), (f32[16,96,1,128]{3,1,0,2:T(8,128)}, f32[16,96,1,128]{3,1,0,2:T(8,128)})) %all-reduce.27.cloned.1.call-update) | async-done | bytes 1572880 | tf_op jit(solution)/shard_map/psum | solution.py:60
  541.6 7.6 %copy.35 = f32[16,96,8,128]{3,2,1,0:T(8,128)} copy(f32[16,96,8,128]{3,1,2,0:T(8,128)S(1)} %subtract_multiply_fusion) | data formatting | bytes 12582912
  (111 shorter events, 99.3 us)
Async XLA Ops:
  7.2 529.2 %all-reduce.27.cloned.1.call-start = ((), (), s32[]{:S(2)}) async-start(), calls=%async_computation | async-start | bytes 3145728 | tf_op jit(solution)/shard_map/psum | solution.py:60
  12.9 20.2 %collective-permute-start = (f32[1,96,8,128]{3,1,2,0:T(8,128)S(1)}, f32[1,96,8,128]{3,1,2,0:T(8,128)S(1)}, u32[]{:S(2)}, u32[]{:S(2)}) collective-permute-start(f32[1,96,8,128]{3,1,2,0:T(8,128)S(1)} %get-tuple-element.43), channel_id=1, source_target_pairs={{64,0},{65,1},{66,2},{67,3},{68,4},{69,5},{70,6},{71,7},{72,8},{73... | collective-permute-start | bytes 1179656 | tf_op jit(solution)/shard_map/ppermute | solution.py:18
  20.7 23.8 %collective-permute-start.4 = (f32[16,96,1,128]{3,1,2,0:T(8,128)S(1)}, f32[16,96,1,128]{3,1,2,0:T(8,128)S(1)}, u32[]{:S(2)}, u32[]{:S(2)}) collective-permute-start(f32[16,96,1,128]{3,1,2,0:T(8,128)S(1)} %get-tuple-element.40), channel_id=1, source_target_pairs={{1,0},{2,1},{3,2},{4,3},{5,4},{6,5},{7,6},{9,8},{10,9},{11,10},{12... | collective-permute-start | bytes 2359304 | tf_op jit(solution)/shard_map/ppermute | solution.py:18
  22.0 23.6 %collective-permute-start.5 = (f32[16,96,1,128]{3,1,2,0:T(8,128)S(1)}, f32[16,96,1,128]{3,1,2,0:T(8,128)S(1)}, u32[]{:S(2)}, u32[]{:S(2)}) collective-permute-start(f32[16,96,1,128]{3,1,2,0:T(8,128)S(1)} %get-tuple-element.39), channel_id=1, source_target_pairs={{0,1},{1,2},{2,3},{3,4},{4,5},{5,6},{6,7},{8,9},{9,10},{10,11},{11... | collective-permute-start | bytes 2359304 | tf_op jit(solution)/shard_map/ppermute | solution.py:17
  69.1 45.0 %collective-permute-start.10 = (f32[16,96,1,128]{3,1,2,0:T(8,128)S(1)}, f32[16,96,1,128]{3,1,2,0:T(8,128)S(1)}, u32[]{:S(2)}, u32[]{:S(2)}) collective-permute-start(f32[16,96,1,128]{3,1,2,0:T(8,128)S(1)} %get-tuple-element.34), channel_id=1, source_target_pairs={{1,0},{2,1},{3,2},{4,3},{5,4},{6,5},{7,6},{9,8},{10,9},{11,10},{12... | collective-permute-start | bytes 2359304 | tf_op jit(solution)/shard_map/ppermute | solution.py:18
  70.4 43.8 %collective-permute-start.11 = (f32[16,96,1,128]{3,1,2,0:T(8,128)S(1)}, f32[16,96,1,128]{3,1,2,0:T(8,128)S(1)}, u32[]{:S(2)}, u32[]{:S(2)}) collective-permute-start(f32[16,96,1,128]{3,1,2,0:T(8,128)S(1)} %get-tuple-element.33), channel_id=1, source_target_pairs={{0,1},{1,2},{2,3},{3,4},{4,5},{5,6},{6,7},{8,9},{9,10},{10,11},{11... | collective-permute-start | bytes 2359304 | tf_op jit(solution)/shard_map/ppermute | solution.py:17
  89.4 24.8 %collective-permute-start.6 = (f32[1,96,8,128]{3,1,2,0:T(8,128)S(1)}, f32[1,96,8,128]{3,1,2,0:T(8,128)S(1)}, u32[]{:S(2)}, u32[]{:S(2)}) collective-permute-start(f32[1,96,8,128]{3,1,2,0:T(8,128)S(1)} %get-tuple-element.38), channel_id=1, source_target_pairs={{64,0},{65,1},{66,2},{67,3},{68,4},{69,5},{70,6},{71,7},{72,8},{73... | collective-permute-start | bytes 1179656 | tf_op jit(solution)/shard_map/ppermute | solution.py:18
  90.7 23.5 %collective-permute-start.7 = (f32[1,96,8,128]{3,1,2,0:T(8,128)S(1)}, f32[1,96,8,128]{3,1,2,0:T(8,128)S(1)}, u32[]{:S(2)}, u32[]{:S(2)}) collective-permute-start(f32[1,96,8,128]{3,1,2,0:T(8,128)S(1)} %get-tuple-element.37), channel_id=1, source_target_pairs={{0,64},{1,65},{2,66},{3,67},{4,68},{5,69},{6,70},{7,71},{8,72},{9,... | collective-permute-start | bytes 1179656 | tf_op jit(solution)/shard_map/ppermute | solution.py:17
  141.0 45.7 %collective-permute-start.16 = (f32[16,96,1,128]{3,1,2,0:T(8,128)S(1)}, f32[16,96,1,128]{3,1,2,0:T(8,128)S(1)}, u32[]{:S(2)}, u32[]{:S(2)}) collective-permute-start(f32[16,96,1,128]{3,1,2,0:T(8,128)S(1)} %get-tuple-element.28), channel_id=1, source_target_pairs={{1,0},{2,1},{3,2},{4,3},{5,4},{6,5},{7,6},{9,8},{10,9},{11,10},{12... | collective-permute-start | bytes 2359304 | tf_op jit(solution)/shard_map/ppermute | solution.py:18
  142.3 44.4 %collective-permute-start.17 = (f32[16,96,1,128]{3,1,2,0:T(8,128)S(1)}, f32[16,96,1,128]{3,1,2,0:T(8,128)S(1)}, u32[]{:S(2)}, u32[]{:S(2)}) collective-permute-start(f32[16,96,1,128]{3,1,2,0:T(8,128)S(1)} %get-tuple-element.27), channel_id=1, source_target_pairs={{0,1},{1,2},{2,3},{3,4},{4,5},{5,6},{6,7},{8,9},{9,10},{10,11},{11... | collective-permute-start | bytes 2359304 | tf_op jit(solution)/shard_map/ppermute | solution.py:17
  161.3 25.4 %collective-permute-start.12 = (f32[1,96,8,128]{3,1,2,0:T(8,128)S(1)}, f32[1,96,8,128]{3,1,2,0:T(8,128)S(1)}, u32[]{:S(2)}, u32[]{:S(2)}) collective-permute-start(f32[1,96,8,128]{3,1,2,0:T(8,128)S(1)} %get-tuple-element.32), channel_id=1, source_target_pairs={{64,0},{65,1},{66,2},{67,3},{68,4},{69,5},{70,6},{71,7},{72,8},{73... | collective-permute-start | bytes 1179656 | tf_op jit(solution)/shard_map/ppermute | solution.py:18
  162.6 24.1 %collective-permute-start.13 = (f32[1,96,8,128]{3,1,2,0:T(8,128)S(1)}, f32[1,96,8,128]{3,1,2,0:T(8,128)S(1)}, u32[]{:S(2)}, u32[]{:S(2)}) collective-permute-start(f32[1,96,8,128]{3,1,2,0:T(8,128)S(1)} %get-tuple-element.31), channel_id=1, source_target_pairs={{0,64},{1,65},{2,66},{3,67},{4,68},{5,69},{6,70},{7,71},{8,72},{9,... | collective-permute-start | bytes 1179656 | tf_op jit(solution)/shard_map/ppermute | solution.py:17
  213.3 41.4 %collective-permute-start.22 = (f32[16,96,1,128]{3,1,2,0:T(8,128)S(1)}, f32[16,96,1,128]{3,1,2,0:T(8,128)S(1)}, u32[]{:S(2)}, u32[]{:S(2)}) collective-permute-start(f32[16,96,1,128]{3,1,2,0:T(8,128)S(1)} %get-tuple-element.22), channel_id=1, source_target_pairs={{1,0},{2,1},{3,2},{4,3},{5,4},{6,5},{7,6},{9,8},{10,9},{11,10},{12... | collective-permute-start | bytes 2359304 | tf_op jit(solution)/shard_map/ppermute | solution.py:18
  214.6 40.1 %collective-permute-start.23 = (f32[16,96,1,128]{3,1,2,0:T(8,128)S(1)}, f32[16,96,1,128]{3,1,2,0:T(8,128)S(1)}, u32[]{:S(2)}, u32[]{:S(2)}) collective-permute-start(f32[16,96,1,128]{3,1,2,0:T(8,128)S(1)} %get-tuple-element.21), channel_id=1, source_target_pairs={{0,1},{1,2},{2,3},{3,4},{4,5},{5,6},{6,7},{8,9},{9,10},{10,11},{11... | collective-permute-start | bytes 2359304 | tf_op jit(solution)/shard_map/ppermute | solution.py:17
  233.6 21.1 %collective-permute-start.18 = (f32[1,96,8,128]{3,1,2,0:T(8,128)S(1)}, f32[1,96,8,128]{3,1,2,0:T(8,128)S(1)}, u32[]{:S(2)}, u32[]{:S(2)}) collective-permute-start(f32[1,96,8,128]{3,1,2,0:T(8,128)S(1)} %get-tuple-element.26), channel_id=1, source_target_pairs={{64,0},{65,1},{66,2},{67,3},{68,4},{69,5},{70,6},{71,7},{72,8},{73... | collective-permute-start | bytes 1179656 | tf_op jit(solution)/shard_map/ppermute | solution.py:18
  234.9 19.8 %collective-permute-start.19 = (f32[1,96,8,128]{3,1,2,0:T(8,128)S(1)}, f32[1,96,8,128]{3,1,2,0:T(8,128)S(1)}, u32[]{:S(2)}, u32[]{:S(2)}) collective-permute-start(f32[1,96,8,128]{3,1,2,0:T(8,128)S(1)} %get-tuple-element.25), channel_id=1, source_target_pairs={{0,64},{1,65},{2,66},{3,67},{4,68},{5,69},{6,70},{7,71},{8,72},{9,... | collective-permute-start | bytes 1179656 | tf_op jit(solution)/shard_map/ppermute | solution.py:17
  281.6 40.4 %collective-permute-start.28 = (f32[16,96,1,128]{3,1,2,0:T(8,128)S(1)}, f32[16,96,1,128]{3,1,2,0:T(8,128)S(1)}, u32[]{:S(2)}, u32[]{:S(2)}) collective-permute-start(f32[16,96,1,128]{3,1,2,0:T(8,128)S(1)} %get-tuple-element.16), channel_id=1, source_target_pairs={{1,0},{2,1},{3,2},{4,3},{5,4},{6,5},{7,6},{9,8},{10,9},{11,10},{12... | collective-permute-start | bytes 2359304 | tf_op jit(solution)/shard_map/ppermute | solution.py:18
  282.9 39.1 %collective-permute-start.29 = (f32[16,96,1,128]{3,1,2,0:T(8,128)S(1)}, f32[16,96,1,128]{3,1,2,0:T(8,128)S(1)}, u32[]{:S(2)}, u32[]{:S(2)}) collective-permute-start(f32[16,96,1,128]{3,1,2,0:T(8,128)S(1)} %get-tuple-element.15), channel_id=1, source_target_pairs={{0,1},{1,2},{2,3},{3,4},{4,5},{5,6},{6,7},{8,9},{9,10},{10,11},{11... | collective-permute-start | bytes 2359304 | tf_op jit(solution)/shard_map/ppermute | solution.py:17
  301.9 20.1 %collective-permute-start.24 = (f32[1,96,8,128]{3,1,2,0:T(8,128)S(1)}, f32[1,96,8,128]{3,1,2,0:T(8,128)S(1)}, u32[]{:S(2)}, u32[]{:S(2)}) collective-permute-start(f32[1,96,8,128]{3,1,2,0:T(8,128)S(1)} %get-tuple-element.20), channel_id=1, source_target_pairs={{64,0},{65,1},{66,2},{67,3},{68,4},{69,5},{70,6},{71,7},{72,8},{73... | collective-permute-start | bytes 1179656 | tf_op jit(solution)/shard_map/ppermute | solution.py:18
  303.2 18.8 %collective-permute-start.25 = (f32[1,96,8,128]{3,1,2,0:T(8,128)S(1)}, f32[1,96,8,128]{3,1,2,0:T(8,128)S(1)}, u32[]{:S(2)}, u32[]{:S(2)}) collective-permute-start(f32[1,96,8,128]{3,1,2,0:T(8,128)S(1)} %get-tuple-element.19), channel_id=1, source_target_pairs={{0,64},{1,65},{2,66},{3,67},{4,68},{5,69},{6,70},{7,71},{8,72},{9,... | collective-permute-start | bytes 1179656 | tf_op jit(solution)/shard_map/ppermute | solution.py:17
  348.6 40.0 %collective-permute-start.34 = (f32[16,96,1,128]{3,1,2,0:T(8,128)S(1)}, f32[16,96,1,128]{3,1,2,0:T(8,128)S(1)}, u32[]{:S(2)}, u32[]{:S(2)}) collective-permute-start(f32[16,96,1,128]{3,1,2,0:T(8,128)S(1)} %get-tuple-element.9), channel_id=1, source_target_pairs={{1,0},{2,1},{3,2},{4,3},{5,4},{6,5},{7,6},{9,8},{10,9},{11,10},{12... | collective-permute-start | bytes 2359304 | tf_op jit(solution)/shard_map/ppermute | solution.py:18
  349.9 39.4 %collective-permute-start.35 = (f32[16,96,1,128]{3,1,2,0:T(8,128)S(1)}, f32[16,96,1,128]{3,1,2,0:T(8,128)S(1)}, u32[]{:S(2)}, u32[]{:S(2)}) collective-permute-start(f32[16,96,1,128]{3,1,2,0:T(8,128)S(1)} %get-tuple-element.10), channel_id=1, source_target_pairs={{0,1},{1,2},{2,3},{3,4},{4,5},{5,6},{6,7},{8,9},{9,10},{10,11},{11... | collective-permute-start | bytes 2359304 | tf_op jit(solution)/shard_map/ppermute | solution.py:17
  369.6 19.0 %collective-permute-start.30 = (f32[1,96,8,128]{3,1,2,0:T(8,128)S(1)}, f32[1,96,8,128]{3,1,2,0:T(8,128)S(1)}, u32[]{:S(2)}, u32[]{:S(2)}) collective-permute-start(f32[1,96,8,128]{3,1,2,0:T(8,128)S(1)} %get-tuple-element.14), channel_id=1, source_target_pairs={{64,0},{65,1},{66,2},{67,3},{68,4},{69,5},{70,6},{71,7},{72,8},{73... | collective-permute-start | bytes 1179656 | tf_op jit(solution)/shard_map/ppermute | solution.py:18
  370.9 17.7 %collective-permute-start.31 = (f32[1,96,8,128]{3,1,2,0:T(8,128)S(1)}, f32[1,96,8,128]{3,1,2,0:T(8,128)S(1)}, u32[]{:S(2)}, u32[]{:S(2)}) collective-permute-start(f32[1,96,8,128]{3,1,2,0:T(8,128)S(1)} %get-tuple-element.13), channel_id=1, source_target_pairs={{0,64},{1,65},{2,66},{3,67},{4,68},{5,69},{6,70},{7,71},{8,72},{9,... | collective-permute-start | bytes 1179656 | tf_op jit(solution)/shard_map/ppermute | solution.py:17
  (20 other events, 232.2 us)
Sparse Core Ops, SparseCore 0:
  418.6 117.6 all-reduce.26
where the time goes:
time: 563 us; the launch traced here: 556 us
  waiting for transfers between devices  171 us (30%)
  starting transfers between devices  163 us (29%)
  other arithmetic  157 us (28%)
  local copies, waits for them, and re-layouts  49.5 us (9%)
  between operations  14.9 us (3%)
    ppermute x18, starting transfers between devices, with_halo(): lax.ppermute(last, axis, up)  140 us
    add x5, other arithmetic, advance(): middle - flow_j * slopes[0] - flow_i * slopes[1] - flow_k * slopes[2]  123 us
    psum x1, waiting for transfers between devices, body(): lax.psum((jnp.sum(moved, axis=2, keepdims=True), jnp.sum(moved * moved, a...  107 us
    ppermute x18, waiting for transfers between devices, with_halo(): lax.ppermute(first, axis, [(b, a) for a, b in up])  53.8 us
    reduce_sum x1, other arithmetic, body(): jnp.sum(moved, axis=2, keepdims=True)  29.2 us
    unnamed x19, local copies, waits for them, and re-layouts  27.5 us
    ppermute x18, starting transfers between devices, with_halo(): lax.ppermute(first, axis, [(b, a) for a, b in up])  23.7 us
    slice x16, local copies, waits for them, and re-layouts, with_halo(): last = lax.slice_in_dim(value, length - width, length, axis=dim)  18.4 us
  transfers between devices with their start and end apart: 37, of which 13 were waited for; matrix products, arithmetic and copies ran while one was open for 5% of the time, Pallas kernels for 0%

commit v1 on v0

v1 whole, which is shorter than its diff:
```python
import functools

import jax
import jax.numpy as jnp
from jax import lax
from jax.experimental import pallas as pl
from jax.experimental.pallas import tpu as pltpu
from jax.sharding import PartitionSpec as P

STEPS = 6
RATE = 0.05
SUB = 8


def step_body(core_ref, d_ref, a0_ref, a7_ref, h_ref, row_ref, lo_ref, hi_ref, fj_ref, fi_ref, fk_ref, *rest, nj, ni, first, last):
    if last:
        out_ref, af_ref, ps_ref, mid_ref, s1_ref, s2_ref, ring = rest
    else:
        out_ref, af_ref, ps_ref, ring = rest
    rows = ni * SUB
    pitch = rows + 2 * SUB
    other = 7 - first
    g = pl.program_id(0)
    core = core_ref[0]
    here = lax.rem(g, 3) * pitch
    middle = lax.rem(g + 2, 3) * pitch
    below = lax.rem(g + 1, 3) * pitch

    @pl.when(g == 0)
    def _():
        ring[pl.ds(middle + SUB, rows), :] = jnp.where(core == 1, row_ref[...], 0.0)

    @pl.when(g < nj)
    def _():
        ring[pl.ds(here + SUB, rows), :] = d_ref[0]
        ring[pl.ds(here + SUB, ni, stride=SUB), :] = a0_ref[0]
        ring[pl.ds(here + SUB + 7, ni, stride=SUB), :] = a7_ref[0]
        ring[pl.ds(here, SUB), :] = lo_ref[0]
        ring[pl.ds(here + SUB + rows, SUB), :] = hi_ref[0]

    @pl.when(g == nj)
    def _():
        ring[pl.ds(here + SUB, rows), :] = jnp.where(core == 0, row_ref[...], 0.0)

    @pl.when(g > 0)
    def _():
        level = lax.broadcasted_iota(jnp.int32, (SUB, 128), 0)
        unroll = 8

        def some(n, carry):
            base = pl.multiple_of(n * (unroll * SUB), SUB)
            for m in range(unroll):
                at = base + m * SUB
                mid = pl.multiple_of(middle + SUB + at, SUB)
                c = ring[pl.ds(mid, SUB), :]
                i_lo = ring[pl.ds(mid - SUB, SUB), :]
                i_hi = ring[pl.ds(mid + SUB, SUB), :]
                j_lo = ring[pl.ds(pl.multiple_of(below + SUB + at, SUB), SUB), :]
                j_hi = ring[pl.ds(pl.multiple_of(here + SUB + at, SUB), SUB), :]
                k_lo = jnp.where(level == 0, 0.0, pltpu.roll(c, 1, 0))
                k_hi = jnp.where(level == 7, 0.0, pltpu.roll(c, 7, 0))
                total = (j_lo + j_hi) + (i_lo + i_hi) + (k_lo + k_hi)
                new = (1.0 - 6.0 * RATE) * c + RATE * total
                new = new - fj_ref[0, pl.ds(at, SUB), :] * (j_hi - j_lo)
                new = new - fi_ref[0, pl.ds(at, SUB), :] * (i_hi - i_lo)
                new = new - fk_ref[0, pl.ds(at, SUB), :] * (k_hi - k_lo)
                out_ref[0, pl.ds(at, SUB), :] = new
            return carry

        lax.fori_loop(0, ni // unroll, some, 0)
        flow = fk_ref[0, pl.ds(first, ni, stride=SUB), :]
        gain = RATE + flow if first == 0 else RATE - flow
        exact = out_ref[0, pl.ds(first, ni, stride=SUB), :] + gain * h_ref[0]
        af_ref[0] = exact
        ps_ref[0] = out_ref[0, pl.ds(other, ni, stride=SUB), :]
        if last:
            centre = out_ref[0, pl.ds(3, ni, stride=SUB), :]
            moved = exact - centre
            s1 = moved
            s2 = moved * moved
            for k in (1, 2, 4, 5, 6):
                moved = out_ref[0, pl.ds(k, ni, stride=SUB), :] - centre
                s1 = s1 + moved
                s2 = s2 + moved * moved
            mid_ref[0] = centre
            s1_ref[0] = s1
            s2_ref[0] = s2


def step_call(core, d, a0, a7, h, row, lo, hi, fj, fi, fk, first, last):
    nj, rows, lanes = d.shape
    ni = rows // SUB
    ahead = lambda g, *_: (jnp.minimum(g, nj - 1), 0, 0)
    behind = lambda g, *_: (jnp.maximum(g - 1, 0), 0, 0)
    block = lambda n, at: pl.BlockSpec((1, n, lanes), at)
    plane = jax.ShapeDtypeStruct((nj, ni, lanes), d.dtype)
    extra = 3 if last else 0
    return pl.pallas_call(
        functools.partial(step_body, nj=nj, ni=ni, first=first, last=last),
        grid_spec=pltpu.PrefetchScalarGridSpec(
            num_scalar_prefetch=1,
            grid=(nj + 1,),
            in_specs=[
                block(rows, ahead),
                block(ni, ahead),
                block(ni, ahead),
                block(ni, behind),
                pl.BlockSpec((rows, lanes), lambda g, *_: (0, 0)),
                block(SUB, ahead),
                block(SUB, ahead),
                block(rows, behind),
                block(rows, behind),
                block(rows, behind),
            ],
            out_specs=[block(rows, behind)] + [block(ni, behind)] * (2 + extra),
            scratch_shapes=[pltpu.VMEM((3 * (rows + 2 * SUB), lanes), jnp.float32)],
        ),
        out_shape=[jax.ShapeDtypeStruct(d.shape, d.dtype)] + [plane] * (2 + extra),
    )(core, d, a0, a7, h, row, lo, hi, fj, fi, fk)


def fix_body(core_ref, ps_ref, g_ref, h_ref, af_ref, row_ref, lo_ref, hi_ref, as_ref, row_out, lo_out, hi_out, *, ni, nj, first):
    other = 7 - first
    as_ref[...] = ps_ref[...] + g_ref[...] * h_ref[...]
    edge = (1 - core_ref[0]) * (nj - 1)
    row_out[...] = row_ref[0]
    row_out[pl.ds(first, ni, stride=SUB), :] = af_ref[edge]
    row_out[pl.ds(other, ni, stride=SUB), :] = as_ref[edge]
    level = lax.broadcasted_iota(jnp.int32, (SUB, 128), 0)
    for j in range(nj):
        for src, dst, i in ((lo_ref, lo_out, 0), (hi_ref, hi_out, ni - 1)):
            v = jnp.where(level == first, af_ref[j, pl.ds(i, 1), :], src[j])
            dst[j] = jnp.where(level == other, as_ref[j, pl.ds(i, 1), :], v)


def fix_call(core, ps, g, h, af, d, first):
    nj, rows, lanes = d.shape
    ni = rows // SUB
    whole = pl.BlockSpec((nj, ni, lanes), lambda g, c: (0, 0, 0))
    return pl.pallas_call(
        functools.partial(fix_body, ni=ni, nj=nj, first=first),
        grid_spec=pltpu.PrefetchScalarGridSpec(
            num_scalar_prefetch=1,
            grid=(1,),
            in_specs=[
                whole,
                whole,
                whole,
                whole,
                pl.BlockSpec((1, rows, lanes), lambda g, c: ((1 - c[0]) * (nj - 1), 0, 0)),
                pl.BlockSpec((nj, SUB, lanes), lambda g, c: (0, 0, 0)),
                pl.BlockSpec((nj, SUB, lanes), lambda g, c: (0, ni - 1, 0)),
            ],
            out_specs=[
                whole,
                pl.BlockSpec((rows, lanes), lambda g, c: (0, 0)),
                pl.BlockSpec((nj, SUB, lanes), lambda g, c: (0, 0, 0)),
                pl.BlockSpec((nj, SUB, lanes), lambda g, c: (0, 0, 0)),
            ],
        ),
        out_shape=[
            jax.ShapeDtypeStruct((nj, ni, lanes), d.dtype),
            jax.ShapeDtypeStruct((rows, lanes), d.dtype),
            jax.ShapeDtypeStruct((nj, SUB, lanes), d.dtype),
            jax.ShapeDtypeStruct((nj, SUB, lanes), d.dtype),
        ],
    )(core, ps, g, h, af, d, d, d)


def sums_body(ps_ref, g_ref, h_ref, mid_ref, s1_ref, s2_ref, as_ref, v_ref):
    exact = ps_ref[...] + g_ref[...] * h_ref[...]
    as_ref[...] = exact
    moved = exact - mid_ref[...]
    s1 = s1_ref[...] + moved
    s2 = s2_ref[...] + moved * moved
    v_ref[:, 0] = mid_ref[...] + s1 * (1.0 / SUB)
    v_ref[:, 1] = s2 - s1 * s1 * (1.0 / SUB)


def sums_call(ps, g, h, mid, s1, s2):
    nj, ni, lanes = ps.shape
    tile = 2
    block = pl.BlockSpec((tile, ni, lanes), lambda n: (n, 0, 0))
    return pl.pallas_call(
        sums_body,
        grid=(nj // tile,),
        in_specs=[block] * 6,
        out_specs=[block, pl.BlockSpec((tile, 2, ni, lanes), lambda n: (n, 0, 0, 0))],
        out_shape=[jax.ShapeDtypeStruct(ps.shape, ps.dtype), jax.ShapeDtypeStruct((nj, 2, ni, lanes), ps.dtype)],
        name="sums",
    )(ps, g, h, mid, s1, s2)


def finish_body(d_ref, a0_ref, a7_ref, v_ref, anomaly_ref, end_ref, *, ni):
    end_ref[0] = d_ref[0]
    end_ref[0, pl.ds(0, ni, stride=SUB), :] = a0_ref[0]
    end_ref[0, pl.ds(7, ni, stride=SUB), :] = a7_ref[0]
    unroll = 8

    def some(n, carry):
        for m in range(unroll):
            i = n * unroll + m
            at = pl.multiple_of(i * SUB, SUB)
            mean = v_ref[0, 0, pl.ds(i, 1), :]
            scale = v_ref[0, 1, pl.ds(i, 1), :]
            anomaly_ref[0, pl.ds(at, SUB), :] = (end_ref[0, pl.ds(at, SUB), :] - mean) * scale
        return carry

    lax.fori_loop(0, ni // unroll, some, 0)


def finish_call(d, a0, a7, v):
    nj, rows, lanes = d.shape
    ni = rows // SUB
    block = lambda n: pl.BlockSpec((1, n, lanes), lambda j: (j, 0, 0))
    return pl.pallas_call(
        functools.partial(finish_body, ni=ni),
        grid=(nj,),
        in_specs=[block(rows), block(ni), block(ni), pl.BlockSpec((1, 2, ni, lanes), lambda j: (j, 0, 0, 0))],
        out_specs=[block(rows), block(rows)],
        out_shape=[jax.ShapeDtypeStruct(d.shape, d.dtype)] * 2,
        name="finish",
    )(d, a0, a7, v)


def send(value, axis, direction):
    size = lax.axis_size(axis)
    up = [(i, i + 1) for i in range(size - 1)]
    return lax.ppermute(value, axis, up if direction > 0 else [(b, a) for a, b in up])


def body(density, flow_j, flow_i, flow_k):
    nj, ni, nk, lanes = density.shape
    flat = lambda v: v.reshape(nj, ni * nk, lanes)
    core = lax.axis_index("rows").astype(jnp.int32).reshape(1)
    slabs = lax.axis_size("slabs")
    d, fj, fi, fk = flat(density), flat(flow_j), flat(flow_i), flat(flow_k)
    planes = {0: density[:, :, 0, :], 7: density[:, :, 7, :]}
    gains = {0: RATE + flow_k[:, :, 0, :], 7: RATE - flow_k[:, :, 7, :]}
    edge = (1 - core[0]) * (nj - 1)
    row_send = lax.dynamic_index_in_dim(d, edge, 0, keepdims=False)
    lo_send = density[:, 0]
    hi_send = density[:, ni - 1]
    halo = {}
    for t in range(STEPS):
        first = 7 if t % 2 == 0 else 0
        other = 7 - first
        if t == 0:
            halo[first] = send(planes[other], "slabs", -1 if other == 0 else 1)
        row = lax.ppermute(row_send, "rows", [(0, 1), (1, 0)])
        hi = send(lo_send, "cols", -1)
        lo = send(hi_send, "cols", 1)
        halo[other] = send(planes[first], "slabs", -1 if first == 0 else 1)
        last = t == STEPS - 1
        d, exact, part, *sums = step_call(
            core, d, planes[0], planes[7], halo[first], row, lo, hi, fj, fi, fk, first, last
        )
        if last:
            break
        early = send(exact, "slabs", -1 if first == 0 else 1)
        fixed, row_send, lo_send, hi_send = fix_call(core, part, gains[other], halo[other], exact, d, first)
        planes = {first: exact, other: fixed}
        halo = {other: early}
    fixed, v = sums_call(part, gains[other], halo[other], *sums)
    planes = {first: exact, other: fixed}
    got = lax.all_to_all(v, "slabs", 0, 0, tiled=True)
    got = got.reshape(slabs, nj // slabs, 2, ni, lanes)
    mean = jnp.sum(got[:, :, 0], axis=0) / slabs
    off = got[:, :, 0] - mean
    line_variance = jnp.sum(got[:, :, 1] + nk * (off * off), axis=0) / (nk * slabs)
    mine = jnp.stack([mean, lax.rsqrt(line_variance + 0.0001)], axis=1)
    v = lax.all_gather(mine, "slabs", axis=0, tiled=True)
    anomaly, end = finish_call(d, planes[0], planes[7], v)
    return (anomaly.reshape(density.shape), end.reshape(density.shape))


def solution(mesh):
    placed = P("rows", "cols", "slabs", None)
    return jax.shard_map(
        body,
        mesh=mesh,
        in_specs=(placed,) * 4,
        out_specs=(placed, placed),
        check_vma=False,
    )
```

time: 563 us -> 480 us (0.85)
  other arithmetic: 157 us -> 2.9 us
  Pallas kernels: 0 us -> 154 us
  waiting for transfers between devices: 171 us -> 109 us
  blocking collectives: 0 us -> 45.8 us
  starting transfers between devices: 163 us -> 121 us
  local copies, waits for them, and re-layouts: 49.5 us -> 28.6 us
    pallas_call x0 -> x13, Pallas kernels: none -> 154 us  [the longest x6 118 us: step_call(): pl.pallas_call(functools.partial(step_body, nj=nj, ni=ni, first=first, la...]
    add x5 -> x1, other arithmetic: 123 us -> 1.02 us  [body(): gains = {0: RATE + flow_k[:, :, 0, :], 7: RATE - flow_k[:, :, 7, :]}]
    psum x1 -> x0, waiting for transfers between devices: 107 us -> none  [body(): lax.psum((jnp.sum(moved, axis=2, keepdims=True), jnp.sum(moved * moved, a...]
    all_to_all x0 -> x1, blocking collectives: none -> 45.8 us  [body(): got = lax.all_to_all(v, 'slabs', 0, 0, tiled=True)]
    all_gather x0 -> x1, waiting for transfers between devices: none -> 44.1 us  [body(): v = lax.all_gather(mine, 'slabs', axis=0, tiled=True)]
    ppermute x36 -> x30, starting transfers between devices: 163 us -> 121 us  [the longest x24 120 us: send(): lax.ppermute(value, axis, up if direction > 0 else [(b, a) for a, b in up])]
    reduce_sum x1 -> x2, other arithmetic: 29.2 us -> 0.18 us  [the longest x1 0.14 us: body(): jnp.sum(got[:, :, 1] + nk * (off * off), axis=0) / (nk * slabs)]
    unnamed x19 -> x60, local copies, waits for them, and re-layouts: 27.5 us -> 14.4 us
  transfers between devices with their start and end apart: 37 -> 31, of which waited for: 13 -> 12; matrix products, arithmetic and copies ran while one was open for 5% -> 3% of each run, Pallas kernels for 0% -> 28%
where the time goes in v1:
time: 480 us; the launch traced here: 476 us
  Pallas kernels  154 us (32%)
  starting transfers between devices  121 us (25%)
  waiting for transfers between devices  109 us (23%)
  blocking collectives  45.8 us (10%)
  local copies, waits for them, and re-layouts  28.6 us (6%)
  between operations  14.5 us (3%)
    ppermute x24, starting transfers between devices, send(): lax.ppermute(value, axis, up if direction > 0 else [(b, a) for a, b in up])  120 us
    pallas_call x6, Pallas kernels, step_call(): pl.pallas_call(functools.partial(step_body, nj=nj, ni=ni, first=first, la...  118 us
    ppermute x24, waiting for transfers between devices, send(): lax.ppermute(value, axis, up if direction > 0 else [(b, a) for a, b in up])  64.9 us
    all_to_all x1, blocking collectives, body(): got = lax.all_to_all(v, 'slabs', 0, 0, tiled=True)  45.8 us
    all_gather x1, waiting for transfers between devices, body(): v = lax.all_gather(mine, 'slabs', axis=0, tiled=True)  44.1 us
    pallas_call x5, Pallas kernels, fix_call(): pl.pallas_call(functools.partial(fix_body, ni=ni, nj=nj, first=first), gr...  16.2 us
    unnamed x60, local copies, waits for them, and re-layouts  14.4 us
    pallas_call x1, Pallas kernels, finish_call(): pl.pallas_call(functools.partial(finish_body, ni=ni), grid=(nj,), in_spec...  13.8 us
  transfers between devices with their start and end apart: 31, of which 12 were waited for; matrix products, arithmetic and copies ran while one was open for 3% of the time, Pallas kernels for 28%

profile of v1, /device:TPU:0, one launch (start us, length us, event | category | flops | bytes accessed | tf_op | source)
XLA Modules:
  0.0 476.0 jit_solution(6057852692708835824)
XLA Ops:
  10.0 5.2 %collective-permute-start.2 = (f32[16,8,128]{2,1,0:T(8,128)}, f32[16,8,128]{2,1,0:T(8,128)}, u32[]{:S(2)}, u32[]{:S(2)}) collective-permute-start(f32[16,8,128]{2,1,0:T(8,128)} %get-tuple-element.95), channel_id=1, source_target_pairs={{0,8},{8,16},{16,24},{24,32},{32,40},{40,48},{48,56},{1,9},{9,17},... | collective-permute-start | bytes 196616 | tf_op jit(solution)/shard_map/ppermute | solution.py:229
  16.3 5.9 %fusion.6 = (f32[16,96,1,128]{3,2,1,0:T(1,128)S(1)}, f32[16,96,1,128]{3,2,1,0:T(1,128)S(1)}) fusion(f32[16,96,8,128]{3,2,1,0:T(8,128)} %param.4), kind=kLoop, calls=%fused_computation.17 | loop fusion | bytes 3145728 | tf_op jit(solution)/shard_map/slice | solution.py:238
  23.5 6.1 %collective-permute-start.4 = (f32[16,96,128]{2,1,0:T(8,128)S(1)}, f32[16,96,128]{2,1,0:T(8,128)S(1)}, u32[]{:S(2)}, u32[]{:S(2)}) collective-permute-start(f32[16,96,128]{2,1,0:T(8,128)S(1)} %bitcast.73), channel_id=1, source_target_pairs={{0,1},{1,2},{2,3},{3,4},{4,5},{5,6},{6,7},{8,9},{9,10},{10,11},{11... | collective-permute-start | bytes 2359304 | tf_op jit(solution)/shard_map/ppermute | solution.py:229
  29.6 5.8 %fusion.5 = (f32[16,96,1,128]{3,2,1,0:T(1,128)S(1)}, f32[16,96,1,128]{3,2,1,0:T(1,128)S(1)}) fusion(f32[16,96,8,128]{3,2,1,0:T(8,128)} %param.7), kind=kLoop, calls=%fused_computation.16 | loop fusion | bytes 3145728 | tf_op jit(solution)/shard_map/slice | solution.py:239
  36.5 9.5 %collective-permute-done.h_ref = f32[16,96,128]{2,1,0:T(8,128)S(1)} collective-permute-done((f32[16,96,128]{2,1,0:T(8,128)S(1)}, f32[16,96,128]{2,1,0:T(8,128)S(1)}, u32[]{:S(2)}, u32[]{:S(2)}) %collective-permute-start) | collective-permute-done | bytes 786464 | tf_op jit(solution)/shard_map/ppermute | solution.py:229
  46.9 19.5 %shard_map.59 = (f32[16,768,128]{2,1,0:T(8,128)}, f32[16,96,128]{2,1,0:T(8,128)}, f32[16,96,128]{2,1,0:T(8,128)}) custom-call(s32[1]{0:T(128)} %bitcast.core_ref, f32[16,768,128]{2,1,0:T(8,128)} %bitcast.70, f32[16,96,128]{2,1,0:T(8,128)} %bitcast.76, f32[16,96,128]{2,1,0:T(8,128)} %bitcast.74, f32[16,96,128]{2,1,0:T(8,128)} %copy-done.12, ...), custom_call_target="tpu_custom_call" | custom-call | tf_op jit(solution)/shard_map/pallas_call | solution.py:98
  66.5 6.0 %collective-permute-start.5 = (f32[16,96,128]{2,1,0:T(8,128)}, f32[16,96,128]{2,1,0:T(8,128)S(1)}, u32[]{:S(2)}, u32[]{:S(2)}) collective-permute-start(f32[16,96,128]{2,1,0:T(8,128)} %get-tuple-element.49.af_ref.a7_ref), channel_id=1, source_target_pairs={{0,1},{1,2},{2,3},{3,4},{4,5},{5,6},{6,7},{8,9},{9,10},{10,11},{11... | collective-permute-start | bytes 2359304 | tf_op jit(solution)/shard_map/ppermute | solution.py:229
  83.0 7.3 %collective-permute-done.7.lo_ref = f32[16,8,128]{2,1,0:T(8,128)S(1)} collective-permute-done((f32[16,8,128]{2,1,0:T(8,128)}, f32[16,8,128]{2,1,0:T(8,128)S(1)}, u32[]{:S(2)}, u32[]{:S(2)}) %collective-permute-start.7) | collective-permute-done | bytes 65568 | tf_op jit(solution)/shard_map/ppermute | solution.py:229
  94.6 19.5 %shard_map.61 = (f32[16,768,128]{2,1,0:T(8,128)}, f32[16,96,128]{2,1,0:T(8,128)}, f32[16,96,128]{2,1,0:T(8,128)}) custom-call(s32[1]{0:T(128)} %bitcast.core_ref, f32[16,768,128]{2,1,0:T(8,128)} %get-tuple-element.47.row_ref.lo_ref.hi_ref.d_ref, f32[16,96,128]{2,1,0:T(8,128)} %get-tuple-element.50.a0_ref, f32[16,96,128]{2,1,0:T(8,128)} %get-tuple-element.49.af_ref.a7_ref, ...), custom_call_target="tpu_custom_call" | custom-call | tf_op jit(solution)/shard_map/pallas_call | solution.py:98
  119.5 21.5 %collective-permute-start.14 = (f32[16,96,128]{2,1,0:T(8,128)}, f32[16,96,128]{2,1,0:T(8,128)S(1)}, u32[]{:S(2)}, u32[]{:S(2)}) collective-permute-start(f32[16,96,128]{2,1,0:T(8,128)} %get-tuple-element.57.a7_ref), channel_id=1, source_target_pairs={{0,1},{1,2},{2,3},{3,4},{4,5},{5,6},{6,7},{8,9},{9,10},{10,11},{11... | collective-permute-start | bytes 2359304 | tf_op jit(solution)/shard_map/ppermute | solution.py:229
  144.2 13.8 %collective-permute-done.12.lo_ref = f32[16,8,128]{2,1,0:T(8,128)S(1)} collective-permute-done((f32[16,8,128]{2,1,0:T(8,128)}, f32[16,8,128]{2,1,0:T(8,128)S(1)}, u32[]{:S(2)}, u32[]{:S(2)}) %collective-permute-start.12) | collective-permute-done | bytes 65568 | tf_op jit(solution)/shard_map/ppermute | solution.py:229
  161.2 19.5 %shard_map.63 = (f32[16,768,128]{2,1,0:T(8,128)}, f32[16,96,128]{2,1,0:T(8,128)}, f32[16,96,128]{2,1,0:T(8,128)}) custom-call(s32[1]{0:T(128)} %bitcast.core_ref, f32[16,768,128]{2,1,0:T(8,128)} %get-tuple-element.54.row_ref.lo_ref.hi_ref.d_ref, f32[16,96,128]{2,1,0:T(8,128)} %get-tuple-element.55.af_ref.a0_ref, f32[16,96,128]{2,1,0:T(8,128)} %get-tuple-element.57.a7_ref, ...), custom_call_target="tpu_custom_call" | custom-call | tf_op jit(solution)/shard_map/pallas_call | solution.py:98
  180.8 13.7 %collective-permute-start.15 = (f32[16,96,128]{2,1,0:T(8,128)}, f32[16,96,128]{2,1,0:T(8,128)S(1)}, u32[]{:S(2)}, u32[]{:S(2)}) collective-permute-start(f32[16,96,128]{2,1,0:T(8,128)} %get-tuple-element.63.af_ref.a7_ref), channel_id=1, source_target_pairs={{0,1},{1,2},{2,3},{3,4},{4,5},{5,6},{6,7},{8,9},{9,10},{10,11},{11... | collective-permute-start | bytes 2359304 | tf_op jit(solution)/shard_map/ppermute | solution.py:229
  205.5 4.9 %collective-permute-done.17.lo_ref = f32[16,8,128]{2,1,0:T(8,128)S(1)} collective-permute-done((f32[16,8,128]{2,1,0:T(8,128)}, f32[16,8,128]{2,1,0:T(8,128)S(1)}, u32[]{:S(2)}, u32[]{:S(2)}) %collective-permute-start.17) | collective-permute-done | bytes 65568 | tf_op jit(solution)/shard_map/ppermute | solution.py:229
  216.3 19.5 %shard_map.65 = (f32[16,768,128]{2,1,0:T(8,128)}, f32[16,96,128]{2,1,0:T(8,128)}, f32[16,96,128]{2,1,0:T(8,128)}) custom-call(s32[1]{0:T(128)} %bitcast.core_ref, f32[16,768,128]{2,1,0:T(8,128)} %get-tuple-element.61.row_ref.lo_ref.hi_ref.d_ref, f32[16,96,128]{2,1,0:T(8,128)} %get-tuple-element.64.a0_ref, f32[16,96,128]{2,1,0:T(8,128)} %get-tuple-element.63.af_ref.a7_ref, ...), custom_call_target="tpu_custom_call" | custom-call | tf_op jit(solution)/shard_map/pallas_call | solution.py:98
  241.3 24.5 %collective-permute-start.24 = (f32[16,96,128]{2,1,0:T(8,128)}, f32[16,96,128]{2,1,0:T(8,128)S(1)}, u32[]{:S(2)}, u32[]{:S(2)}) collective-permute-start(f32[16,96,128]{2,1,0:T(8,128)} %get-tuple-element.71.a7_ref), channel_id=1, source_target_pairs={{0,1},{1,2},{2,3},{3,4},{4,5},{5,6},{6,7},{8,9},{9,10},{10,11},{11... | collective-permute-start | bytes 2359304 | tf_op jit(solution)/shard_map/ppermute | solution.py:229
  268.6 12.1 %collective-permute-done.22.lo_ref = f32[16,8,128]{2,1,0:T(8,128)S(1)} collective-permute-done((f32[16,8,128]{2,1,0:T(8,128)}, f32[16,8,128]{2,1,0:T(8,128)S(1)}, u32[]{:S(2)}, u32[]{:S(2)}) %collective-permute-start.22) | collective-permute-done | bytes 65568 | tf_op jit(solution)/shard_map/ppermute | solution.py:229
  284.2 19.5 %shard_map.67 = (f32[16,768,128]{2,1,0:T(8,128)}, f32[16,96,128]{2,1,0:T(8,128)}, f32[16,96,128]{2,1,0:T(8,128)}) custom-call(s32[1]{0:T(128)} %bitcast.core_ref, f32[16,768,128]{2,1,0:T(8,128)} %get-tuple-element.68.row_ref.lo_ref.hi_ref.d_ref, f32[16,96,128]{2,1,0:T(8,128)} %get-tuple-element.69.af_ref.a0_ref, f32[16,96,128]{2,1,0:T(8,128)} %get-tuple-element.71.a7_ref, ...), custom_call_target="tpu_custom_call" | custom-call | tf_op jit(solution)/shard_map/pallas_call | solution.py:98
  303.7 13.7 %collective-permute-start.25 = (f32[16,96,128]{2,1,0:T(8,128)}, f32[16,96,128]{2,1,0:T(8,128)S(1)}, u32[]{:S(2)}, u32[]{:S(2)}) collective-permute-start(f32[16,96,128]{2,1,0:T(8,128)} %get-tuple-element.77.af_ref.a7_ref), channel_id=1, source_target_pairs={{0,1},{1,2},{2,3},{3,4},{4,5},{5,6},{6,7},{8,9},{9,10},{10,11},{11... | collective-permute-start | bytes 2359304 | tf_op jit(solution)/shard_map/ppermute | solution.py:229
  336.9 20.4 %shard_map.69 = (f32[16,768,128]{2,1,0:T(8,128)}, f32[16,96,128]{2,1,0:T(8,128)}, f32[16,96,128]{2,1,0:T(8,128)}, f32[16,96,128]{2,1,0:T(8,128)}, f32[16,96,128]{2,1,0:T(8,128)}, /*index=5*/f32[16,96,128]{2,1,0:T(8,128)}) custom-call(s32[1]{0:T(128)} %bitcast.core_ref, f32[16,768,128]{2,1,0:T(8,128)} %get-tuple-element.75.row_ref.lo_ref.hi_ref.d_ref, ...), custom_call_target="tpu_custom_call" | custom-call | tf_op jit(solution)/shard_map/pallas_call | solution.py:98
  358.3 6.3 %sums.1 = (f32[16,96,128]{2,1,0:T(8,128)}, f32[16,2,96,128]{3,2,1,0:T(8,128)}) custom-call(f32[16,96,128]{2,1,0:T(8,128)} %get-tuple-element.84.ps_ref, f32[16,96,128]{2,1,0:T(8,128)} %subtract_bitcast_fusion.g_ref, f32[16,96,128]{2,1,0:T(8,128)} %copy-done.13, f32[16,96,128]{2,1,0:T(8,128)} %get-tuple-element.85.mid_ref, ...), custom_call_target="tpu_custom_call" | custom-call | tf_op jit(solution)/shard_map/sums/pallas_call | solution.py:184
  364.5 45.8 %all_to_all.5 = f32[16,2,96,128]{3,2,1,0:T(8,128)S(1)} all-to-all(f32[16,2,96,128]{3,2,1,0:T(8,128)} %get-tuple-element.89), channel_id=1, replica_groups=mesh['rows'=2,'cols'=8,'slabs'=8] {'slabs'}, dimensions={0} | all-to-all | bytes 3145728 | tf_op jit(solution)/shard_map/all_to_all | solution.py:266
  411.2 44.1 %all-gather.2.cloned.1.call-done.v_ref = f32[16,2,96,128]{3,2,1,0:T(8,128)} async-done(((f32[2,2,96,128]{3,2,1,0:T(8,128)}), f32[16,2,96,128]{3,2,1,0:T(8,128)}) %all-gather.2.cloned.1.call-update) | async-done | bytes 1572880 | tf_op jit(solution)/shard_map/all_gather | solution.py:272
  455.3 13.8 %finish.1 = (f32[16,768,128]{2,1,0:T(8,128)}, f32[16,768,128]{2,1,0:T(8,128)}) custom-call(f32[16,768,128]{2,1,0:T(8,128)} %get-tuple-element.82.d_ref, f32[16,96,128]{2,1,0:T(8,128)} %get-tuple-element.83.a0_ref, f32[16,96,128]{2,1,0:T(8,128)} %get-tuple-element.88.a7_ref, f32[16,2,96,128]{3,2,1,0:T(8,128)} %all-gather.2.cloned.1.call-done.v_ref), custom_call_target="tpu_custom_call" | custom-call | tf_op jit(solution)/shard_map/finish/pallas_call | solution.py:216
  (124 shorter events, 83.5 us)
Async XLA Ops:
  7.2 448.2 %all-gather.2.cloned.1.call-start = ((), (), s32[]{:S(2)}) async-start(), calls=%async_computation.1 | async-start | bytes 1769472 | tf_op jit(solution)/shard_map/all_gather | solution.py:272
  8.7 27.8 %collective-permute-start.3 = (f32[16,8,128]{2,1,0:T(8,128)}, f32[16,8,128]{2,1,0:T(8,128)}, u32[]{:S(2)}, u32[]{:S(2)}) collective-permute-start(f32[16,8,128]{2,1,0:T(8,128)} %get-tuple-element.94), channel_id=1, source_target_pairs={{8,0},{16,8},{24,16},{32,24},{40,32},{48,40},{56,48},{9,1},{17,9},... | collective-permute-start | bytes 196616 | tf_op jit(solution)/shard_map/ppermute | solution.py:229
  10.0 26.5 %collective-permute-start.2 = (f32[16,8,128]{2,1,0:T(8,128)}, f32[16,8,128]{2,1,0:T(8,128)}, u32[]{:S(2)}, u32[]{:S(2)}) collective-permute-start(f32[16,8,128]{2,1,0:T(8,128)} %get-tuple-element.95), channel_id=1, source_target_pairs={{0,8},{8,16},{16,24},{24,32},{32,40},{40,48},{48,56},{1,9},{9,17},... | collective-permute-start | bytes 196616 | tf_op jit(solution)/shard_map/ppermute | solution.py:229
  16.2 20.2 %collective-permute-start.1 = (f32[768,128]{1,0:T(8,128)S(1)}, f32[768,128]{1,0:T(8,128)S(1)}, u32[]{:S(2)}, u32[]{:S(2)}) collective-permute-start(f32[768,128]{1,0:T(8,128)S(1)} %dynamic-slice_bitcast_fusion), channel_id=1, source_target_pairs={{0,64},{64,0},{1,65},{65,1},{2,66},{66,2},{3,67},{67,3},{4,68},{68... | collective-permute-start | bytes 1179656 | tf_op jit(solution)/shard_map/ppermute | solution.py:250
  22.2 23.8 %collective-permute-start = (f32[16,96,128]{2,1,0:T(8,128)S(1)}, f32[16,96,128]{2,1,0:T(8,128)S(1)}, u32[]{:S(2)}, u32[]{:S(2)}) collective-permute-start(f32[16,96,128]{2,1,0:T(8,128)S(1)} %bitcast.75), channel_id=1, source_target_pairs={{1,0},{2,1},{3,2},{4,3},{5,4},{6,5},{7,6},{9,8},{10,9},{11,10},{12... | collective-permute-start | bytes 2359304 | tf_op jit(solution)/shard_map/ppermute | solution.py:229
  23.5 48.9 %collective-permute-start.4 = (f32[16,96,128]{2,1,0:T(8,128)S(1)}, f32[16,96,128]{2,1,0:T(8,128)S(1)}, u32[]{:S(2)}, u32[]{:S(2)}) collective-permute-start(f32[16,96,128]{2,1,0:T(8,128)S(1)} %bitcast.73), channel_id=1, source_target_pairs={{0,1},{1,2},{2,3},{3,4},{4,5},{5,6},{6,7},{8,9},{9,10},{10,11},{11... | collective-permute-start | bytes 2359304 | tf_op jit(solution)/shard_map/ppermute | solution.py:229
  66.5 26.4 %collective-permute-start.5 = (f32[16,96,128]{2,1,0:T(8,128)}, f32[16,96,128]{2,1,0:T(8,128)S(1)}, u32[]{:S(2)}, u32[]{:S(2)}) collective-permute-start(f32[16,96,128]{2,1,0:T(8,128)} %get-tuple-element.49.af_ref.a7_ref), channel_id=1, source_target_pairs={{0,1},{1,2},{2,3},{3,4},{4,5},{5,6},{6,7},{8,9},{9,10},{10,11},{11... | collective-permute-start | bytes 2359304 | tf_op jit(solution)/shard_map/ppermute | solution.py:229
  76.6 38.8 %collective-permute-start.9 = (f32[16,96,128]{2,1,0:T(8,128)}, f32[16,96,128]{2,1,0:T(8,128)S(1)}, u32[]{:S(2)}, u32[]{:S(2)}) collective-permute-start(f32[16,96,128]{2,1,0:T(8,128)} %get-tuple-element.50.a0_ref), channel_id=1, source_target_pairs={{1,0},{2,1},{3,2},{4,3},{5,4},{6,5},{7,6},{9,8},{10,9},{11,10},{12... | collective-permute-start | bytes 2359304 | tf_op jit(solution)/shard_map/ppermute | solution.py:229
  77.9 15.0 %collective-permute-start.6 = (f32[768,128]{1,0:T(8,128)}, f32[768,128]{1,0:T(8,128)S(1)}, u32[]{:S(2)}, u32[]{:S(2)}) collective-permute-start(f32[768,128]{1,0:T(8,128)} %get-tuple-element.51), channel_id=1, source_target_pairs={{0,64},{64,0},{1,65},{65,1},{2,66},{66,2},{3,67},{67,3},{4,68},{68... | collective-permute-start | bytes 1179656 | tf_op jit(solution)/shard_map/ppermute | solution.py:250
  114.1 45.5 %collective-permute-start.10 = (f32[16,96,128]{2,1,0:T(8,128)}, f32[16,96,128]{2,1,0:T(8,128)S(1)}, u32[]{:S(2)}, u32[]{:S(2)}) collective-permute-start(f32[16,96,128]{2,1,0:T(8,128)} %get-tuple-element.55.af_ref.a0_ref), channel_id=1, source_target_pairs={{1,0},{2,1},{3,2},{4,3},{5,4},{6,5},{7,6},{9,8},{10,9},{11,10},{12... | collective-permute-start | bytes 2359304 | tf_op jit(solution)/shard_map/ppermute | solution.py:229
  119.5 74.9 %collective-permute-start.14 = (f32[16,96,128]{2,1,0:T(8,128)}, f32[16,96,128]{2,1,0:T(8,128)S(1)}, u32[]{:S(2)}, u32[]{:S(2)}) collective-permute-start(f32[16,96,128]{2,1,0:T(8,128)} %get-tuple-element.57.a7_ref), channel_id=1, source_target_pairs={{0,1},{1,2},{2,3},{3,4},{4,5},{5,6},{6,7},{8,9},{9,10},{10,11},{11... | collective-permute-start | bytes 2359304 | tf_op jit(solution)/shard_map/ppermute | solution.py:229
  141.1 18.5 %collective-permute-start.11 = (f32[768,128]{1,0:T(8,128)}, f32[768,128]{1,0:T(8,128)S(1)}, u32[]{:S(2)}, u32[]{:S(2)}) collective-permute-start(f32[768,128]{1,0:T(8,128)} %get-tuple-element.58), channel_id=1, source_target_pairs={{0,64},{64,0},{1,65},{65,1},{2,66},{66,2},{3,67},{67,3},{4,68},{68... | collective-permute-start | bytes 1179656 | tf_op jit(solution)/shard_map/ppermute | solution.py:250
  141.2 16.8 %collective-permute-start.12 = (f32[16,8,128]{2,1,0:T(8,128)}, f32[16,8,128]{2,1,0:T(8,128)S(1)}, u32[]{:S(2)}, u32[]{:S(2)}) collective-permute-start(f32[16,8,128]{2,1,0:T(8,128)} %get-tuple-element.59), channel_id=1, source_target_pairs={{0,8},{8,16},{16,24},{24,32},{32,40},{40,48},{48,56},{1,9},{9,17},... | collective-permute-start | bytes 196616 | tf_op jit(solution)/shard_map/ppermute | solution.py:229
  142.9 16.7 %collective-permute-start.13 = (f32[16,8,128]{2,1,0:T(8,128)}, f32[16,8,128]{2,1,0:T(8,128)S(1)}, u32[]{:S(2)}, u32[]{:S(2)}) collective-permute-start(f32[16,8,128]{2,1,0:T(8,128)} %get-tuple-element.60), channel_id=1, source_target_pairs={{8,0},{16,8},{24,16},{32,24},{40,32},{48,40},{56,48},{9,1},{17,9},... | collective-permute-start | bytes 196616 | tf_op jit(solution)/shard_map/ppermute | solution.py:229
  180.8 33.9 %collective-permute-start.15 = (f32[16,96,128]{2,1,0:T(8,128)}, f32[16,96,128]{2,1,0:T(8,128)S(1)}, u32[]{:S(2)}, u32[]{:S(2)}) collective-permute-start(f32[16,96,128]{2,1,0:T(8,128)} %get-tuple-element.63.af_ref.a7_ref), channel_id=1, source_target_pairs={{0,1},{1,2},{2,3},{3,4},{4,5},{5,6},{6,7},{8,9},{9,10},{10,11},{11... | collective-permute-start | bytes 2359304 | tf_op jit(solution)/shard_map/ppermute | solution.py:229
  198.6 38.6 %collective-permute-start.19 = (f32[16,96,128]{2,1,0:T(8,128)}, f32[16,96,128]{2,1,0:T(8,128)S(1)}, u32[]{:S(2)}, u32[]{:S(2)}) collective-permute-start(f32[16,96,128]{2,1,0:T(8,128)} %get-tuple-element.64.a0_ref), channel_id=1, source_target_pairs={{1,0},{2,1},{3,2},{4,3},{5,4},{6,5},{7,6},{9,8},{10,9},{11,10},{12... | collective-permute-start | bytes 2359304 | tf_op jit(solution)/shard_map/ppermute | solution.py:229
  199.8 14.8 %collective-permute-start.16 = (f32[768,128]{1,0:T(8,128)}, f32[768,128]{1,0:T(8,128)S(1)}, u32[]{:S(2)}, u32[]{:S(2)}) collective-permute-start(f32[768,128]{1,0:T(8,128)} %get-tuple-element.65), channel_id=1, source_target_pairs={{0,64},{64,0},{1,65},{65,1},{2,66},{66,2},{3,67},{67,3},{4,68},{68... | collective-permute-start | bytes 1179656 | tf_op jit(solution)/shard_map/ppermute | solution.py:250
  235.8 46.7 %collective-permute-start.20 = (f32[16,96,128]{2,1,0:T(8,128)}, f32[16,96,128]{2,1,0:T(8,128)S(1)}, u32[]{:S(2)}, u32[]{:S(2)}) collective-permute-start(f32[16,96,128]{2,1,0:T(8,128)} %get-tuple-element.69.af_ref.a0_ref), channel_id=1, source_target_pairs={{1,0},{2,1},{3,2},{4,3},{5,4},{6,5},{7,6},{9,8},{10,9},{11,10},{12... | collective-permute-start | bytes 2359304 | tf_op jit(solution)/shard_map/ppermute | solution.py:229
  241.3 76.2 %collective-permute-start.24 = (f32[16,96,128]{2,1,0:T(8,128)}, f32[16,96,128]{2,1,0:T(8,128)S(1)}, u32[]{:S(2)}, u32[]{:S(2)}) collective-permute-start(f32[16,96,128]{2,1,0:T(8,128)} %get-tuple-element.71.a7_ref), channel_id=1, source_target_pairs={{0,1},{1,2},{2,3},{3,4},{4,5},{5,6},{6,7},{8,9},{9,10},{10,11},{11... | collective-permute-start | bytes 2359304 | tf_op jit(solution)/shard_map/ppermute | solution.py:229
  265.8 16.8 %collective-permute-start.21 = (f32[768,128]{1,0:T(8,128)}, f32[768,128]{1,0:T(8,128)S(1)}, u32[]{:S(2)}, u32[]{:S(2)}) collective-permute-start(f32[768,128]{1,0:T(8,128)} %get-tuple-element.72), channel_id=1, source_target_pairs={{0,64},{64,0},{1,65},{65,1},{2,66},{66,2},{3,67},{67,3},{4,68},{68... | collective-permute-start | bytes 1179656 | tf_op jit(solution)/shard_map/ppermute | solution.py:250
  265.9 14.8 %collective-permute-start.22 = (f32[16,8,128]{2,1,0:T(8,128)}, f32[16,8,128]{2,1,0:T(8,128)S(1)}, u32[]{:S(2)}, u32[]{:S(2)}) collective-permute-start(f32[16,8,128]{2,1,0:T(8,128)} %get-tuple-element.73), channel_id=1, source_target_pairs={{0,8},{8,16},{16,24},{24,32},{32,40},{40,48},{48,56},{1,9},{9,17},... | collective-permute-start | bytes 196616 | tf_op jit(solution)/shard_map/ppermute | solution.py:229
  267.3 15.2 %collective-permute-start.23 = (f32[16,8,128]{2,1,0:T(8,128)}, f32[16,8,128]{2,1,0:T(8,128)S(1)}, u32[]{:S(2)}, u32[]{:S(2)}) collective-permute-start(f32[16,8,128]{2,1,0:T(8,128)} %get-tuple-element.74), channel_id=1, source_target_pairs={{8,0},{16,8},{24,16},{32,24},{40,32},{48,40},{56,48},{9,1},{17,9},... | collective-permute-start | bytes 196616 | tf_op jit(solution)/shard_map/ppermute | solution.py:229
  303.7 31.6 %collective-permute-start.25 = (f32[16,96,128]{2,1,0:T(8,128)}, f32[16,96,128]{2,1,0:T(8,128)S(1)}, u32[]{:S(2)}, u32[]{:S(2)}) collective-permute-start(f32[16,96,128]{2,1,0:T(8,128)} %get-tuple-element.77.af_ref.a7_ref), channel_id=1, source_target_pairs={{0,1},{1,2},{2,3},{3,4},{4,5},{5,6},{6,7},{8,9},{9,10},{10,11},{11... | collective-permute-start | bytes 2359304 | tf_op jit(solution)/shard_map/ppermute | solution.py:229
  321.6 35.7 %collective-permute-start.29 = (f32[16,96,128]{2,1,0:T(8,128)}, f32[16,96,128]{2,1,0:T(8,128)S(1)}, u32[]{:S(2)}, u32[]{:S(2)}) collective-permute-start(f32[16,96,128]{2,1,0:T(8,128)} %get-tuple-element.78.a0_ref), channel_id=1, source_target_pairs={{1,0},{2,1},{3,2},{4,3},{5,4},{6,5},{7,6},{9,8},{10,9},{11,10},{12... | collective-permute-start | bytes 2359304 | tf_op jit(solution)/shard_map/ppermute | solution.py:229
  (37 other events, 166.1 us)
Sparse Core Ops, SparseCore 0:
  411.4 43.9 all-gather.1

commit v2 on v0

v2 whole, which is shorter than its diff:
```python
import functools

import jax
import jax.numpy as jnp
from jax import lax
from jax.experimental import pallas as pl
from jax.experimental.pallas import tpu as pltpu
from jax.sharding import PartitionSpec as P

STEPS = 6
RATE = 0.05
SUB = 8


def in_vmem(*values):
    return [pltpu.with_memory_space_constraint(v, pltpu.VMEM) for v in values]


def local_call(body, outs, core, *values, scratch=()):
    spec = pl.BlockSpec(memory_space=pltpu.VMEM)
    return pl.pallas_call(
        body,
        in_specs=[pl.BlockSpec(memory_space=pltpu.SMEM)] + [spec] * len(values),
        out_specs=[spec] * len(outs),
        out_shape=[pltpu.VMEM(shape, jnp.float32) for shape in outs],
        scratch_shapes=list(scratch),
        compiler_params=pltpu.CompilerParams(vmem_limit_bytes=4 << 20),
    )(core, *in_vmem(*values))


def prep_body(core_ref, d_ref, a0_ref, a7_ref, row_ref, lo_ref, hi_ref):
    nj, rows, _ = d_ref.shape
    ni = rows // SUB

    def some(j, carry):
        a0_ref[j] = d_ref[j, pl.ds(0, ni, stride=SUB), :]
        a7_ref[j] = d_ref[j, pl.ds(7, ni, stride=SUB), :]
        lo_ref[j] = d_ref[j, pl.ds(0, SUB), :]
        hi_ref[j] = d_ref[j, pl.ds(rows - SUB, SUB), :]
        return carry

    lax.fori_loop(0, nj, some, 0)
    row_ref[...] = d_ref[(1 - core_ref[0]) * (nj - 1)]


def step_body(core_ref, d_ref, a0_ref, a7_ref, h_ref, row_ref, lo_ref, hi_ref, fj_ref, fi_ref, fk_ref, *rest, first, last):
    if last:
        out_ref, af_ref, ps_ref, mid_ref, s1_ref, s2_ref, ring = rest
    else:
        out_ref, af_ref, ps_ref, ring = rest
    nj, rows, _ = d_ref.shape
    ni = rows // SUB
    pitch = rows + 2 * SUB
    other = 7 - first
    core = core_ref[0]
    level = lax.broadcasted_iota(jnp.int32, (SUB, 128), 0)

    def load(j):
        at = pl.multiple_of(lax.rem(j, 3) * pitch, SUB)
        ring[pl.ds(at + SUB, rows), :] = d_ref[j]
        ring[pl.ds(at + SUB, ni, stride=SUB), :] = a0_ref[j]
        ring[pl.ds(at + SUB + 7, ni, stride=SUB), :] = a7_ref[j]
        ring[pl.ds(at, SUB), :] = lo_ref[j]
        ring[pl.ds(at + SUB + rows, SUB), :] = hi_ref[j]

    ring[pl.ds(2 * pitch + SUB, rows), :] = jnp.where(core == 1, row_ref[...], 0.0)
    load(0)

    def plane(j, carry):
        here = lax.rem(j + 1, 3) * pitch
        middle = lax.rem(j, 3) * pitch
        below = lax.rem(j + 2, 3) * pitch

        @pl.when(j + 1 < nj)
        def _():
            load(j + 1)

        @pl.when(j + 1 == nj)
        def _():
            ring[pl.ds(pl.multiple_of(here + SUB, SUB), rows), :] = jnp.where(core == 0, row_ref[...], 0.0)

        unroll = 8

        def some(n, inner):
            base = pl.multiple_of(n * (unroll * SUB), SUB)
            for m in range(unroll):
                at = base + m * SUB
                mid = pl.multiple_of(middle + SUB + at, SUB)
                c = ring[pl.ds(mid, SUB), :]
                i_lo = ring[pl.ds(mid - SUB, SUB), :]
                i_hi = ring[pl.ds(mid + SUB, SUB), :]
                j_lo = ring[pl.ds(pl.multiple_of(below + SUB + at, SUB), SUB), :]
                j_hi = ring[pl.ds(pl.multiple_of(here + SUB + at, SUB), SUB), :]
                k_lo = jnp.where(level == 0, 0.0, pltpu.roll(c, 1, 0))
                k_hi = jnp.where(level == 7, 0.0, pltpu.roll(c, 7, 0))
                total = (j_lo + j_hi) + (i_lo + i_hi) + (k_lo + k_hi)
                new = (1.0 - 6.0 * RATE) * c + RATE * total
                new = new - fj_ref[j, pl.ds(at, SUB), :] * (j_hi - j_lo)
                new = new - fi_ref[j, pl.ds(at, SUB), :] * (i_hi - i_lo)
                new = new - fk_ref[j, pl.ds(at, SUB), :] * (k_hi - k_lo)
                out_ref[j, pl.ds(at, SUB), :] = new
            return inner

        lax.fori_loop(0, ni // unroll, some, 0)
        flow = fk_ref[j, pl.ds(first, ni, stride=SUB), :]
        gain = RATE + flow if first == 0 else RATE - flow
        exact = out_ref[j, pl.ds(first, ni, stride=SUB), :] + gain * h_ref[j]
        af_ref[j] = exact
        ps_ref[j] = out_ref[j, pl.ds(other, ni, stride=SUB), :]
        if last:
            centre = out_ref[j, pl.ds(3, ni, stride=SUB), :]
            moved = exact - centre
            s1 = moved
            s2 = moved * moved
            for k in (1, 2, 4, 5, 6):
                moved = out_ref[j, pl.ds(k, ni, stride=SUB), :] - centre
                s1 = s1 + moved
                s2 = s2 + moved * moved
            mid_ref[j] = centre
            s1_ref[j] = s1
            s2_ref[j] = s2
        return carry

    lax.fori_loop(0, nj, plane, 0)


def fixed_plane(j, ps_ref, h_ref, fk_ref, first):
    ni = ps_ref.shape[1]
    flow = fk_ref[j, pl.ds(7 - first, ni, stride=SUB), :]
    gain = RATE - flow if first == 0 else RATE + flow
    return ps_ref[j] + gain * h_ref[j]


def fix_body(core_ref, ps_ref, fk_ref, h_ref, af_ref, d_ref, as_ref, row_out, lo_out, hi_out, *, first):
    nj, rows, _ = d_ref.shape
    ni = rows // SUB
    other = 7 - first
    level = lax.broadcasted_iota(jnp.int32, (SUB, 128), 0)

    def some(j, carry):
        as_ref[j] = fixed_plane(j, ps_ref, h_ref, fk_ref, first)
        for dst, i in ((lo_out, 0), (hi_out, ni - 1)):
            v = jnp.where(level == first, af_ref[j, pl.ds(i, 1), :], d_ref[j, pl.ds(i * SUB, SUB), :])
            dst[j] = jnp.where(level == other, as_ref[j, pl.ds(i, 1), :], v)
        return carry

    lax.fori_loop(0, nj, some, 0)
    edge = (1 - core_ref[0]) * (nj - 1)
    row_out[...] = d_ref[edge]
    row_out[pl.ds(first, ni, stride=SUB), :] = af_ref[edge]
    row_out[pl.ds(other, ni, stride=SUB), :] = as_ref[edge]


def sums_body(core_ref, ps_ref, fk_ref, h_ref, mid_ref, s1_ref, s2_ref, as_ref, v_ref, *, first):
    def some(j, carry):
        exact = fixed_plane(j, ps_ref, h_ref, fk_ref, first)
        as_ref[j] = exact
        moved = exact - mid_ref[j]
        s1 = s1_ref[j] + moved
        s2 = s2_ref[j] + moved * moved
        v_ref[j, 0] = mid_ref[j] + s1 * (1.0 / SUB)
        v_ref[j, 1] = s2 - s1 * s1 * (1.0 / SUB)
        return carry

    lax.fori_loop(0, ps_ref.shape[0], some, 0)


def finish_body(d_ref, a0_ref, a7_ref, v_ref, anomaly_ref, end_ref):
    j = pl.program_id(0)
    ni = a0_ref.shape[1]
    end_ref[0] = d_ref[j]
    end_ref[0, pl.ds(0, ni, stride=SUB), :] = a0_ref[j]
    end_ref[0, pl.ds(7, ni, stride=SUB), :] = a7_ref[j]
    unroll = 8

    def some(n, carry):
        for m in range(unroll):
            i = n * unroll + m
            at = pl.multiple_of(i * SUB, SUB)
            mean = v_ref[j, 0, pl.ds(i, 1), :]
            scale = v_ref[j, 1, pl.ds(i, 1), :]
            anomaly_ref[0, pl.ds(at, SUB), :] = (end_ref[0, pl.ds(at, SUB), :] - mean) * scale
        return carry

    lax.fori_loop(0, ni // unroll, some, 0)


def finish_call(d, a0, a7, v):
    nj, rows, lanes = d.shape
    whole = pl.BlockSpec(memory_space=pltpu.VMEM)
    block = pl.BlockSpec((1, rows, lanes), lambda j: (j, 0, 0))
    return pl.pallas_call(
        finish_body,
        grid=(nj,),
        in_specs=[whole] * 4,
        out_specs=[block, block],
        out_shape=[jax.ShapeDtypeStruct(d.shape, d.dtype)] * 2,
        compiler_params=pltpu.CompilerParams(vmem_limit_bytes=4 << 20),
        name="finish",
    )(*in_vmem(d, a0, a7, v))


def send(value, axis, direction):
    size = lax.axis_size(axis)
    up = [(i, i + 1) for i in range(size - 1)]
    return lax.ppermute(value, axis, up if direction > 0 else [(b, a) for a, b in up])


def body(density, flow_j, flow_i, flow_k):
    nj, ni, nk, lanes = density.shape
    flat = lambda v: v.reshape(nj, ni * nk, lanes)
    core = lax.axis_index("rows").astype(jnp.int32).reshape(1)
    slabs = lax.axis_size("slabs")
    d, fj, fi, fk = flat(density), flat(flow_j), flat(flow_i), flat(flow_k)
    cube, square, line = d.shape, (nj, ni, lanes), (nj, SUB, lanes)
    edges = [cube[1:], line, line]
    ring = [pltpu.VMEM((3 * (cube[1] + 2 * SUB), lanes), jnp.float32)]
    plane_0, plane_7, row_send, lo_send, hi_send = local_call(
        prep_body, [square, square, *edges], core, d
    )
    planes = {0: plane_0, 7: plane_7}
    halo = {}
    for t in range(STEPS):
        first = 7 if t % 2 == 0 else 0
        other = 7 - first
        last = t == STEPS - 1
        if t == 0:
            halo[first] = send(planes[other], "slabs", -1)
        row = lax.ppermute(row_send, "rows", [(0, 1), (1, 0)])
        hi = send(lo_send, "cols", -1)
        lo = send(hi_send, "cols", 1)
        halo[other] = send(planes[first], "slabs", -1 if first == 0 else 1)
        d, exact, part, *sums = local_call(
            functools.partial(step_body, first=first, last=last),
            [cube] + [square] * (5 if last else 2),
            core,
            *(d, planes[0], planes[7], halo[first], row, lo, hi, fj, fi, fk),
            scratch=ring,
        )
        if last:
            break
        early = send(exact, "slabs", -1 if first == 0 else 1)
        fixed, row_send, lo_send, hi_send = local_call(
            functools.partial(fix_body, first=first),
            [square, *edges],
            core,
            *(part, fk, halo[other], exact, d),
        )
        planes = {first: exact, other: fixed}
        halo = {other: early}
    fixed, v = local_call(
        functools.partial(sums_body, first=first),
        [square, (nj, 2, ni, lanes)],
        core,
        *(part, fk, halo[other], *sums),
    )
    planes = {first: exact, other: fixed}
    got = lax.all_to_all(v, "slabs", 0, 0, tiled=True)
    got = got.reshape(slabs, nj // slabs, 2, ni, lanes)
    mean = jnp.sum(got[:, :, 0], axis=0) / slabs
    off = got[:, :, 0] - mean
    line_variance = jnp.sum(got[:, :, 1] + nk * (off * off), axis=0) / (nk * slabs)
    mine = jnp.stack([mean, lax.rsqrt(line_variance + 0.0001)], axis=1)
    copies = jnp.broadcast_to(mine[None], (slabs, *mine.shape))
    v = lax.all_to_all(copies, "slabs", 0, 0, tiled=True).reshape(nj, 2, ni, lanes)
    anomaly, end = finish_call(d, planes[0], planes[7], v)
    return (anomaly.reshape(density.shape), end.reshape(density.shape))


def solution(mesh):
    placed = P("rows", "cols", "slabs", None)
    return jax.shard_map(
        body,
        mesh=mesh,
        in_specs=(placed,) * 4,
        out_specs=(placed, placed),
        check_vma=False,
    )
```

time: 563 us -> 352 us (0.63); the launches traced: 556 us -> 351 us
  other arithmetic: 157 us -> 0.23 us
  waiting for transfers between devices: 171 us -> 103 us
  Pallas kernels: 0 us -> 58.7 us
  blocking collectives: 0 us -> 53.5 us
  local copies, waits for them, and re-layouts: 49.5 us -> 8.68 us
  starting transfers between devices: 163 us -> 126 us
  between operations: 14.9 us -> 1.08 us
    add x5 -> x0, other arithmetic: 123 us -> none  [advance(): middle - flow_j * slopes[0] - flow_i * slopes[1] - flow_k * slopes[2]]
    psum x1 -> x0, waiting for transfers between devices: 107 us -> none  [body(): lax.psum((jnp.sum(moved, axis=2, keepdims=True), jnp.sum(moved * moved, a...]
    pallas_call x0 -> x14, Pallas kernels: none -> 58.7 us  [the longest x13 50.2 us: local_call(): pl.pallas_call(body, in_specs=[pl.BlockSpec(memory_space=pltpu.SMEM)] + [...]
    all_to_all x0 -> x2, blocking collectives: none -> 53.5 us  [the longest x1 34.4 us: body(): got = lax.all_to_all(v, 'slabs', 0, 0, tiled=True)]
    ppermute x36 -> x30, waiting for transfers between devices: 63.5 us -> 103 us  [the longest x24 103 us: send(): lax.ppermute(value, axis, up if direction > 0 else [(b, a) for a, b in up])]
    ppermute x36 -> x30, starting transfers between devices: 163 us -> 126 us  [the longest x24 126 us: send(): lax.ppermute(value, axis, up if direction > 0 else [(b, a) for a, b in up])]
    reduce_sum x1 -> x2, other arithmetic: 29.2 us -> 0.18 us  [the longest x1 0.14 us: body(): jnp.sum(got[:, :, 1] + nk * (off * off), axis=0) / (nk * slabs)]
    slice x18 -> x0, local copies, waits for them, and re-layouts: 19.9 us -> none  [the longest x16 18.4 us: with_halo(): last = lax.slice_in_dim(value, length - width, length, axis=dim)]
  transfers between devices with their start and end apart: 37 -> 30, of which waited for: 13 -> 15; matrix products, arithmetic and copies ran while one was open for 5% -> 0% of each run, Pallas kernels for 0% -> 14%
where the time goes in v2:
time: 352 us; the launch traced here: 351 us
  starting transfers between devices  126 us (36%)
  waiting for transfers between devices  103 us (29%)
  Pallas kernels  58.7 us (17%)
  blocking collectives  53.5 us (15%)
  local copies, waits for them, and re-layouts  8.68 us (2%)
    ppermute x24, starting transfers between devices, send(): lax.ppermute(value, axis, up if direction > 0 else [(b, a) for a, b in up])  126 us
    ppermute x24, waiting for transfers between devices, send(): lax.ppermute(value, axis, up if direction > 0 else [(b, a) for a, b in up])  103 us
    pallas_call x13, Pallas kernels, local_call(): pl.pallas_call(body, in_specs=[pl.BlockSpec(memory_space=pltpu.SMEM)] + [...  50.2 us
    all_to_all x1, blocking collectives, body(): got = lax.all_to_all(v, 'slabs', 0, 0, tiled=True)  34.4 us
    all_to_all x1, blocking collectives, body(): lax.all_to_all(copies, 'slabs', 0, 0, tiled=True).reshape(nj, 2, ni, lanes)  19.1 us
    unnamed x12, local copies, waits for them, and re-layouts  8.51 us
    pallas_call x1, Pallas kernels, finish_call(): pl.pallas_call(finish_body, grid=(nj,), in_specs=[whole] * 4, out_specs=[...  8.49 us
  transfers between devices with their start and end apart: 30, of which 15 were waited for; matrix products, arithmetic and copies ran while one was open for 0% of the time, Pallas kernels for 14%

profile of v2, /device:TPU:0, one launch (start us, length us, event | category | flops | bytes accessed | tf_op | source)
XLA Modules:
  0.0 351.4 jit_solution(2361481726244282176)
XLA Ops:
  5.4 6.1 %collective-permute-start.4 = (f32[16,96,128]{2,1,0:T(8,128)S(1)}, f32[16,96,128]{2,1,0:T(8,128)S(1)}, u32[]{:S(2)}, u32[]{:S(2)}) collective-permute-start(f32[16,96,128]{2,1,0:T(8,128)S(1)} %get-tuple-element.53.a7_ref), channel_id=1, source_target_pairs={{0,1},{1,2},{2,3},{3,4},{4,5},{5,6},{6,7},{8,9},{9,10},{10,11},{11... | collective-permute-start | bytes 2359304 | tf_op jit(solution)/shard_map/ppermute | solution.py:206
  16.4 12.8 %collective-permute-done.2.lo_ref = f32[16,8,128]{2,1,0:T(8,128)S(1)} collective-permute-done((f32[16,8,128]{2,1,0:T(8,128)S(1)}, f32[16,8,128]{2,1,0:T(8,128)S(1)}, u32[]{:S(2)}, u32[]{:S(2)}) %collective-permute-start.2) | collective-permute-done | bytes 65568 | tf_op jit(solution)/shard_map/ppermute | solution.py:206
  38.4 7.6 %shard_map.60 = (f32[16,768,128]{2,1,0:T(8,128)S(1)}, f32[16,96,128]{2,1,0:T(8,128)S(1)}, f32[16,96,128]{2,1,0:T(8,128)S(1)}) custom-call(s32[1]{0:T(128)} %bitcast.core_ref, f32[16,768,128]{2,1,0:T(8,128)S(1)} %bitcast.55, f32[16,96,128]{2,1,0:T(8,128)S(1)} %get-tuple-element.52.a0_ref, f32[16,96,128]{2,1,0:T(8,128)S(1)} %get-tuple-element.53.a7_ref, ...), custom_call_target="tpu_custom_call" | custom-call | tf_op jit(solution)/shard_map/pallas_call | solution.py:21
  46.0 17.8 %collective-permute-start.5 = (f32[16,96,128]{2,1,0:T(8,128)S(1)}, f32[16,96,128]{2,1,0:T(8,128)S(1)}, u32[]{:S(2)}, u32[]{:S(2)}) collective-permute-start(f32[16,96,128]{2,1,0:T(8,128)S(1)} %get-tuple-element.59.af_ref.a7_ref), channel_id=1, source_target_pairs={{0,1},{1,2},{2,3},{3,4},{4,5},{5,6},{6,7},{8,9},{9,10},{10,11},{11... | collective-permute-start | bytes 2359304 | tf_op jit(solution)/shard_map/ppermute | solution.py:206
  70.2 10.6 %collective-permute-done.7.lo_ref = f32[16,8,128]{2,1,0:T(8,128)S(1)} collective-permute-done((f32[16,8,128]{2,1,0:T(8,128)S(1)}, f32[16,8,128]{2,1,0:T(8,128)S(1)}, u32[]{:S(2)}, u32[]{:S(2)}) %collective-permute-start.7) | collective-permute-done | bytes 65568 | tf_op jit(solution)/shard_map/ppermute | solution.py:206
  83.4 7.7 %shard_map.62 = (f32[16,768,128]{2,1,0:T(8,128)S(1)}, f32[16,96,128]{2,1,0:T(8,128)S(1)}, f32[16,96,128]{2,1,0:T(8,128)S(1)}) custom-call(s32[1]{0:T(128)} %bitcast.core_ref, f32[16,768,128]{2,1,0:T(8,128)S(1)} %get-tuple-element.57.d_ref, f32[16,96,128]{2,1,0:T(8,128)S(1)} %get-tuple-element.60.a0_ref, f32[16,96,128]{2,1,0:T(8,128)S(1)} %get-tuple-element.59.af_ref.a7_ref, ...), custom_call_target="tpu_custom_call" | custom-call | tf_op jit(solution)/shard_map/pallas_call | solution.py:21
  92.3 7.5 %collective-permute-done.9.h_ref = f32[16,96,128]{2,1,0:T(8,128)S(1)} collective-permute-done((f32[16,96,128]{2,1,0:T(8,128)S(1)}, f32[16,96,128]{2,1,0:T(8,128)S(1)}, u32[]{:S(2)}, u32[]{:S(2)}) %collective-permute-start.9) | collective-permute-done | bytes 786464 | tf_op jit(solution)/shard_map/ppermute | solution.py:206
  100.3 17.1 %collective-permute-start.14 = (f32[16,96,128]{2,1,0:T(8,128)S(1)}, f32[16,96,128]{2,1,0:T(8,128)S(1)}, u32[]{:S(2)}, u32[]{:S(2)}) collective-permute-start(f32[16,96,128]{2,1,0:T(8,128)S(1)} %get-tuple-element.67.a7_ref), channel_id=1, source_target_pairs={{0,1},{1,2},{2,3},{3,4},{4,5},{5,6},{6,7},{8,9},{9,10},{10,11},{11... | collective-permute-start | bytes 2359304 | tf_op jit(solution)/shard_map/ppermute | solution.py:206
  120.4 12.9 %collective-permute-done.12.lo_ref = f32[16,8,128]{2,1,0:T(8,128)S(1)} collective-permute-done((f32[16,8,128]{2,1,0:T(8,128)S(1)}, f32[16,8,128]{2,1,0:T(8,128)S(1)}, u32[]{:S(2)}, u32[]{:S(2)}) %collective-permute-start.12) | collective-permute-done | bytes 65568 | tf_op jit(solution)/shard_map/ppermute | solution.py:206
  135.3 7.6 %shard_map.64 = (f32[16,768,128]{2,1,0:T(8,128)S(1)}, f32[16,96,128]{2,1,0:T(8,128)S(1)}, f32[16,96,128]{2,1,0:T(8,128)S(1)}) custom-call(s32[1]{0:T(128)} %bitcast.core_ref, f32[16,768,128]{2,1,0:T(8,128)S(1)} %get-tuple-element.64.d_ref, f32[16,96,128]{2,1,0:T(8,128)S(1)} %get-tuple-element.65.af_ref.a0_ref, f32[16,96,128]{2,1,0:T(8,128)S(1)} %get-tuple-element.67.a7_ref, ...), custom_call_target="tpu_custom_call" | custom-call | tf_op jit(solution)/shard_map/pallas_call | solution.py:21
  143.0 17.3 %collective-permute-start.15 = (f32[16,96,128]{2,1,0:T(8,128)S(1)}, f32[16,96,128]{2,1,0:T(8,128)S(1)}, u32[]{:S(2)}, u32[]{:S(2)}) collective-permute-start(f32[16,96,128]{2,1,0:T(8,128)S(1)} %get-tuple-element.73.af_ref.a7_ref), channel_id=1, source_target_pairs={{0,1},{1,2},{2,3},{3,4},{4,5},{5,6},{6,7},{8,9},{9,10},{10,11},{11... | collective-permute-start | bytes 2359304 | tf_op jit(solution)/shard_map/ppermute | solution.py:206
  167.5 8.2 %collective-permute-done.17.lo_ref = f32[16,8,128]{2,1,0:T(8,128)S(1)} collective-permute-done((f32[16,8,128]{2,1,0:T(8,128)S(1)}, f32[16,8,128]{2,1,0:T(8,128)S(1)}, u32[]{:S(2)}, u32[]{:S(2)}) %collective-permute-start.17) | collective-permute-done | bytes 65568 | tf_op jit(solution)/shard_map/ppermute | solution.py:206
  179.4 7.6 %shard_map.66 = (f32[16,768,128]{2,1,0:T(8,128)S(1)}, f32[16,96,128]{2,1,0:T(8,128)S(1)}, f32[16,96,128]{2,1,0:T(8,128)S(1)}) custom-call(s32[1]{0:T(128)} %bitcast.core_ref, f32[16,768,128]{2,1,0:T(8,128)S(1)} %get-tuple-element.71.d_ref, f32[16,96,128]{2,1,0:T(8,128)S(1)} %get-tuple-element.74.a0_ref, f32[16,96,128]{2,1,0:T(8,128)S(1)} %get-tuple-element.73.af_ref.a7_ref, ...), custom_call_target="tpu_custom_call" | custom-call | tf_op jit(solution)/shard_map/pallas_call | solution.py:21
  188.4 7.6 %collective-permute-done.19.h_ref = f32[16,96,128]{2,1,0:T(8,128)S(1)} collective-permute-done((f32[16,96,128]{2,1,0:T(8,128)S(1)}, f32[16,96,128]{2,1,0:T(8,128)S(1)}, u32[]{:S(2)}, u32[]{:S(2)}) %collective-permute-start.19) | collective-permute-done | bytes 786464 | tf_op jit(solution)/shard_map/ppermute | solution.py:206
  196.4 17.0 %collective-permute-start.24 = (f32[16,96,128]{2,1,0:T(8,128)S(1)}, f32[16,96,128]{2,1,0:T(8,128)S(1)}, u32[]{:S(2)}, u32[]{:S(2)}) collective-permute-start(f32[16,96,128]{2,1,0:T(8,128)S(1)} %get-tuple-element.81.a7_ref), channel_id=1, source_target_pairs={{0,1},{1,2},{2,3},{3,4},{4,5},{5,6},{6,7},{8,9},{9,10},{10,11},{11... | collective-permute-start | bytes 2359304 | tf_op jit(solution)/shard_map/ppermute | solution.py:206
  216.2 11.2 %collective-permute-done.22.lo_ref = f32[16,8,128]{2,1,0:T(8,128)S(1)} collective-permute-done((f32[16,8,128]{2,1,0:T(8,128)S(1)}, f32[16,8,128]{2,1,0:T(8,128)S(1)}, u32[]{:S(2)}, u32[]{:S(2)}) %collective-permute-start.22) | collective-permute-done | bytes 65568 | tf_op jit(solution)/shard_map/ppermute | solution.py:206
  229.4 7.6 %shard_map.68 = (f32[16,768,128]{2,1,0:T(8,128)S(1)}, f32[16,96,128]{2,1,0:T(8,128)S(1)}, f32[16,96,128]{2,1,0:T(8,128)S(1)}) custom-call(s32[1]{0:T(128)} %bitcast.core_ref, f32[16,768,128]{2,1,0:T(8,128)S(1)} %get-tuple-element.78.d_ref, f32[16,96,128]{2,1,0:T(8,128)S(1)} %get-tuple-element.79.af_ref.a0_ref, f32[16,96,128]{2,1,0:T(8,128)S(1)} %get-tuple-element.81.a7_ref, ...), custom_call_target="tpu_custom_call" | custom-call | tf_op jit(solution)/shard_map/pallas_call | solution.py:21
  237.1 17.3 %collective-permute-start.25 = (f32[16,96,128]{2,1,0:T(8,128)S(1)}, f32[16,96,128]{2,1,0:T(8,128)S(1)}, u32[]{:S(2)}, u32[]{:S(2)}) collective-permute-start(f32[16,96,128]{2,1,0:T(8,128)S(1)} %get-tuple-element.87.af_ref.a7_ref), channel_id=1, source_target_pairs={{0,1},{1,2},{2,3},{3,4},{4,5},{5,6},{6,7},{8,9},{9,10},{10,11},{11... | collective-permute-start | bytes 2359304 | tf_op jit(solution)/shard_map/ppermute | solution.py:206
  261.5 6.7 %collective-permute-done.27.lo_ref = f32[16,8,128]{2,1,0:T(8,128)S(1)} collective-permute-done((f32[16,8,128]{2,1,0:T(8,128)S(1)}, f32[16,8,128]{2,1,0:T(8,128)S(1)}, u32[]{:S(2)}, u32[]{:S(2)}) %collective-permute-start.27) | collective-permute-done | bytes 65568 | tf_op jit(solution)/shard_map/ppermute | solution.py:206
  271.5 8.5 %shard_map.70 = (f32[16,768,128]{2,1,0:T(8,128)S(1)}, f32[16,96,128]{2,1,0:T(8,128)S(1)}, f32[16,96,128]{2,1,0:T(8,128)S(1)}, f32[16,96,128]{2,1,0:T(8,128)S(1)}...) custom-call(s32[1]{0:T(128)} %bitcast.core_ref, f32[16,768,128]{2,1,0:T(8,128)S(1)} %get-tuple-element.85.d_ref, ...), custom_call_target="tpu_custom_call" | custom-call | tf_op jit(solution)/shard_map/pallas_call | solution.py:21
  280.0 8.3 %collective-permute-done.29.h_ref = f32[16,96,128]{2,1,0:T(8,128)S(1)} collective-permute-done((f32[16,96,128]{2,1,0:T(8,128)S(1)}, f32[16,96,128]{2,1,0:T(8,128)S(1)}, u32[]{:S(2)}, u32[]{:S(2)}) %collective-permute-start.29) | collective-permute-done | bytes 786464 | tf_op jit(solution)/shard_map/ppermute | solution.py:206
  288.9 34.4 %all_to_all.10 = f32[16,2,96,128]{3,2,1,0:T(8,128)S(1)} all-to-all(f32[16,2,96,128]{3,2,1,0:T(8,128)S(1)} %get-tuple-element.99), channel_id=1, replica_groups=mesh['rows'=2,'cols'=8,'slabs'=8] {'slabs'}, dimensions={0} | all-to-all | bytes 3145728 | tf_op jit(solution)/shard_map/all_to_all | solution.py:258
  323.8 19.1 %all_to_all.11 = f32[8,2,2,96,128]{4,3,2,1,0:T(8,128)S(1)} all-to-all(f32[8,2,2,96,128]{4,3,2,1,0:T(8,128)S(1)} %broadcast_in_dim.2), channel_id=1, replica_groups=mesh['rows'=2,'cols'=8,'slabs'=8] {'slabs'}, dimensions={0} | all-to-all | bytes 3145728 | tf_op jit(solution)/shard_map/all_to_all | solution.py:265
  342.9 8.5 %finish.1 = (f32[16,768,128]{2,1,0:T(8,128)}, f32[16,768,128]{2,1,0:T(8,128)}) custom-call(f32[16,768,128]{2,1,0:T(8,128)S(1)} %get-tuple-element.92.d_ref, f32[16,96,128]{2,1,0:T(8,128)S(1)} %get-tuple-element.93.a0_ref, f32[16,96,128]{2,1,0:T(8,128)S(1)} %get-tuple-element.98.a7_ref, f32[16,2,96,128]{3,2,1,0:T(8,128)S(1)} %bitcast.56), custom_call_target="tpu_custom_call" | custom-call | tf_op jit(solution)/shard_map/finish/pallas_call | solution.py:192
  (70 shorter events, 63.2 us)
Async XLA Ops:
  3.9 28.9 %collective-permute-start = (f32[16,96,128]{2,1,0:T(8,128)S(1)}, f32[16,96,128]{2,1,0:T(8,128)S(1)}, u32[]{:S(2)}, u32[]{:S(2)}) collective-permute-start(f32[16,96,128]{2,1,0:T(8,128)S(1)} %get-tuple-element.52.a0_ref), channel_id=1, source_target_pairs={{1,0},{2,1},{3,2},{4,3},{5,4},{6,5},{7,6},{9,8},{10,9},{11,10},{12... | collective-permute-start | bytes 2359304 | tf_op jit(solution)/shard_map/ppermute | solution.py:206
  5.4 58.4 %collective-permute-start.4 = (f32[16,96,128]{2,1,0:T(8,128)S(1)}, f32[16,96,128]{2,1,0:T(8,128)S(1)}, u32[]{:S(2)}, u32[]{:S(2)}) collective-permute-start(f32[16,96,128]{2,1,0:T(8,128)S(1)} %get-tuple-element.53.a7_ref), channel_id=1, source_target_pairs={{0,1},{1,2},{2,3},{3,4},{4,5},{5,6},{6,7},{8,9},{9,10},{10,11},{11... | collective-permute-start | bytes 2359304 | tf_op jit(solution)/shard_map/ppermute | solution.py:206
  11.5 21.3 %collective-permute-start.1 = (f32[768,128]{1,0:T(8,128)S(1)}, f32[768,128]{1,0:T(8,128)S(1)}, u32[]{:S(2)}, u32[]{:S(2)}) collective-permute-start(f32[768,128]{1,0:T(8,128)S(1)} %get-tuple-element.54), channel_id=1, source_target_pairs={{0,64},{64,0},{1,65},{65,1},{2,66},{66,2},{3,67},{67,3},{4,68},{68... | collective-permute-start | bytes 1179656 | tf_op jit(solution)/shard_map/ppermute | solution.py:229
  11.6 17.7 %collective-permute-start.2 = (f32[16,8,128]{2,1,0:T(8,128)S(1)}, f32[16,8,128]{2,1,0:T(8,128)S(1)}, u32[]{:S(2)}, u32[]{:S(2)}) collective-permute-start(f32[16,8,128]{2,1,0:T(8,128)S(1)} %get-tuple-element.55), channel_id=1, source_target_pairs={{0,8},{8,16},{16,24},{24,32},{32,40},{40,48},{48,56},{1,9},{9,17},... | collective-permute-start | bytes 196616 | tf_op jit(solution)/shard_map/ppermute | solution.py:206
  15.1 17.7 %collective-permute-start.3 = (f32[16,8,128]{2,1,0:T(8,128)S(1)}, f32[16,8,128]{2,1,0:T(8,128)S(1)}, u32[]{:S(2)}, u32[]{:S(2)}) collective-permute-start(f32[16,8,128]{2,1,0:T(8,128)S(1)} %get-tuple-element.56), channel_id=1, source_target_pairs={{8,0},{16,8},{24,16},{32,24},{40,32},{48,40},{56,48},{9,1},{17,9},... | collective-permute-start | bytes 196616 | tf_op jit(solution)/shard_map/ppermute | solution.py:206
  46.0 37.3 %collective-permute-start.5 = (f32[16,96,128]{2,1,0:T(8,128)S(1)}, f32[16,96,128]{2,1,0:T(8,128)S(1)}, u32[]{:S(2)}, u32[]{:S(2)}) collective-permute-start(f32[16,96,128]{2,1,0:T(8,128)S(1)} %get-tuple-element.59.af_ref.a7_ref), channel_id=1, source_target_pairs={{0,1},{1,2},{2,3},{3,4},{4,5},{5,6},{6,7},{8,9},{9,10},{10,11},{11... | collective-permute-start | bytes 2359304 | tf_op jit(solution)/shard_map/ppermute | solution.py:206
  64.4 35.5 %collective-permute-start.9 = (f32[16,96,128]{2,1,0:T(8,128)S(1)}, f32[16,96,128]{2,1,0:T(8,128)S(1)}, u32[]{:S(2)}, u32[]{:S(2)}) collective-permute-start(f32[16,96,128]{2,1,0:T(8,128)S(1)} %get-tuple-element.60.a0_ref), channel_id=1, source_target_pairs={{1,0},{2,1},{3,2},{4,3},{5,4},{6,5},{7,6},{9,8},{10,9},{11,10},{12... | collective-permute-start | bytes 2359304 | tf_op jit(solution)/shard_map/ppermute | solution.py:206
  65.9 17.4 %collective-permute-start.6 = (f32[768,128]{1,0:T(8,128)S(1)}, f32[768,128]{1,0:T(8,128)S(1)}, u32[]{:S(2)}, u32[]{:S(2)}) collective-permute-start(f32[768,128]{1,0:T(8,128)S(1)} %get-tuple-element.61), channel_id=1, source_target_pairs={{0,64},{64,0},{1,65},{65,1},{2,66},{66,2},{3,67},{67,3},{4,68},{68... | collective-permute-start | bytes 1179656 | tf_op jit(solution)/shard_map/ppermute | solution.py:229
  66.0 14.8 %collective-permute-start.7 = (f32[16,8,128]{2,1,0:T(8,128)S(1)}, f32[16,8,128]{2,1,0:T(8,128)S(1)}, u32[]{:S(2)}, u32[]{:S(2)}) collective-permute-start(f32[16,8,128]{2,1,0:T(8,128)S(1)} %get-tuple-element.62), channel_id=1, source_target_pairs={{0,8},{8,16},{16,24},{24,32},{32,40},{40,48},{48,56},{1,9},{9,17},... | collective-permute-start | bytes 196616 | tf_op jit(solution)/shard_map/ppermute | solution.py:206
  91.0 44.3 %collective-permute-start.10 = (f32[16,96,128]{2,1,0:T(8,128)S(1)}, f32[16,96,128]{2,1,0:T(8,128)S(1)}, u32[]{:S(2)}, u32[]{:S(2)}) collective-permute-start(f32[16,96,128]{2,1,0:T(8,128)S(1)} %get-tuple-element.65.af_ref.a0_ref), channel_id=1, source_target_pairs={{1,0},{2,1},{3,2},{4,3},{5,4},{6,5},{7,6},{9,8},{10,9},{11,10},{12... | collective-permute-start | bytes 2359304 | tf_op jit(solution)/shard_map/ppermute | solution.py:206
  100.3 59.9 %collective-permute-start.14 = (f32[16,96,128]{2,1,0:T(8,128)S(1)}, f32[16,96,128]{2,1,0:T(8,128)S(1)}, u32[]{:S(2)}, u32[]{:S(2)}) collective-permute-start(f32[16,96,128]{2,1,0:T(8,128)S(1)} %get-tuple-element.67.a7_ref), channel_id=1, source_target_pairs={{0,1},{1,2},{2,3},{3,4},{4,5},{5,6},{6,7},{8,9},{9,10},{10,11},{11... | collective-permute-start | bytes 2359304 | tf_op jit(solution)/shard_map/ppermute | solution.py:206
  117.4 17.9 %collective-permute-start.11 = (f32[768,128]{1,0:T(8,128)S(1)}, f32[768,128]{1,0:T(8,128)S(1)}, u32[]{:S(2)}, u32[]{:S(2)}) collective-permute-start(f32[768,128]{1,0:T(8,128)S(1)} %get-tuple-element.68), channel_id=1, source_target_pairs={{0,64},{64,0},{1,65},{65,1},{2,66},{66,2},{3,67},{67,3},{4,68},{68... | collective-permute-start | bytes 1179656 | tf_op jit(solution)/shard_map/ppermute | solution.py:229
  117.5 15.7 %collective-permute-start.12 = (f32[16,8,128]{2,1,0:T(8,128)S(1)}, f32[16,8,128]{2,1,0:T(8,128)S(1)}, u32[]{:S(2)}, u32[]{:S(2)}) collective-permute-start(f32[16,8,128]{2,1,0:T(8,128)S(1)} %get-tuple-element.69), channel_id=1, source_target_pairs={{0,8},{8,16},{16,24},{24,32},{32,40},{40,48},{48,56},{1,9},{9,17},... | collective-permute-start | bytes 196616 | tf_op jit(solution)/shard_map/ppermute | solution.py:206
  119.1 16.3 %collective-permute-start.13 = (f32[16,8,128]{2,1,0:T(8,128)S(1)}, f32[16,8,128]{2,1,0:T(8,128)S(1)}, u32[]{:S(2)}, u32[]{:S(2)}) collective-permute-start(f32[16,8,128]{2,1,0:T(8,128)S(1)} %get-tuple-element.70), channel_id=1, source_target_pairs={{8,0},{16,8},{24,16},{32,24},{40,32},{48,40},{56,48},{9,1},{17,9},... | collective-permute-start | bytes 196616 | tf_op jit(solution)/shard_map/ppermute | solution.py:206
  143.0 36.4 %collective-permute-start.15 = (f32[16,96,128]{2,1,0:T(8,128)S(1)}, f32[16,96,128]{2,1,0:T(8,128)S(1)}, u32[]{:S(2)}, u32[]{:S(2)}) collective-permute-start(f32[16,96,128]{2,1,0:T(8,128)S(1)} %get-tuple-element.73.af_ref.a7_ref), channel_id=1, source_target_pairs={{0,1},{1,2},{2,3},{3,4},{4,5},{5,6},{6,7},{8,9},{9,10},{10,11},{11... | collective-permute-start | bytes 2359304 | tf_op jit(solution)/shard_map/ppermute | solution.py:206
  160.8 35.2 %collective-permute-start.19 = (f32[16,96,128]{2,1,0:T(8,128)S(1)}, f32[16,96,128]{2,1,0:T(8,128)S(1)}, u32[]{:S(2)}, u32[]{:S(2)}) collective-permute-start(f32[16,96,128]{2,1,0:T(8,128)S(1)} %get-tuple-element.74.a0_ref), channel_id=1, source_target_pairs={{1,0},{2,1},{3,2},{4,3},{5,4},{6,5},{7,6},{9,8},{10,9},{11,10},{12... | collective-permute-start | bytes 2359304 | tf_op jit(solution)/shard_map/ppermute | solution.py:206
  162.1 17.4 %collective-permute-start.16 = (f32[768,128]{1,0:T(8,128)S(1)}, f32[768,128]{1,0:T(8,128)S(1)}, u32[]{:S(2)}, u32[]{:S(2)}) collective-permute-start(f32[768,128]{1,0:T(8,128)S(1)} %get-tuple-element.75), channel_id=1, source_target_pairs={{0,64},{64,0},{1,65},{65,1},{2,66},{66,2},{3,67},{67,3},{4,68},{68... | collective-permute-start | bytes 1179656 | tf_op jit(solution)/shard_map/ppermute | solution.py:229
  187.1 42.4 %collective-permute-start.20 = (f32[16,96,128]{2,1,0:T(8,128)S(1)}, f32[16,96,128]{2,1,0:T(8,128)S(1)}, u32[]{:S(2)}, u32[]{:S(2)}) collective-permute-start(f32[16,96,128]{2,1,0:T(8,128)S(1)} %get-tuple-element.79.af_ref.a0_ref), channel_id=1, source_target_pairs={{1,0},{2,1},{3,2},{4,3},{5,4},{6,5},{7,6},{9,8},{10,9},{11,10},{12... | collective-permute-start | bytes 2359304 | tf_op jit(solution)/shard_map/ppermute | solution.py:206
  196.4 57.9 %collective-permute-start.24 = (f32[16,96,128]{2,1,0:T(8,128)S(1)}, f32[16,96,128]{2,1,0:T(8,128)S(1)}, u32[]{:S(2)}, u32[]{:S(2)}) collective-permute-start(f32[16,96,128]{2,1,0:T(8,128)S(1)} %get-tuple-element.81.a7_ref), channel_id=1, source_target_pairs={{0,1},{1,2},{2,3},{3,4},{4,5},{5,6},{6,7},{8,9},{9,10},{10,11},{11... | collective-permute-start | bytes 2359304 | tf_op jit(solution)/shard_map/ppermute | solution.py:206
  213.4 16.0 %collective-permute-start.21 = (f32[768,128]{1,0:T(8,128)S(1)}, f32[768,128]{1,0:T(8,128)S(1)}, u32[]{:S(2)}, u32[]{:S(2)}) collective-permute-start(f32[768,128]{1,0:T(8,128)S(1)} %get-tuple-element.82), channel_id=1, source_target_pairs={{0,64},{64,0},{1,65},{65,1},{2,66},{66,2},{3,67},{67,3},{4,68},{68... | collective-permute-start | bytes 1179656 | tf_op jit(solution)/shard_map/ppermute | solution.py:229
  214.9 14.5 %collective-permute-start.23 = (f32[16,8,128]{2,1,0:T(8,128)S(1)}, f32[16,8,128]{2,1,0:T(8,128)S(1)}, u32[]{:S(2)}, u32[]{:S(2)}) collective-permute-start(f32[16,8,128]{2,1,0:T(8,128)S(1)} %get-tuple-element.84), channel_id=1, source_target_pairs={{8,0},{16,8},{24,16},{32,24},{40,32},{48,40},{56,48},{9,1},{17,9},... | collective-permute-start | bytes 196616 | tf_op jit(solution)/shard_map/ppermute | solution.py:206
  237.1 34.4 %collective-permute-start.25 = (f32[16,96,128]{2,1,0:T(8,128)S(1)}, f32[16,96,128]{2,1,0:T(8,128)S(1)}, u32[]{:S(2)}, u32[]{:S(2)}) collective-permute-start(f32[16,96,128]{2,1,0:T(8,128)S(1)} %get-tuple-element.87.af_ref.a7_ref), channel_id=1, source_target_pairs={{0,1},{1,2},{2,3},{3,4},{4,5},{5,6},{6,7},{8,9},{9,10},{10,11},{11... | collective-permute-start | bytes 2359304 | tf_op jit(solution)/shard_map/ppermute | solution.py:206
  254.9 33.4 %collective-permute-start.29 = (f32[16,96,128]{2,1,0:T(8,128)S(1)}, f32[16,96,128]{2,1,0:T(8,128)S(1)}, u32[]{:S(2)}, u32[]{:S(2)}) collective-permute-start(f32[16,96,128]{2,1,0:T(8,128)S(1)} %get-tuple-element.88.a0_ref), channel_id=1, source_target_pairs={{1,0},{2,1},{3,2},{4,3},{5,4},{6,5},{7,6},{9,8},{10,9},{11,10},{12... | collective-permute-start | bytes 2359304 | tf_op jit(solution)/shard_map/ppermute | solution.py:206
  256.2 15.3 %collective-permute-start.26 = (f32[768,128]{1,0:T(8,128)S(1)}, f32[768,128]{1,0:T(8,128)S(1)}, u32[]{:S(2)}, u32[]{:S(2)}) collective-permute-start(f32[768,128]{1,0:T(8,128)S(1)} %get-tuple-element.89), channel_id=1, source_target_pairs={{0,64},{64,0},{1,65},{65,1},{2,66},{66,2},{3,67},{67,3},{4,68},{68... | collective-permute-start | bytes 1179656 | tf_op jit(solution)/shard_map/ppermute | solution.py:229
  (12 other events, 158.1 us)

commit v3 on v2

--- a/solution.py
+++ b/solution.py
@@ -16,7 +16,7 @@
     return [pltpu.with_memory_space_constraint(v, pltpu.VMEM) for v in values]
 
 
-def local_call(body, outs, core, *values, scratch=()):
+def local_call(body, outs, core, *values, scratch=(), aliases={}):
     spec = pl.BlockSpec(memory_space=pltpu.VMEM)
     return pl.pallas_call(
         body,
@@ -24,8 +24,30 @@
         out_specs=[spec] * len(outs),
         out_shape=[pltpu.VMEM(shape, jnp.float32) for shape in outs],
         scratch_shapes=list(scratch),
+        input_output_aliases=aliases,
         compiler_params=pltpu.CompilerParams(vmem_limit_bytes=4 << 20),
     )(core, *in_vmem(*values))
+
+
+def fetch_body(*refs):
+    count = len(refs) // 3
+    copies = [pltpu.make_async_copy(refs[n], refs[count + n], refs[2 * count + n]) for n in range(count)]
+    for copy in copies:
+        copy.start()
+    for copy in copies:
+        copy.wait()
+
+
+def fetch_call(*values):
+    return pl.pallas_call(
+        fetch_body,
+        in_specs=[pl.BlockSpec(memory_space=pltpu.HBM)] * len(values),
+        out_specs=[pl.BlockSpec(memory_space=pltpu.VMEM)] * len(values),
+        out_shape=[pltpu.VMEM(v.shape, v.dtype) for v in values],
+        scratch_shapes=[pltpu.SemaphoreType.DMA] * len(values),
+        compiler_params=pltpu.CompilerParams(vmem_limit_bytes=4 << 20),
+        name="fetch",
+    )(*[pltpu.with_memory_space_constraint(v, pltpu.HBM) for v in values])
 
 
 def prep_body(core_ref, d_ref, a0_ref, a7_ref, row_ref, lo_ref, hi_ref):
@@ -108,6 +130,7 @@
         af_ref[j] = exact
         ps_ref[j] = out_ref[j, pl.ds(other, ni, stride=SUB), :]
         if last:
+            out_ref[j, pl.ds(first, ni, stride=SUB), :] = exact
             centre = out_ref[j, pl.ds(3, ni, stride=SUB), :]
             moved = exact - centre
             s1 = moved
@@ -151,10 +174,10 @@
     row_out[pl.ds(other, ni, stride=SUB), :] = as_ref[edge]
 
 
-def sums_body(core_ref, ps_ref, fk_ref, h_ref, mid_ref, s1_ref, s2_ref, as_ref, v_ref, *, first):
+def sums_body(core_ref, d_ref, ps_ref, fk_ref, h_ref, mid_ref, s1_ref, s2_ref, end_ref, v_ref, *, first):
     def some(j, carry):
         exact = fixed_plane(j, ps_ref, h_ref, fk_ref, first)
-        as_ref[j] = exact
+        end_ref[j, pl.ds(7 - first, ps_ref.shape[1], stride=SUB), :] = exact
         moved = exact - mid_ref[j]
         s1 = s1_ref[j] + moved
         s2 = s2_ref[j] + moved * moved
@@ -165,39 +188,43 @@
     lax.fori_loop(0, ps_ref.shape[0], some, 0)
 
 
-def finish_body(d_ref, a0_ref, a7_ref, v_ref, anomaly_ref, end_ref):
-    j = pl.program_id(0)
-    ni = a0_ref.shape[1]
-    end_ref[0] = d_ref[j]
-    end_ref[0, pl.ds(0, ni, stride=SUB), :] = a0_ref[j]
-    end_ref[0, pl.ds(7, ni, stride=SUB), :] = a7_ref[j]
+def finish_body(d_ref, v_ref, anomaly_ref, end_ref, made, sent, sent_end):
+    nj = d_ref.shape[0]
+    ni = v_ref.shape[2]
     unroll = 8
-
-    def some(n, carry):
-        for m in range(unroll):
-            i = n * unroll + m
-            at = pl.multiple_of(i * SUB, SUB)
-            mean = v_ref[j, 0, pl.ds(i, 1), :]
-            scale = v_ref[j, 1, pl.ds(i, 1), :]
-            anomaly_ref[0, pl.ds(at, SUB), :] = (end_ref[0, pl.ds(at, SUB), :] - mean) * scale
-        return carry
-
-    lax.fori_loop(0, ni // unroll, some, 0)
-
-
-def finish_call(d, a0, a7, v):
-    nj, rows, lanes = d.shape
-    whole = pl.BlockSpec(memory_space=pltpu.VMEM)
-    block = pl.BlockSpec((1, rows, lanes), lambda j: (j, 0, 0))
+    whole = pltpu.make_async_copy(d_ref, end_ref, sent_end)
+    whole.start()
+
+    def plane(j, carry):
+        def some(n, inner):
+            for m in range(unroll):
+                i = n * unroll + m
+                at = pl.multiple_of(i * SUB, SUB)
+                mean = v_ref[j, 0, pl.ds(i, 1), :]
+                scale = v_ref[j, 1, pl.ds(i, 1), :]
+                made[j, pl.ds(at, SUB), :] = (d_ref[j, pl.ds(at, SUB), :] - mean) * scale
+            return inner
+
+        lax.fori_loop(0, ni // unroll, some, 0)
+        pltpu.make_async_copy(made.at[j], anomaly_ref.at[j], sent).start()
+        return carry
+
+    lax.fori_loop(0, nj, plane, 0)
+    pltpu.make_async_copy(made, anomaly_ref, sent).wait()
+    whole.wait()
+
+
+def finish_call(d, v):
+    hbm = pl.BlockSpec(memory_space=pltpu.HBM)
     return pl.pallas_call(
         finish_body,
-        grid=(nj,),
-        in_specs=[whole] * 4,
-        out_specs=[block, block],
+        in_specs=[pl.BlockSpec(memory_space=pltpu.VMEM)] * 2,
+        out_specs=[hbm, hbm],
         out_shape=[jax.ShapeDtypeStruct(d.shape, d.dtype)] * 2,
-        compiler_params=pltpu.CompilerParams(vmem_limit_bytes=4 << 20),
+        scratch_shapes=[pltpu.VMEM(d.shape, d.dtype), pltpu.SemaphoreType.DMA, pltpu.SemaphoreType.DMA],
+        compiler_params=pltpu.CompilerParams(vmem_limit_bytes=10 << 20),
         name="finish",
-    )(*in_vmem(d, a0, a7, v))
+    )(*in_vmem(d, v))
 
 
 def send(value, axis, direction):
@@ -215,9 +242,7 @@
     cube, square, line = d.shape, (nj, ni, lanes), (nj, SUB, lanes)
     edges = [cube[1:], line, line]
     ring = [pltpu.VMEM((3 * (cube[1] + 2 * SUB), lanes), jnp.float32)]
-    plane_0, plane_7, row_send, lo_send, hi_send = local_call(
-        prep_body, [square, square, *edges], core, d
-    )
+    plane_0, plane_7, row_send, lo_send, hi_send = local_call(prep_body, [square, square, *edges], core, d)
     planes = {0: plane_0, 7: plane_7}
     halo = {}
     for t in range(STEPS):
@@ -230,6 +255,8 @@
         hi = send(lo_send, "cols", -1)
         lo = send(hi_send, "cols", 1)
         halo[other] = send(planes[first], "slabs", -1 if first == 0 else 1)
+        if t == 0:
+            fj, fi, fk = fetch_call(fj, fi, fk)
         d, exact, part, *sums = local_call(
             functools.partial(step_body, first=first, last=last),
             [cube] + [square] * (5 if last else 2),
@@ -241,20 +268,17 @@
             break
         early = send(exact, "slabs", -1 if first == 0 else 1)
         fixed, row_send, lo_send, hi_send = local_call(
-            functools.partial(fix_body, first=first),
-            [square, *edges],
-            core,
-            *(part, fk, halo[other], exact, d),
+            functools.partial(fix_body, first=first), [square, *edges], core, *(part, fk, halo[other], exact, d)
         )
         planes = {first: exact, other: fixed}
         halo = {other: early}
-    fixed, v = local_call(
+    end, v = local_call(
         functools.partial(sums_body, first=first),
-        [square, (nj, 2, ni, lanes)],
+        [cube, (nj, 2, ni, lanes)],
         core,
-        *(part, fk, halo[other], *sums),
+        *(d, part, fk, halo[other], *sums),
+        aliases={1: 0},
     )
-    planes = {first: exact, other: fixed}
     got = lax.all_to_all(v, "slabs", 0, 0, tiled=True)
     got = got.reshape(slabs, nj // slabs, 2, ni, lanes)
     mean = jnp.sum(got[:, :, 0], axis=0) / slabs
@@ -263,7 +287,7 @@
     mine = jnp.stack([mean, lax.rsqrt(line_variance + 0.0001)], axis=1)
     copies = jnp.broadcast_to(mine[None], (slabs, *mine.shape))
     v = lax.all_to_all(copies, "slabs", 0, 0, tiled=True).reshape(nj, 2, ni, lanes)
-    anomaly, end = finish_call(d, planes[0], planes[7], v)
+    anomaly, end = finish_call(end, v)
     return (anomaly.reshape(density.shape), end.reshape(density.shape))
 
 

time: 352 us -> 343 us (0.974)
  waiting for transfers between devices: 103 us -> 96.5 us
  local copies, waits for them, and re-layouts: 8.68 us -> 2.95 us
    ppermute x24, waiting for transfers between devices: 103 us -> 96.4 us  [send(): lax.ppermute(value, axis, up if direction > 0 else [(b, a) for a, b in up])]
    unnamed x12 -> x2, local copies, waits for them, and re-layouts: 8.51 us -> 2.78 us
    pallas_call x1 -> x2, Pallas kernels: 8.49 us -> 11 us  [the longest x1 6.43 us: fetch_call(): pl.pallas_call(fetch_body, in_specs=[pl.BlockSpec(memory_space=pltpu.HBM)...]
  transfers between devices with their start and end apart: 30 -> 30, of which waited for: 15 -> 15; matrix products, arithmetic and copies ran while one was open for 0% -> 0% of each run, Pallas kernels for 14% -> 16%
where the time goes in v3:
time: 343 us; the launch traced here: 342 us
  starting transfers between devices  125 us (36%)
  waiting for transfers between devices  96.5 us (28%)
  Pallas kernels  62 us (18%)
  blocking collectives  54.2 us (16%)
    ppermute x24, starting transfers between devices, send(): lax.ppermute(value, axis, up if direction > 0 else [(b, a) for a, b in up])  125 us
    ppermute x24, waiting for transfers between devices, send(): lax.ppermute(value, axis, up if direction > 0 else [(b, a) for a, b in up])  96.4 us
    pallas_call x13, Pallas kernels, local_call(): pl.pallas_call(body, in_specs=[pl.BlockSpec(memory_space=pltpu.SMEM)] + [...  51 us
    all_to_all x1, blocking collectives, body(): got = lax.all_to_all(v, 'slabs', 0, 0, tiled=True)  35.1 us
    all_to_all x1, blocking collectives, body(): lax.all_to_all(copies, 'slabs', 0, 0, tiled=True).reshape(nj, 2, ni, lanes)  19.1 us
  transfers between devices with their start and end apart: 30, of which 15 were waited for; matrix products, arithmetic and copies ran while one was open for 0% of the time, Pallas kernels for 16%

profile of v3, /device:TPU:0, one launch (start us, length us, event | category | flops | bytes accessed | tf_op | source)
XLA Modules:
  0.0 342.3 jit_solution(7896466086559971618)
XLA Ops:
  5.1 6.1 %collective-permute-start.4 = (f32[16,96,128]{2,1,0:T(8,128)S(1)}, f32[16,96,128]{2,1,0:T(8,128)S(1)}, u32[]{:S(2)}, u32[]{:S(2)}) collective-permute-start(f32[16,96,128]{2,1,0:T(8,128)S(1)} %get-tuple-element.55.a7_ref), channel_id=1, source_target_pairs={{0,1},{1,2},{2,3},{3,4},{4,5},{5,6},{6,7},{8,9},{9,10},{10,11},{11... | collective-permute-start | bytes 2359304 | tf_op jit(solution)/shard_map/ppermute | solution.py:233
  16.1 6.4 %fetch.1 = (f32[16,768,128]{2,1,0:T(8,128)S(1)}, f32[16,768,128]{2,1,0:T(8,128)S(1)}, f32[16,768,128]{2,1,0:T(8,128)S(1)}) custom-call(f32[16,768,128]{2,1,0:T(8,128)} %bitcast.35, f32[16,768,128]{2,1,0:T(8,128)} %bitcast.36, f32[16,768,128]{2,1,0:T(8,128)} %bitcast.37), custom_call_target="tpu_custom_call" | custom-call | tf_op jit(solution)/shard_map/fetch/pallas_call | solution.py:42
  22.5 6.4 %collective-permute-done.2.lo_ref = f32[16,8,128]{2,1,0:T(8,128)S(1)} collective-permute-done((f32[16,8,128]{2,1,0:T(8,128)S(1)}, f32[16,8,128]{2,1,0:T(8,128)S(1)}, u32[]{:S(2)}, u32[]{:S(2)}) %collective-permute-start.2) | collective-permute-done | bytes 65568 | tf_op jit(solution)/shard_map/ppermute | solution.py:233
  32.5 7.6 %shard_map.60 = (f32[16,768,128]{2,1,0:T(8,128)S(1)}, f32[16,96,128]{2,1,0:T(8,128)S(1)}, f32[16,96,128]{2,1,0:T(8,128)S(1)}) custom-call(s32[1]{0:T(128)} %bitcast.core_ref, f32[16,768,128]{2,1,0:T(8,128)S(1)} %bitcast.31, f32[16,96,128]{2,1,0:T(8,128)S(1)} %get-tuple-element.54.a0_ref, f32[16,96,128]{2,1,0:T(8,128)S(1)} %get-tuple-element.55.a7_ref, ...), custom_call_target="tpu_custom_call" | custom-call | tf_op jit(solution)/shard_map/pallas_call | solution.py:21
  40.2 17.8 %collective-permute-start.5 = (f32[16,96,128]{2,1,0:T(8,128)S(1)}, f32[16,96,128]{2,1,0:T(8,128)S(1)}, u32[]{:S(2)}, u32[]{:S(2)}) collective-permute-start(f32[16,96,128]{2,1,0:T(8,128)S(1)} %get-tuple-element.64.af_ref.a7_ref), channel_id=1, source_target_pairs={{0,1},{1,2},{2,3},{3,4},{4,5},{5,6},{6,7},{8,9},{9,10},{10,11},{11... | collective-permute-start | bytes 2359304 | tf_op jit(solution)/shard_map/ppermute | solution.py:233
  63.8 11.2 %collective-permute-done.7.lo_ref = f32[16,8,128]{2,1,0:T(8,128)S(1)} collective-permute-done((f32[16,8,128]{2,1,0:T(8,128)S(1)}, f32[16,8,128]{2,1,0:T(8,128)S(1)}, u32[]{:S(2)}, u32[]{:S(2)}) %collective-permute-start.7) | collective-permute-done | bytes 65568 | tf_op jit(solution)/shard_map/ppermute | solution.py:233
  77.5 7.6 %shard_map.62 = (f32[16,768,128]{2,1,0:T(8,128)S(1)}, f32[16,96,128]{2,1,0:T(8,128)S(1)}, f32[16,96,128]{2,1,0:T(8,128)S(1)}) custom-call(s32[1]{0:T(128)} %bitcast.core_ref, f32[16,768,128]{2,1,0:T(8,128)S(1)} %get-tuple-element.62.d_ref, f32[16,96,128]{2,1,0:T(8,128)S(1)} %get-tuple-element.65.a0_ref, f32[16,96,128]{2,1,0:T(8,128)S(1)} %get-tuple-element.64.af_ref.a7_ref, ...), custom_call_target="tpu_custom_call" | custom-call | tf_op jit(solution)/shard_map/pallas_call | solution.py:21
  86.4 7.5 %collective-permute-done.9.h_ref = f32[16,96,128]{2,1,0:T(8,128)S(1)} collective-permute-done((f32[16,96,128]{2,1,0:T(8,128)S(1)}, f32[16,96,128]{2,1,0:T(8,128)S(1)}, u32[]{:S(2)}, u32[]{:S(2)}) %collective-permute-start.9) | collective-permute-done | bytes 786464 | tf_op jit(solution)/shard_map/ppermute | solution.py:233
  94.5 17.1 %collective-permute-start.14 = (f32[16,96,128]{2,1,0:T(8,128)S(1)}, f32[16,96,128]{2,1,0:T(8,128)S(1)}, u32[]{:S(2)}, u32[]{:S(2)}) collective-permute-start(f32[16,96,128]{2,1,0:T(8,128)S(1)} %get-tuple-element.72.a7_ref), channel_id=1, source_target_pairs={{0,1},{1,2},{2,3},{3,4},{4,5},{5,6},{6,7},{8,9},{9,10},{10,11},{11... | collective-permute-start | bytes 2359304 | tf_op jit(solution)/shard_map/ppermute | solution.py:233
  114.5 12.9 %collective-permute-done.12.lo_ref = f32[16,8,128]{2,1,0:T(8,128)S(1)} collective-permute-done((f32[16,8,128]{2,1,0:T(8,128)S(1)}, f32[16,8,128]{2,1,0:T(8,128)S(1)}, u32[]{:S(2)}, u32[]{:S(2)}) %collective-permute-start.12) | collective-permute-done | bytes 65568 | tf_op jit(solution)/shard_map/ppermute | solution.py:233
  129.5 7.6 %shard_map.64 = (f32[16,768,128]{2,1,0:T(8,128)S(1)}, f32[16,96,128]{2,1,0:T(8,128)S(1)}, f32[16,96,128]{2,1,0:T(8,128)S(1)}) custom-call(s32[1]{0:T(128)} %bitcast.core_ref, f32[16,768,128]{2,1,0:T(8,128)S(1)} %get-tuple-element.69.d_ref, f32[16,96,128]{2,1,0:T(8,128)S(1)} %get-tuple-element.70.af_ref.a0_ref, f32[16,96,128]{2,1,0:T(8,128)S(1)} %get-tuple-element.72.a7_ref, ...), custom_call_target="tpu_custom_call" | custom-call | tf_op jit(solution)/shard_map/pallas_call | solution.py:21
  137.1 17.3 %collective-permute-start.15 = (f32[16,96,128]{2,1,0:T(8,128)S(1)}, f32[16,96,128]{2,1,0:T(8,128)S(1)}, u32[]{:S(2)}, u32[]{:S(2)}) collective-permute-start(f32[16,96,128]{2,1,0:T(8,128)S(1)} %get-tuple-element.78.af_ref.a7_ref), channel_id=1, source_target_pairs={{0,1},{1,2},{2,3},{3,4},{4,5},{5,6},{6,7},{8,9},{9,10},{10,11},{11... | collective-permute-start | bytes 2359304 | tf_op jit(solution)/shard_map/ppermute | solution.py:233
  161.6 8.2 %collective-permute-done.17.lo_ref = f32[16,8,128]{2,1,0:T(8,128)S(1)} collective-permute-done((f32[16,8,128]{2,1,0:T(8,128)S(1)}, f32[16,8,128]{2,1,0:T(8,128)S(1)}, u32[]{:S(2)}, u32[]{:S(2)}) %collective-permute-start.17) | collective-permute-done | bytes 65568 | tf_op jit(solution)/shard_map/ppermute | solution.py:233
  173.5 7.6 %shard_map.66 = (f32[16,768,128]{2,1,0:T(8,128)S(1)}, f32[16,96,128]{2,1,0:T(8,128)S(1)}, f32[16,96,128]{2,1,0:T(8,128)S(1)}) custom-call(s32[1]{0:T(128)} %bitcast.core_ref, f32[16,768,128]{2,1,0:T(8,128)S(1)} %get-tuple-element.76.d_ref, f32[16,96,128]{2,1,0:T(8,128)S(1)} %get-tuple-element.79.a0_ref, f32[16,96,128]{2,1,0:T(8,128)S(1)} %get-tuple-element.78.af_ref.a7_ref, ...), custom_call_target="tpu_custom_call" | custom-call | tf_op jit(solution)/shard_map/pallas_call | solution.py:21
  182.5 7.6 %collective-permute-done.19.h_ref = f32[16,96,128]{2,1,0:T(8,128)S(1)} collective-permute-done((f32[16,96,128]{2,1,0:T(8,128)S(1)}, f32[16,96,128]{2,1,0:T(8,128)S(1)}, u32[]{:S(2)}, u32[]{:S(2)}) %collective-permute-start.19) | collective-permute-done | bytes 786464 | tf_op jit(solution)/shard_map/ppermute | solution.py:233
  190.6 17.0 %collective-permute-start.24 = (f32[16,96,128]{2,1,0:T(8,128)S(1)}, f32[16,96,128]{2,1,0:T(8,128)S(1)}, u32[]{:S(2)}, u32[]{:S(2)}) collective-permute-start(f32[16,96,128]{2,1,0:T(8,128)S(1)} %get-tuple-element.86.a7_ref), channel_id=1, source_target_pairs={{0,1},{1,2},{2,3},{3,4},{4,5},{5,6},{6,7},{8,9},{9,10},{10,11},{11... | collective-permute-start | bytes 2359304 | tf_op jit(solution)/shard_map/ppermute | solution.py:233
  210.3 11.2 %collective-permute-done.22.lo_ref = f32[16,8,128]{2,1,0:T(8,128)S(1)} collective-permute-done((f32[16,8,128]{2,1,0:T(8,128)S(1)}, f32[16,8,128]{2,1,0:T(8,128)S(1)}, u32[]{:S(2)}, u32[]{:S(2)}) %collective-permute-start.22) | collective-permute-done | bytes 65568 | tf_op jit(solution)/shard_map/ppermute | solution.py:233
  223.6 7.6 %shard_map.68 = (f32[16,768,128]{2,1,0:T(8,128)S(1)}, f32[16,96,128]{2,1,0:T(8,128)S(1)}, f32[16,96,128]{2,1,0:T(8,128)S(1)}) custom-call(s32[1]{0:T(128)} %bitcast.core_ref, f32[16,768,128]{2,1,0:T(8,128)S(1)} %get-tuple-element.83.d_ref, f32[16,96,128]{2,1,0:T(8,128)S(1)} %get-tuple-element.84.af_ref.a0_ref, f32[16,96,128]{2,1,0:T(8,128)S(1)} %get-tuple-element.86.a7_ref, ...), custom_call_target="tpu_custom_call" | custom-call | tf_op jit(solution)/shard_map/pallas_call | solution.py:21
  231.2 17.3 %collective-permute-start.25 = (f32[16,96,128]{2,1,0:T(8,128)S(1)}, f32[16,96,128]{2,1,0:T(8,128)S(1)}, u32[]{:S(2)}, u32[]{:S(2)}) collective-permute-start(f32[16,96,128]{2,1,0:T(8,128)S(1)} %get-tuple-element.92.af_ref.a7_ref), channel_id=1, source_target_pairs={{0,1},{1,2},{2,3},{3,4},{4,5},{5,6},{6,7},{8,9},{9,10},{10,11},{11... | collective-permute-start | bytes 2359304 | tf_op jit(solution)/shard_map/ppermute | solution.py:233
  255.6 6.7 %collective-permute-done.27.lo_ref = f32[16,8,128]{2,1,0:T(8,128)S(1)} collective-permute-done((f32[16,8,128]{2,1,0:T(8,128)S(1)}, f32[16,8,128]{2,1,0:T(8,128)S(1)}, u32[]{:S(2)}, u32[]{:S(2)}) %collective-permute-start.27) | collective-permute-done | bytes 65568 | tf_op jit(solution)/shard_map/ppermute | solution.py:233
  265.6 9.3 %shard_map.70 = (f32[16,768,128]{2,1,0:T(8,128)S(1)}, f32[16,96,128]{2,1,0:T(8,128)}, f32[16,96,128]{2,1,0:T(8,128)S(1)}, f32[16,96,128]{2,1,0:T(8,128)S(1)}, f3...) custom-call(s32[1]{0:T(128)} %bitcast.core_ref, f32[16,768,128]{2,1,0:T(8,128)S(1)} %get-tuple-element.90.d_ref, ...), custom_call_target="tpu_custom_call" | custom-call | tf_op jit(solution)/shard_map/pallas_call | solution.py:21
  274.9 7.6 %collective-permute-done.29.h_ref = f32[16,96,128]{2,1,0:T(8,128)S(1)} collective-permute-done((f32[16,96,128]{2,1,0:T(8,128)S(1)}, f32[16,96,128]{2,1,0:T(8,128)S(1)}, u32[]{:S(2)}, u32[]{:S(2)}) %collective-permute-start.29) | collective-permute-done | bytes 786464 | tf_op jit(solution)/shard_map/ppermute | solution.py:233
  283.0 35.1 %all_to_all.10 = f32[16,2,96,128]{3,2,1,0:T(8,128)S(1)} all-to-all(f32[16,2,96,128]{3,2,1,0:T(8,128)S(1)} %get-tuple-element.103), channel_id=1, replica_groups=mesh['rows'=2,'cols'=8,'slabs'=8] {'slabs'}, dimensions={0} | all-to-all | bytes 3145728 | tf_op jit(solution)/shard_map/all_to_all | solution.py:282
  318.6 19.1 %all_to_all.11 = f32[8,2,2,96,128]{4,3,2,1,0:T(8,128)S(1)} all-to-all(f32[8,2,2,96,128]{4,3,2,1,0:T(8,128)S(1)} %broadcast_in_dim.2), channel_id=1, replica_groups=mesh['rows'=2,'cols'=8,'slabs'=8] {'slabs'}, dimensions={0} | all-to-all | bytes 3145728 | tf_op jit(solution)/shard_map/all_to_all | solution.py:289
  (61 shorter events, 61.5 us)
Async XLA Ops:
  3.8 28.7 %collective-permute-start = (f32[16,96,128]{2,1,0:T(8,128)S(1)}, f32[16,96,128]{2,1,0:T(8,128)S(1)}, u32[]{:S(2)}, u32[]{:S(2)}) collective-permute-start(f32[16,96,128]{2,1,0:T(8,128)S(1)} %get-tuple-element.54.a0_ref), channel_id=1, source_target_pairs={{1,0},{2,1},{3,2},{4,3},{5,4},{6,5},{7,6},{9,8},{10,9},{11,10},{12... | collective-permute-start | bytes 2359304 | tf_op jit(solution)/shard_map/ppermute | solution.py:233
  5.1 52.9 %collective-permute-start.4 = (f32[16,96,128]{2,1,0:T(8,128)S(1)}, f32[16,96,128]{2,1,0:T(8,128)S(1)}, u32[]{:S(2)}, u32[]{:S(2)}) collective-permute-start(f32[16,96,128]{2,1,0:T(8,128)S(1)} %get-tuple-element.55.a7_ref), channel_id=1, source_target_pairs={{0,1},{1,2},{2,3},{3,4},{4,5},{5,6},{6,7},{8,9},{9,10},{10,11},{11... | collective-permute-start | bytes 2359304 | tf_op jit(solution)/shard_map/ppermute | solution.py:233
  11.2 21.3 %collective-permute-start.1 = (f32[768,128]{1,0:T(8,128)S(1)}, f32[768,128]{1,0:T(8,128)S(1)}, u32[]{:S(2)}, u32[]{:S(2)}) collective-permute-start(f32[768,128]{1,0:T(8,128)S(1)} %get-tuple-element.56), channel_id=1, source_target_pairs={{0,64},{64,0},{1,65},{65,1},{2,66},{66,2},{3,67},{67,3},{4,68},{68... | collective-permute-start | bytes 1179656 | tf_op jit(solution)/shard_map/ppermute | solution.py:254
  11.3 17.7 %collective-permute-start.2 = (f32[16,8,128]{2,1,0:T(8,128)S(1)}, f32[16,8,128]{2,1,0:T(8,128)S(1)}, u32[]{:S(2)}, u32[]{:S(2)}) collective-permute-start(f32[16,8,128]{2,1,0:T(8,128)S(1)} %get-tuple-element.57), channel_id=1, source_target_pairs={{0,8},{8,16},{16,24},{24,32},{32,40},{40,48},{48,56},{1,9},{9,17},... | collective-permute-start | bytes 196616 | tf_op jit(solution)/shard_map/ppermute | solution.py:233
  14.8 17.7 %collective-permute-start.3 = (f32[16,8,128]{2,1,0:T(8,128)S(1)}, f32[16,8,128]{2,1,0:T(8,128)S(1)}, u32[]{:S(2)}, u32[]{:S(2)}) collective-permute-start(f32[16,8,128]{2,1,0:T(8,128)S(1)} %get-tuple-element.58), channel_id=1, source_target_pairs={{8,0},{16,8},{24,16},{32,24},{40,32},{48,40},{56,48},{9,1},{17,9},... | collective-permute-start | bytes 196616 | tf_op jit(solution)/shard_map/ppermute | solution.py:233
  40.2 37.3 %collective-permute-start.5 = (f32[16,96,128]{2,1,0:T(8,128)S(1)}, f32[16,96,128]{2,1,0:T(8,128)S(1)}, u32[]{:S(2)}, u32[]{:S(2)}) collective-permute-start(f32[16,96,128]{2,1,0:T(8,128)S(1)} %get-tuple-element.64.af_ref.a7_ref), channel_id=1, source_target_pairs={{0,1},{1,2},{2,3},{3,4},{4,5},{5,6},{6,7},{8,9},{9,10},{10,11},{11... | collective-permute-start | bytes 2359304 | tf_op jit(solution)/shard_map/ppermute | solution.py:233
  58.5 35.5 %collective-permute-start.9 = (f32[16,96,128]{2,1,0:T(8,128)S(1)}, f32[16,96,128]{2,1,0:T(8,128)S(1)}, u32[]{:S(2)}, u32[]{:S(2)}) collective-permute-start(f32[16,96,128]{2,1,0:T(8,128)S(1)} %get-tuple-element.65.a0_ref), channel_id=1, source_target_pairs={{1,0},{2,1},{3,2},{4,3},{5,4},{6,5},{7,6},{9,8},{10,9},{11,10},{12... | collective-permute-start | bytes 2359304 | tf_op jit(solution)/shard_map/ppermute | solution.py:233
  59.8 17.7 %collective-permute-start.6 = (f32[768,128]{1,0:T(8,128)S(1)}, f32[768,128]{1,0:T(8,128)S(1)}, u32[]{:S(2)}, u32[]{:S(2)}) collective-permute-start(f32[768,128]{1,0:T(8,128)S(1)} %get-tuple-element.66), channel_id=1, source_target_pairs={{0,64},{64,0},{1,65},{65,1},{2,66},{66,2},{3,67},{67,3},{4,68},{68... | collective-permute-start | bytes 1179656 | tf_op jit(solution)/shard_map/ppermute | solution.py:254
  59.9 15.1 %collective-permute-start.7 = (f32[16,8,128]{2,1,0:T(8,128)S(1)}, f32[16,8,128]{2,1,0:T(8,128)S(1)}, u32[]{:S(2)}, u32[]{:S(2)}) collective-permute-start(f32[16,8,128]{2,1,0:T(8,128)S(1)} %get-tuple-element.67), channel_id=1, source_target_pairs={{0,8},{8,16},{16,24},{24,32},{32,40},{40,48},{48,56},{1,9},{9,17},... | collective-permute-start | bytes 196616 | tf_op jit(solution)/shard_map/ppermute | solution.py:233
  62.5 15.0 %collective-permute-start.8 = (f32[16,8,128]{2,1,0:T(8,128)S(1)}, f32[16,8,128]{2,1,0:T(8,128)S(1)}, u32[]{:S(2)}, u32[]{:S(2)}) collective-permute-start(f32[16,8,128]{2,1,0:T(8,128)S(1)} %get-tuple-element.68), channel_id=1, source_target_pairs={{8,0},{16,8},{24,16},{32,24},{40,32},{48,40},{56,48},{9,1},{17,9},... | collective-permute-start | bytes 196616 | tf_op jit(solution)/shard_map/ppermute | solution.py:233
  85.1 44.3 %collective-permute-start.10 = (f32[16,96,128]{2,1,0:T(8,128)S(1)}, f32[16,96,128]{2,1,0:T(8,128)S(1)}, u32[]{:S(2)}, u32[]{:S(2)}) collective-permute-start(f32[16,96,128]{2,1,0:T(8,128)S(1)} %get-tuple-element.70.af_ref.a0_ref), channel_id=1, source_target_pairs={{1,0},{2,1},{3,2},{4,3},{5,4},{6,5},{7,6},{9,8},{10,9},{11,10},{12... | collective-permute-start | bytes 2359304 | tf_op jit(solution)/shard_map/ppermute | solution.py:233
  94.5 59.9 %collective-permute-start.14 = (f32[16,96,128]{2,1,0:T(8,128)S(1)}, f32[16,96,128]{2,1,0:T(8,128)S(1)}, u32[]{:S(2)}, u32[]{:S(2)}) collective-permute-start(f32[16,96,128]{2,1,0:T(8,128)S(1)} %get-tuple-element.72.a7_ref), channel_id=1, source_target_pairs={{0,1},{1,2},{2,3},{3,4},{4,5},{5,6},{6,7},{8,9},{9,10},{10,11},{11... | collective-permute-start | bytes 2359304 | tf_op jit(solution)/shard_map/ppermute | solution.py:233
  111.5 17.9 %collective-permute-start.11 = (f32[768,128]{1,0:T(8,128)S(1)}, f32[768,128]{1,0:T(8,128)S(1)}, u32[]{:S(2)}, u32[]{:S(2)}) collective-permute-start(f32[768,128]{1,0:T(8,128)S(1)} %get-tuple-element.73), channel_id=1, source_target_pairs={{0,64},{64,0},{1,65},{65,1},{2,66},{66,2},{3,67},{67,3},{4,68},{68... | collective-permute-start | bytes 1179656 | tf_op jit(solution)/shard_map/ppermute | solution.py:254
  111.6 15.7 %collective-permute-start.12 = (f32[16,8,128]{2,1,0:T(8,128)S(1)}, f32[16,8,128]{2,1,0:T(8,128)S(1)}, u32[]{:S(2)}, u32[]{:S(2)}) collective-permute-start(f32[16,8,128]{2,1,0:T(8,128)S(1)} %get-tuple-element.74), channel_id=1, source_target_pairs={{0,8},{8,16},{16,24},{24,32},{32,40},{40,48},{48,56},{1,9},{9,17},... | collective-permute-start | bytes 196616 | tf_op jit(solution)/shard_map/ppermute | solution.py:233
  113.2 16.3 %collective-permute-start.13 = (f32[16,8,128]{2,1,0:T(8,128)S(1)}, f32[16,8,128]{2,1,0:T(8,128)S(1)}, u32[]{:S(2)}, u32[]{:S(2)}) collective-permute-start(f32[16,8,128]{2,1,0:T(8,128)S(1)} %get-tuple-element.75), channel_id=1, source_target_pairs={{8,0},{16,8},{24,16},{32,24},{40,32},{48,40},{56,48},{9,1},{17,9},... | collective-permute-start | bytes 196616 | tf_op jit(solution)/shard_map/ppermute | solution.py:233
  137.1 36.4 %collective-permute-start.15 = (f32[16,96,128]{2,1,0:T(8,128)S(1)}, f32[16,96,128]{2,1,0:T(8,128)S(1)}, u32[]{:S(2)}, u32[]{:S(2)}) collective-permute-start(f32[16,96,128]{2,1,0:T(8,128)S(1)} %get-tuple-element.78.af_ref.a7_ref), channel_id=1, source_target_pairs={{0,1},{1,2},{2,3},{3,4},{4,5},{5,6},{6,7},{8,9},{9,10},{10,11},{11... | collective-permute-start | bytes 2359304 | tf_op jit(solution)/shard_map/ppermute | solution.py:233
  154.9 35.2 %collective-permute-start.19 = (f32[16,96,128]{2,1,0:T(8,128)S(1)}, f32[16,96,128]{2,1,0:T(8,128)S(1)}, u32[]{:S(2)}, u32[]{:S(2)}) collective-permute-start(f32[16,96,128]{2,1,0:T(8,128)S(1)} %get-tuple-element.79.a0_ref), channel_id=1, source_target_pairs={{1,0},{2,1},{3,2},{4,3},{5,4},{6,5},{7,6},{9,8},{10,9},{11,10},{12... | collective-permute-start | bytes 2359304 | tf_op jit(solution)/shard_map/ppermute | solution.py:233
  156.2 17.4 %collective-permute-start.16 = (f32[768,128]{1,0:T(8,128)S(1)}, f32[768,128]{1,0:T(8,128)S(1)}, u32[]{:S(2)}, u32[]{:S(2)}) collective-permute-start(f32[768,128]{1,0:T(8,128)S(1)} %get-tuple-element.80), channel_id=1, source_target_pairs={{0,64},{64,0},{1,65},{65,1},{2,66},{66,2},{3,67},{67,3},{4,68},{68... | collective-permute-start | bytes 1179656 | tf_op jit(solution)/shard_map/ppermute | solution.py:254
  181.2 42.4 %collective-permute-start.20 = (f32[16,96,128]{2,1,0:T(8,128)S(1)}, f32[16,96,128]{2,1,0:T(8,128)S(1)}, u32[]{:S(2)}, u32[]{:S(2)}) collective-permute-start(f32[16,96,128]{2,1,0:T(8,128)S(1)} %get-tuple-element.84.af_ref.a0_ref), channel_id=1, source_target_pairs={{1,0},{2,1},{3,2},{4,3},{5,4},{6,5},{7,6},{9,8},{10,9},{11,10},{12... | collective-permute-start | bytes 2359304 | tf_op jit(solution)/shard_map/ppermute | solution.py:233
  190.6 57.9 %collective-permute-start.24 = (f32[16,96,128]{2,1,0:T(8,128)S(1)}, f32[16,96,128]{2,1,0:T(8,128)S(1)}, u32[]{:S(2)}, u32[]{:S(2)}) collective-permute-start(f32[16,96,128]{2,1,0:T(8,128)S(1)} %get-tuple-element.86.a7_ref), channel_id=1, source_target_pairs={{0,1},{1,2},{2,3},{3,4},{4,5},{5,6},{6,7},{8,9},{9,10},{10,11},{11... | collective-permute-start | bytes 2359304 | tf_op jit(solution)/shard_map/ppermute | solution.py:233
  207.5 16.0 %collective-permute-start.21 = (f32[768,128]{1,0:T(8,128)S(1)}, f32[768,128]{1,0:T(8,128)S(1)}, u32[]{:S(2)}, u32[]{:S(2)}) collective-permute-start(f32[768,128]{1,0:T(8,128)S(1)} %get-tuple-element.87), channel_id=1, source_target_pairs={{0,64},{64,0},{1,65},{65,1},{2,66},{66,2},{3,67},{67,3},{4,68},{68... | collective-permute-start | bytes 1179656 | tf_op jit(solution)/shard_map/ppermute | solution.py:254
  231.2 34.4 %collective-permute-start.25 = (f32[16,96,128]{2,1,0:T(8,128)S(1)}, f32[16,96,128]{2,1,0:T(8,128)S(1)}, u32[]{:S(2)}, u32[]{:S(2)}) collective-permute-start(f32[16,96,128]{2,1,0:T(8,128)S(1)} %get-tuple-element.92.af_ref.a7_ref), channel_id=1, source_target_pairs={{0,1},{1,2},{2,3},{3,4},{4,5},{5,6},{6,7},{8,9},{9,10},{10,11},{11... | collective-permute-start | bytes 2359304 | tf_op jit(solution)/shard_map/ppermute | solution.py:233
  249.0 33.4 %collective-permute-start.29 = (f32[16,96,128]{2,1,0:T(8,128)S(1)}, f32[16,96,128]{2,1,0:T(8,128)S(1)}, u32[]{:S(2)}, u32[]{:S(2)}) collective-permute-start(f32[16,96,128]{2,1,0:T(8,128)S(1)} %get-tuple-element.93.a0_ref), channel_id=1, source_target_pairs={{1,0},{2,1},{3,2},{4,3},{5,4},{6,5},{7,6},{9,8},{10,9},{11,10},{12... | collective-permute-start | bytes 2359304 | tf_op jit(solution)/shard_map/ppermute | solution.py:233
  250.3 15.3 %collective-permute-start.26 = (f32[768,128]{1,0:T(8,128)S(1)}, f32[768,128]{1,0:T(8,128)S(1)}, u32[]{:S(2)}, u32[]{:S(2)}) collective-permute-start(f32[768,128]{1,0:T(8,128)S(1)} %get-tuple-element.94), channel_id=1, source_target_pairs={{0,64},{64,0},{1,65},{65,1},{2,66},{66,2},{3,67},{67,3},{4,68},{68... | collective-permute-start | bytes 1179656 | tf_op jit(solution)/shard_map/ppermute | solution.py:254
  (7 other events, 81.3 us)

commit v4 on v3

--- a/solution.py
+++ b/solution.py
@@ -16,13 +16,15 @@
     return [pltpu.with_memory_space_constraint(v, pltpu.VMEM) for v in values]
 
 
-def local_call(body, outs, core, *values, scratch=(), aliases={}):
+def local_call(body, outs, core, *values, scratch=(), aliases={}, stored=()):
     spec = pl.BlockSpec(memory_space=pltpu.VMEM)
+    hbm = pl.BlockSpec(memory_space=pltpu.HBM)
     return pl.pallas_call(
         body,
         in_specs=[pl.BlockSpec(memory_space=pltpu.SMEM)] + [spec] * len(values),
-        out_specs=[spec] * len(outs),
-        out_shape=[pltpu.VMEM(shape, jnp.float32) for shape in outs],
+        out_specs=[spec] * len(outs) + [hbm] * len(stored),
+        out_shape=[pltpu.VMEM(shape, jnp.float32) for shape in outs]
+        + [jax.ShapeDtypeStruct(shape, jnp.float32) for shape in stored],
         scratch_shapes=list(scratch),
         input_output_aliases=aliases,
         compiler_params=pltpu.CompilerParams(vmem_limit_bytes=4 << 20),
@@ -50,24 +52,41 @@
     )(*[pltpu.with_memory_space_constraint(v, pltpu.HBM) for v in values])
 
 
-def prep_body(core_ref, d_ref, a0_ref, a7_ref, row_ref, lo_ref, hi_ref):
-    nj, rows, _ = d_ref.shape
-    ni = rows // SUB
-
-    def some(j, carry):
-        a0_ref[j] = d_ref[j, pl.ds(0, ni, stride=SUB), :]
-        a7_ref[j] = d_ref[j, pl.ds(7, ni, stride=SUB), :]
-        lo_ref[j] = d_ref[j, pl.ds(0, SUB), :]
-        hi_ref[j] = d_ref[j, pl.ds(rows - SUB, SUB), :]
-        return carry
-
-    lax.fori_loop(0, nj, some, 0)
-    row_ref[...] = d_ref[(1 - core_ref[0]) * (nj - 1)]
+def prep_body(core_ref, d_ref, *refs, parts):
+    outs, sems = refs[: len(parts)], refs[len(parts) :]
+    nj, ni, _, _ = d_ref.shape
+    edge = (1 - core_ref[0]) * (nj - 1)
+    source = {
+        0: lambda: d_ref.at[:, :, 0, :],
+        7: lambda: d_ref.at[:, :, 7, :],
+        "row": lambda: d_ref.at[edge],
+        "low": lambda: d_ref.at[:, 0],
+        "high": lambda: d_ref.at[:, ni - 1],
+    }
+    copies = [pltpu.make_async_copy(source[p](), o, s) for p, o, s in zip(parts, outs, sems)]
+    for copy in copies:
+        copy.start()
+    for copy in copies:
+        copy.wait()
+
+
+def prep_call(core, density, *parts):
+    nj, ni, nk, lanes = density.shape
+    shape = {0: (nj, ni, lanes), 7: (nj, ni, lanes), "row": (ni, nk, lanes), "low": (nj, nk, lanes), "high": (nj, nk, lanes)}
+    return pl.pallas_call(
+        functools.partial(prep_body, parts=parts),
+        in_specs=[pl.BlockSpec(memory_space=pltpu.SMEM), pl.BlockSpec(memory_space=pltpu.HBM)],
+        out_specs=[pl.BlockSpec(memory_space=pltpu.VMEM)] * len(parts),
+        out_shape=[pltpu.VMEM(shape[p], density.dtype) for p in parts],
+        scratch_shapes=[pltpu.SemaphoreType.DMA] * len(parts),
+        compiler_params=pltpu.CompilerParams(vmem_limit_bytes=4 << 20),
+        name="prep",
+    )(core, pltpu.with_memory_space_constraint(density, pltpu.HBM))
 
 
 def step_body(core_ref, d_ref, a0_ref, a7_ref, h_ref, row_ref, lo_ref, hi_ref, fj_ref, fi_ref, fk_ref, *rest, first, last):
     if last:
-        out_ref, af_ref, ps_ref, mid_ref, s1_ref, s2_ref, ring = rest
+        out_ref, af_ref, ps_ref, mid_ref, s1_ref, s2_ref, end_ref, ring, sent = rest
     else:
         out_ref, af_ref, ps_ref, ring = rest
     nj, rows, _ = d_ref.shape
@@ -142,9 +161,12 @@
             mid_ref[j] = centre
             s1_ref[j] = s1
             s2_ref[j] = s2
+            pltpu.make_async_copy(out_ref.at[j], end_ref.at[j], sent).start()
         return carry
 
     lax.fori_loop(0, nj, plane, 0)
+    if last:
+        pltpu.make_async_copy(out_ref, end_ref, sent).wait()
 
 
 def fixed_plane(j, ps_ref, h_ref, fk_ref, first):
@@ -174,10 +196,11 @@
     row_out[pl.ds(other, ni, stride=SUB), :] = as_ref[edge]
 
 
-def sums_body(core_ref, d_ref, ps_ref, fk_ref, h_ref, mid_ref, s1_ref, s2_ref, end_ref, v_ref, *, first):
+def sums_body(core_ref, d_ref, ps_ref, fk_ref, h_ref, mid_ref, s1_ref, s2_ref, full_ref, as_ref, v_ref, *, first):
     def some(j, carry):
         exact = fixed_plane(j, ps_ref, h_ref, fk_ref, first)
-        end_ref[j, pl.ds(7 - first, ps_ref.shape[1], stride=SUB), :] = exact
+        as_ref[j] = exact
+        full_ref[j, pl.ds(7 - first, ps_ref.shape[1], stride=SUB), :] = exact
         moved = exact - mid_ref[j]
         s1 = s1_ref[j] + moved
         s2 = s2_ref[j] + moved * moved
@@ -188,12 +211,12 @@
     lax.fori_loop(0, ps_ref.shape[0], some, 0)
 
 
-def finish_body(d_ref, v_ref, anomaly_ref, end_ref, made, sent, sent_end):
+def finish_body(d_ref, as_ref, v_ref, _, anomaly_ref, end_ref, made, sent, sent_end, *, other):
     nj = d_ref.shape[0]
     ni = v_ref.shape[2]
     unroll = 8
-    whole = pltpu.make_async_copy(d_ref, end_ref, sent_end)
-    whole.start()
+    patch = pltpu.make_async_copy(as_ref, end_ref.at[:, :, other, :], sent_end)
+    patch.start()
 
     def plane(j, carry):
         def some(n, inner):
@@ -211,20 +234,22 @@
 
     lax.fori_loop(0, nj, plane, 0)
     pltpu.make_async_copy(made, anomaly_ref, sent).wait()
-    whole.wait()
-
-
-def finish_call(d, v):
+    patch.wait()
+
+
+def finish_call(d, fixed, v, end, other):
     hbm = pl.BlockSpec(memory_space=pltpu.HBM)
+    vmem = pl.BlockSpec(memory_space=pltpu.VMEM)
     return pl.pallas_call(
-        finish_body,
-        in_specs=[pl.BlockSpec(memory_space=pltpu.VMEM)] * 2,
+        functools.partial(finish_body, other=other),
+        in_specs=[vmem, vmem, vmem, hbm],
         out_specs=[hbm, hbm],
-        out_shape=[jax.ShapeDtypeStruct(d.shape, d.dtype)] * 2,
+        out_shape=[jax.ShapeDtypeStruct(d.shape, d.dtype), jax.ShapeDtypeStruct(end.shape, d.dtype)],
         scratch_shapes=[pltpu.VMEM(d.shape, d.dtype), pltpu.SemaphoreType.DMA, pltpu.SemaphoreType.DMA],
+        input_output_aliases={3: 1},
         compiler_params=pltpu.CompilerParams(vmem_limit_bytes=10 << 20),
         name="finish",
-    )(*in_vmem(d, v))
+    )(*in_vmem(d, fixed, v), end)
 
 
 def send(value, axis, direction):
@@ -242,7 +267,9 @@
     cube, square, line = d.shape, (nj, ni, lanes), (nj, SUB, lanes)
     edges = [cube[1:], line, line]
     ring = [pltpu.VMEM((3 * (cube[1] + 2 * SUB), lanes), jnp.float32)]
-    plane_0, plane_7, row_send, lo_send, hi_send = local_call(prep_body, [square, square, *edges], core, d)
+    (plane_0,) = prep_call(core, density, 0)
+    plane_7, row_send, lo_send, hi_send = prep_call(core, density, 7, "row", "low", "high")
+    row_send = row_send.reshape(ni * nk, lanes)
     planes = {0: plane_0, 7: plane_7}
     halo = {}
     for t in range(STEPS):
@@ -262,7 +289,8 @@
             [cube] + [square] * (5 if last else 2),
             core,
             *(d, planes[0], planes[7], halo[first], row, lo, hi, fj, fi, fk),
-            scratch=ring,
+            scratch=ring + [pltpu.SemaphoreType.DMA] * last,
+            stored=[cube] * last,
         )
         if last:
             break
@@ -272,9 +300,10 @@
         )
         planes = {first: exact, other: fixed}
         halo = {other: early}
-    end, v = local_call(
+    *sums, end = sums
+    full, fixed, v = local_call(
         functools.partial(sums_body, first=first),
-        [cube, (nj, 2, ni, lanes)],
+        [cube, square, (nj, 2, ni, lanes)],
         core,
         *(d, part, fk, halo[other], *sums),
         aliases={1: 0},
@@ -287,7 +316,7 @@
     mine = jnp.stack([mean, lax.rsqrt(line_variance + 0.0001)], axis=1)
     copies = jnp.broadcast_to(mine[None], (slabs, *mine.shape))
     v = lax.all_to_all(copies, "slabs", 0, 0, tiled=True).reshape(nj, 2, ni, lanes)
-    anomaly, end = finish_call(end, v)
+    anomaly, end = finish_call(full, fixed, v, end.reshape(density.shape), other)
     return (anomaly.reshape(density.shape), end.reshape(density.shape))
 
 

time: 343 us -> 340 us (level)
    pallas_call x13 -> x12, Pallas kernels: 51 us -> 51.4 us  [local_call(): pl.pallas_call(body, in_specs=[pl.BlockSpec(memory_space=pltpu.SMEM)] + [...]
  transfers between devices with their start and end apart: 30 -> 30, of which waited for: 15 -> 15; matrix products, arithmetic and copies ran while one was open for 0% -> 0% of each run, Pallas kernels for 16% -> 17%
where the time goes in v4:
time: 340 us; the launch traced here: 339 us
  starting transfers between devices  124 us (36%)
  waiting for transfers between devices  95.5 us (28%)
  Pallas kernels  63.4 us (19%)
  blocking collectives  55.1 us (16%)
    ppermute x24, starting transfers between devices, send(): lax.ppermute(value, axis, up if direction > 0 else [(b, a) for a, b in up])  123 us
    ppermute x24, waiting for transfers between devices, send(): lax.ppermute(value, axis, up if direction > 0 else [(b, a) for a, b in up])  95.5 us
    pallas_call x12, Pallas kernels, local_call(): pl.pallas_call(body, in_specs=[pl.BlockSpec(memory_space=pltpu.SMEM)] + [...  51.4 us
    all_to_all x1, blocking collectives, body(): got = lax.all_to_all(v, 'slabs', 0, 0, tiled=True)  36 us
    all_to_all x1, blocking collectives, body(): lax.all_to_all(copies, 'slabs', 0, 0, tiled=True).reshape(nj, 2, ni, lanes)  19.1 us
  transfers between devices with their start and end apart: 30, of which 15 were waited for; matrix products, arithmetic and copies ran while one was open for 0% of the time, Pallas kernels for 17%

profile of v4, /device:TPU:0, one launch (start us, length us, event | category | flops | bytes accessed | tf_op | source)
XLA Modules:
  0.0 339.5 jit_solution(13220544352181910390)
XLA Ops:
  4.5 6.1 %collective-permute-start.4 = (f32[16,96,128]{2,1,0:T(8,128)S(1)}, f32[16,96,128]{2,1,0:T(8,128)S(1)}, u32[]{:S(2)}, u32[]{:S(2)}) collective-permute-start(f32[16,96,128]{2,1,0:T(8,128)S(1)} %get-tuple-element.55.a7_ref), channel_id=1, source_target_pairs={{0,1},{1,2},{2,3},{3,4},{4,5},{5,6},{6,7},{8,9},{9,10},{10,11},{11... | collective-permute-start | bytes 2359304 | tf_op jit(solution)/shard_map/ppermute | solution.py:258
  15.6 6.6 %fetch.1 = (f32[16,768,128]{2,1,0:T(8,128)S(1)}, f32[16,768,128]{2,1,0:T(8,128)S(1)}, f32[16,768,128]{2,1,0:T(8,128)S(1)}) custom-call(f32[16,768,128]{2,1,0:T(8,128)} %bitcast.39, f32[16,768,128]{2,1,0:T(8,128)} %bitcast.40, f32[16,768,128]{2,1,0:T(8,128)} %bitcast.41), custom_call_target="tpu_custom_call" | custom-call | tf_op jit(solution)/shard_map/fetch/pallas_call | solution.py:44
  22.1 6.3 %collective-permute-done.2.lo_ref = f32[16,8,128]{2,1,0:T(8,128)S(1)} collective-permute-done((f32[16,8,128]{2,1,0:T(8,128)S(1)}, f32[16,8,128]{2,1,0:T(8,128)S(1)}, u32[]{:S(2)}, u32[]{:S(2)}) %collective-permute-start.2) | collective-permute-done | bytes 65568 | tf_op jit(solution)/shard_map/ppermute | solution.py:258
  32.0 7.7 %shard_map.59 = (f32[16,768,128]{2,1,0:T(8,128)S(1)}, f32[16,96,128]{2,1,0:T(8,128)S(1)}, f32[16,96,128]{2,1,0:T(8,128)S(1)}) custom-call(s32[1]{0:T(128)} %bitcast.core_ref, f32[16,768,128]{2,1,0:T(8,128)S(1)} %bitcast.33, f32[16,96,128]{2,1,0:T(8,128)S(1)} %prep.2.a0_ref, f32[16,96,128]{2,1,0:T(8,128)S(1)} %get-tuple-element.55.a7_ref, ...), custom_call_target="tpu_custom_call" | custom-call | tf_op jit(solution)/shard_map/pallas_call | solution.py:22
  39.6 16.3 %collective-permute-start.5 = (f32[16,96,128]{2,1,0:T(8,128)S(1)}, f32[16,96,128]{2,1,0:T(8,128)S(1)}, u32[]{:S(2)}, u32[]{:S(2)}) collective-permute-start(f32[16,96,128]{2,1,0:T(8,128)S(1)} %get-tuple-element.64.af_ref.a7_ref), channel_id=1, source_target_pairs={{0,1},{1,2},{2,3},{3,4},{4,5},{5,6},{6,7},{8,9},{9,10},{10,11},{11... | collective-permute-start | bytes 2359304 | tf_op jit(solution)/shard_map/ppermute | solution.py:258
  61.8 11.2 %collective-permute-done.7.lo_ref = f32[16,8,128]{2,1,0:T(8,128)S(1)} collective-permute-done((f32[16,8,128]{2,1,0:T(8,128)S(1)}, f32[16,8,128]{2,1,0:T(8,128)S(1)}, u32[]{:S(2)}, u32[]{:S(2)}) %collective-permute-start.7) | collective-permute-done | bytes 65568 | tf_op jit(solution)/shard_map/ppermute | solution.py:258
  75.5 7.6 %shard_map.61 = (f32[16,768,128]{2,1,0:T(8,128)S(1)}, f32[16,96,128]{2,1,0:T(8,128)S(1)}, f32[16,96,128]{2,1,0:T(8,128)S(1)}) custom-call(s32[1]{0:T(128)} %bitcast.core_ref, f32[16,768,128]{2,1,0:T(8,128)S(1)} %get-tuple-element.62.d_ref, f32[16,96,128]{2,1,0:T(8,128)S(1)} %get-tuple-element.65.a0_ref, f32[16,96,128]{2,1,0:T(8,128)S(1)} %get-tuple-element.64.af_ref.a7_ref, ...), custom_call_target="tpu_custom_call" | custom-call | tf_op jit(solution)/shard_map/pallas_call | solution.py:22
  84.5 7.5 %collective-permute-done.9.h_ref = f32[16,96,128]{2,1,0:T(8,128)S(1)} collective-permute-done((f32[16,96,128]{2,1,0:T(8,128)S(1)}, f32[16,96,128]{2,1,0:T(8,128)S(1)}, u32[]{:S(2)}, u32[]{:S(2)}) %collective-permute-start.9) | collective-permute-done | bytes 786464 | tf_op jit(solution)/shard_map/ppermute | solution.py:258
  92.5 17.1 %collective-permute-start.14 = (f32[16,96,128]{2,1,0:T(8,128)S(1)}, f32[16,96,128]{2,1,0:T(8,128)S(1)}, u32[]{:S(2)}, u32[]{:S(2)}) collective-permute-start(f32[16,96,128]{2,1,0:T(8,128)S(1)} %get-tuple-element.72.a7_ref), channel_id=1, source_target_pairs={{0,1},{1,2},{2,3},{3,4},{4,5},{5,6},{6,7},{8,9},{9,10},{10,11},{11... | collective-permute-start | bytes 2359304 | tf_op jit(solution)/shard_map/ppermute | solution.py:258
  112.5 12.9 %collective-permute-done.12.lo_ref = f32[16,8,128]{2,1,0:T(8,128)S(1)} collective-permute-done((f32[16,8,128]{2,1,0:T(8,128)S(1)}, f32[16,8,128]{2,1,0:T(8,128)S(1)}, u32[]{:S(2)}, u32[]{:S(2)}) %collective-permute-start.12) | collective-permute-done | bytes 65568 | tf_op jit(solution)/shard_map/ppermute | solution.py:258
  127.5 7.6 %shard_map.63 = (f32[16,768,128]{2,1,0:T(8,128)S(1)}, f32[16,96,128]{2,1,0:T(8,128)S(1)}, f32[16,96,128]{2,1,0:T(8,128)S(1)}) custom-call(s32[1]{0:T(128)} %bitcast.core_ref, f32[16,768,128]{2,1,0:T(8,128)S(1)} %get-tuple-element.69.d_ref, f32[16,96,128]{2,1,0:T(8,128)S(1)} %get-tuple-element.70.af_ref.a0_ref, f32[16,96,128]{2,1,0:T(8,128)S(1)} %get-tuple-element.72.a7_ref, ...), custom_call_target="tpu_custom_call" | custom-call | tf_op jit(solution)/shard_map/pallas_call | solution.py:22
  135.1 17.3 %collective-permute-start.15 = (f32[16,96,128]{2,1,0:T(8,128)S(1)}, f32[16,96,128]{2,1,0:T(8,128)S(1)}, u32[]{:S(2)}, u32[]{:S(2)}) collective-permute-start(f32[16,96,128]{2,1,0:T(8,128)S(1)} %get-tuple-element.78.af_ref.a7_ref), channel_id=1, source_target_pairs={{0,1},{1,2},{2,3},{3,4},{4,5},{5,6},{6,7},{8,9},{9,10},{10,11},{11... | collective-permute-start | bytes 2359304 | tf_op jit(solution)/shard_map/ppermute | solution.py:258
  159.7 8.2 %collective-permute-done.17.lo_ref = f32[16,8,128]{2,1,0:T(8,128)S(1)} collective-permute-done((f32[16,8,128]{2,1,0:T(8,128)S(1)}, f32[16,8,128]{2,1,0:T(8,128)S(1)}, u32[]{:S(2)}, u32[]{:S(2)}) %collective-permute-start.17) | collective-permute-done | bytes 65568 | tf_op jit(solution)/shard_map/ppermute | solution.py:258
  171.6 7.6 %shard_map.65 = (f32[16,768,128]{2,1,0:T(8,128)S(1)}, f32[16,96,128]{2,1,0:T(8,128)S(1)}, f32[16,96,128]{2,1,0:T(8,128)S(1)}) custom-call(s32[1]{0:T(128)} %bitcast.core_ref, f32[16,768,128]{2,1,0:T(8,128)S(1)} %get-tuple-element.76.d_ref, f32[16,96,128]{2,1,0:T(8,128)S(1)} %get-tuple-element.79.a0_ref, f32[16,96,128]{2,1,0:T(8,128)S(1)} %get-tuple-element.78.af_ref.a7_ref, ...), custom_call_target="tpu_custom_call" | custom-call | tf_op jit(solution)/shard_map/pallas_call | solution.py:22
  180.5 7.6 %collective-permute-done.19.h_ref = f32[16,96,128]{2,1,0:T(8,128)S(1)} collective-permute-done((f32[16,96,128]{2,1,0:T(8,128)S(1)}, f32[16,96,128]{2,1,0:T(8,128)S(1)}, u32[]{:S(2)}, u32[]{:S(2)}) %collective-permute-start.19) | collective-permute-done | bytes 786464 | tf_op jit(solution)/shard_map/ppermute | solution.py:258
  188.6 17.0 %collective-permute-start.24 = (f32[16,96,128]{2,1,0:T(8,128)S(1)}, f32[16,96,128]{2,1,0:T(8,128)S(1)}, u32[]{:S(2)}, u32[]{:S(2)}) collective-permute-start(f32[16,96,128]{2,1,0:T(8,128)S(1)} %get-tuple-element.86.a7_ref), channel_id=1, source_target_pairs={{0,1},{1,2},{2,3},{3,4},{4,5},{5,6},{6,7},{8,9},{9,10},{10,11},{11... | collective-permute-start | bytes 2359304 | tf_op jit(solution)/shard_map/ppermute | solution.py:258
  208.3 11.2 %collective-permute-done.22.lo_ref = f32[16,8,128]{2,1,0:T(8,128)S(1)} collective-permute-done((f32[16,8,128]{2,1,0:T(8,128)S(1)}, f32[16,8,128]{2,1,0:T(8,128)S(1)}, u32[]{:S(2)}, u32[]{:S(2)}) %collective-permute-start.22) | collective-permute-done | bytes 65568 | tf_op jit(solution)/shard_map/ppermute | solution.py:258
  221.6 7.6 %shard_map.67 = (f32[16,768,128]{2,1,0:T(8,128)S(1)}, f32[16,96,128]{2,1,0:T(8,128)S(1)}, f32[16,96,128]{2,1,0:T(8,128)S(1)}) custom-call(s32[1]{0:T(128)} %bitcast.core_ref, f32[16,768,128]{2,1,0:T(8,128)S(1)} %get-tuple-element.83.d_ref, f32[16,96,128]{2,1,0:T(8,128)S(1)} %get-tuple-element.84.af_ref.a0_ref, f32[16,96,128]{2,1,0:T(8,128)S(1)} %get-tuple-element.86.a7_ref, ...), custom_call_target="tpu_custom_call" | custom-call | tf_op jit(solution)/shard_map/pallas_call | solution.py:22
  229.2 17.3 %collective-permute-start.25 = (f32[16,96,128]{2,1,0:T(8,128)S(1)}, f32[16,96,128]{2,1,0:T(8,128)S(1)}, u32[]{:S(2)}, u32[]{:S(2)}) collective-permute-start(f32[16,96,128]{2,1,0:T(8,128)S(1)} %get-tuple-element.92.af_ref.a7_ref), channel_id=1, source_target_pairs={{0,1},{1,2},{2,3},{3,4},{4,5},{5,6},{6,7},{8,9},{9,10},{10,11},{11... | collective-permute-start | bytes 2359304 | tf_op jit(solution)/shard_map/ppermute | solution.py:258
  253.7 6.7 %collective-permute-done.27.lo_ref = f32[16,8,128]{2,1,0:T(8,128)S(1)} collective-permute-done((f32[16,8,128]{2,1,0:T(8,128)S(1)}, f32[16,8,128]{2,1,0:T(8,128)S(1)}, u32[]{:S(2)}, u32[]{:S(2)}) %collective-permute-start.27) | collective-permute-done | bytes 65568 | tf_op jit(solution)/shard_map/ppermute | solution.py:258
  263.6 10.1 %shard_map.69 = (f32[16,768,128]{2,1,0:T(8,128)S(1)}, f32[16,96,128]{2,1,0:T(8,128)}, f32[16,96,128]{2,1,0:T(8,128)S(1)}, f32[16,96,128]{2,1,0:T(8,128)S(1)}, f3...) custom-call(s32[1]{0:T(128)} %bitcast.core_ref, ...), custom_call_target="tpu_custom_call" | custom-call | tf_op jit(solution)/shard_map/pallas_call | solution.py:22
  273.7 6.8 %collective-permute-done.29.h_ref = f32[16,96,128]{2,1,0:T(8,128)S(1)} collective-permute-done((f32[16,96,128]{2,1,0:T(8,128)S(1)}, f32[16,96,128]{2,1,0:T(8,128)S(1)}, u32[]{:S(2)}, u32[]{:S(2)}) %collective-permute-start.29) | collective-permute-done | bytes 786464 | tf_op jit(solution)/shard_map/ppermute | solution.py:258
  281.1 36.0 %all_to_all.10 = f32[16,2,96,128]{3,2,1,0:T(8,128)S(1)} all-to-all(f32[16,2,96,128]{3,2,1,0:T(8,128)S(1)} %get-tuple-element.104), channel_id=1, replica_groups=mesh['rows'=2,'cols'=8,'slabs'=8] {'slabs'}, dimensions={0} | all-to-all | bytes 3145728 | tf_op jit(solution)/shard_map/all_to_all | solution.py:311
  317.5 19.1 %all_to_all.11 = f32[8,2,2,96,128]{4,3,2,1,0:T(8,128)S(1)} all-to-all(f32[8,2,2,96,128]{4,3,2,1,0:T(8,128)S(1)} %broadcast_in_dim.2), channel_id=1, replica_groups=mesh['rows'=2,'cols'=8,'slabs'=8] {'slabs'}, dimensions={0} | all-to-all | bytes 3145728 | tf_op jit(solution)/shard_map/all_to_all | solution.py:318
  (65 shorter events, 59.2 us)
Async XLA Ops:
  1.8 30.2 %collective-permute-start = (f32[16,96,128]{2,1,0:T(8,128)S(1)}, f32[16,96,128]{2,1,0:T(8,128)S(1)}, u32[]{:S(2)}, u32[]{:S(2)}) collective-permute-start(f32[16,96,128]{2,1,0:T(8,128)S(1)} %prep.2.a0_ref), channel_id=1, source_target_pairs={{1,0},{2,1},{3,2},{4,3},{5,4},{6,5},{7,6},{9,8},{10,9},{11,10},{12... | collective-permute-start | bytes 2359304 | tf_op jit(solution)/shard_map/ppermute | solution.py:258
  4.5 51.5 %collective-permute-start.4 = (f32[16,96,128]{2,1,0:T(8,128)S(1)}, f32[16,96,128]{2,1,0:T(8,128)S(1)}, u32[]{:S(2)}, u32[]{:S(2)}) collective-permute-start(f32[16,96,128]{2,1,0:T(8,128)S(1)} %get-tuple-element.55.a7_ref), channel_id=1, source_target_pairs={{0,1},{1,2},{2,3},{3,4},{4,5},{5,6},{6,7},{8,9},{9,10},{10,11},{11... | collective-permute-start | bytes 2359304 | tf_op jit(solution)/shard_map/ppermute | solution.py:258
  10.6 21.3 %collective-permute-start.1 = (f32[768,128]{1,0:T(8,128)S(1)}, f32[768,128]{1,0:T(8,128)S(1)}, u32[]{:S(2)}, u32[]{:S(2)}) collective-permute-start(f32[768,128]{1,0:T(8,128)S(1)} %bitcast.35), channel_id=1, source_target_pairs={{0,64},{64,0},{1,65},{65,1},{2,66},{66,2},{3,67},{67,3},{4,68},{68... | collective-permute-start | bytes 1179656 | tf_op jit(solution)/shard_map/ppermute | solution.py:281
  10.7 17.7 %collective-permute-start.2 = (f32[16,8,128]{2,1,0:T(8,128)S(1)}, f32[16,8,128]{2,1,0:T(8,128)S(1)}, u32[]{:S(2)}, u32[]{:S(2)}) collective-permute-start(f32[16,8,128]{2,1,0:T(8,128)S(1)} %get-tuple-element.57), channel_id=1, source_target_pairs={{0,8},{8,16},{16,24},{24,32},{32,40},{40,48},{48,56},{1,9},{9,17},... | collective-permute-start | bytes 196616 | tf_op jit(solution)/shard_map/ppermute | solution.py:258
  14.2 17.7 %collective-permute-start.3 = (f32[16,8,128]{2,1,0:T(8,128)S(1)}, f32[16,8,128]{2,1,0:T(8,128)S(1)}, u32[]{:S(2)}, u32[]{:S(2)}) collective-permute-start(f32[16,8,128]{2,1,0:T(8,128)S(1)} %get-tuple-element.58), channel_id=1, source_target_pairs={{8,0},{16,8},{24,16},{32,24},{40,32},{48,40},{56,48},{9,1},{17,9},... | collective-permute-start | bytes 196616 | tf_op jit(solution)/shard_map/ppermute | solution.py:258
  39.6 35.9 %collective-permute-start.5 = (f32[16,96,128]{2,1,0:T(8,128)S(1)}, f32[16,96,128]{2,1,0:T(8,128)S(1)}, u32[]{:S(2)}, u32[]{:S(2)}) collective-permute-start(f32[16,96,128]{2,1,0:T(8,128)S(1)} %get-tuple-element.64.af_ref.a7_ref), channel_id=1, source_target_pairs={{0,1},{1,2},{2,3},{3,4},{4,5},{5,6},{6,7},{8,9},{9,10},{10,11},{11... | collective-permute-start | bytes 2359304 | tf_op jit(solution)/shard_map/ppermute | solution.py:258
  56.5 35.5 %collective-permute-start.9 = (f32[16,96,128]{2,1,0:T(8,128)S(1)}, f32[16,96,128]{2,1,0:T(8,128)S(1)}, u32[]{:S(2)}, u32[]{:S(2)}) collective-permute-start(f32[16,96,128]{2,1,0:T(8,128)S(1)} %get-tuple-element.65.a0_ref), channel_id=1, source_target_pairs={{1,0},{2,1},{3,2},{4,3},{5,4},{6,5},{7,6},{9,8},{10,9},{11,10},{12... | collective-permute-start | bytes 2359304 | tf_op jit(solution)/shard_map/ppermute | solution.py:258
  57.8 17.7 %collective-permute-start.6 = (f32[768,128]{1,0:T(8,128)S(1)}, f32[768,128]{1,0:T(8,128)S(1)}, u32[]{:S(2)}, u32[]{:S(2)}) collective-permute-start(f32[768,128]{1,0:T(8,128)S(1)} %get-tuple-element.66), channel_id=1, source_target_pairs={{0,64},{64,0},{1,65},{65,1},{2,66},{66,2},{3,67},{67,3},{4,68},{68... | collective-permute-start | bytes 1179656 | tf_op jit(solution)/shard_map/ppermute | solution.py:281
  57.9 15.1 %collective-permute-start.7 = (f32[16,8,128]{2,1,0:T(8,128)S(1)}, f32[16,8,128]{2,1,0:T(8,128)S(1)}, u32[]{:S(2)}, u32[]{:S(2)}) collective-permute-start(f32[16,8,128]{2,1,0:T(8,128)S(1)} %get-tuple-element.67), channel_id=1, source_target_pairs={{0,8},{8,16},{16,24},{24,32},{32,40},{40,48},{48,56},{1,9},{9,17},... | collective-permute-start | bytes 196616 | tf_op jit(solution)/shard_map/ppermute | solution.py:258
  60.5 15.0 %collective-permute-start.8 = (f32[16,8,128]{2,1,0:T(8,128)S(1)}, f32[16,8,128]{2,1,0:T(8,128)S(1)}, u32[]{:S(2)}, u32[]{:S(2)}) collective-permute-start(f32[16,8,128]{2,1,0:T(8,128)S(1)} %get-tuple-element.68), channel_id=1, source_target_pairs={{8,0},{16,8},{24,16},{32,24},{40,32},{48,40},{56,48},{9,1},{17,9},... | collective-permute-start | bytes 196616 | tf_op jit(solution)/shard_map/ppermute | solution.py:258
  83.2 44.3 %collective-permute-start.10 = (f32[16,96,128]{2,1,0:T(8,128)S(1)}, f32[16,96,128]{2,1,0:T(8,128)S(1)}, u32[]{:S(2)}, u32[]{:S(2)}) collective-permute-start(f32[16,96,128]{2,1,0:T(8,128)S(1)} %get-tuple-element.70.af_ref.a0_ref), channel_id=1, source_target_pairs={{1,0},{2,1},{3,2},{4,3},{5,4},{6,5},{7,6},{9,8},{10,9},{11,10},{12... | collective-permute-start | bytes 2359304 | tf_op jit(solution)/shard_map/ppermute | solution.py:258
  92.5 59.9 %collective-permute-start.14 = (f32[16,96,128]{2,1,0:T(8,128)S(1)}, f32[16,96,128]{2,1,0:T(8,128)S(1)}, u32[]{:S(2)}, u32[]{:S(2)}) collective-permute-start(f32[16,96,128]{2,1,0:T(8,128)S(1)} %get-tuple-element.72.a7_ref), channel_id=1, source_target_pairs={{0,1},{1,2},{2,3},{3,4},{4,5},{5,6},{6,7},{8,9},{9,10},{10,11},{11... | collective-permute-start | bytes 2359304 | tf_op jit(solution)/shard_map/ppermute | solution.py:258
  109.6 17.9 %collective-permute-start.11 = (f32[768,128]{1,0:T(8,128)S(1)}, f32[768,128]{1,0:T(8,128)S(1)}, u32[]{:S(2)}, u32[]{:S(2)}) collective-permute-start(f32[768,128]{1,0:T(8,128)S(1)} %get-tuple-element.73), channel_id=1, source_target_pairs={{0,64},{64,0},{1,65},{65,1},{2,66},{66,2},{3,67},{67,3},{4,68},{68... | collective-permute-start | bytes 1179656 | tf_op jit(solution)/shard_map/ppermute | solution.py:281
  109.7 15.7 %collective-permute-start.12 = (f32[16,8,128]{2,1,0:T(8,128)S(1)}, f32[16,8,128]{2,1,0:T(8,128)S(1)}, u32[]{:S(2)}, u32[]{:S(2)}) collective-permute-start(f32[16,8,128]{2,1,0:T(8,128)S(1)} %get-tuple-element.74), channel_id=1, source_target_pairs={{0,8},{8,16},{16,24},{24,32},{32,40},{40,48},{48,56},{1,9},{9,17},... | collective-permute-start | bytes 196616 | tf_op jit(solution)/shard_map/ppermute | solution.py:258
  111.2 16.3 %collective-permute-start.13 = (f32[16,8,128]{2,1,0:T(8,128)S(1)}, f32[16,8,128]{2,1,0:T(8,128)S(1)}, u32[]{:S(2)}, u32[]{:S(2)}) collective-permute-start(f32[16,8,128]{2,1,0:T(8,128)S(1)} %get-tuple-element.75), channel_id=1, source_target_pairs={{8,0},{16,8},{24,16},{32,24},{40,32},{48,40},{56,48},{9,1},{17,9},... | collective-permute-start | bytes 196616 | tf_op jit(solution)/shard_map/ppermute | solution.py:258
  135.1 36.4 %collective-permute-start.15 = (f32[16,96,128]{2,1,0:T(8,128)S(1)}, f32[16,96,128]{2,1,0:T(8,128)S(1)}, u32[]{:S(2)}, u32[]{:S(2)}) collective-permute-start(f32[16,96,128]{2,1,0:T(8,128)S(1)} %get-tuple-element.78.af_ref.a7_ref), channel_id=1, source_target_pairs={{0,1},{1,2},{2,3},{3,4},{4,5},{5,6},{6,7},{8,9},{9,10},{10,11},{11... | collective-permute-start | bytes 2359304 | tf_op jit(solution)/shard_map/ppermute | solution.py:258
  152.9 35.2 %collective-permute-start.19 = (f32[16,96,128]{2,1,0:T(8,128)S(1)}, f32[16,96,128]{2,1,0:T(8,128)S(1)}, u32[]{:S(2)}, u32[]{:S(2)}) collective-permute-start(f32[16,96,128]{2,1,0:T(8,128)S(1)} %get-tuple-element.79.a0_ref), channel_id=1, source_target_pairs={{1,0},{2,1},{3,2},{4,3},{5,4},{6,5},{7,6},{9,8},{10,9},{11,10},{12... | collective-permute-start | bytes 2359304 | tf_op jit(solution)/shard_map/ppermute | solution.py:258
  154.2 17.4 %collective-permute-start.16 = (f32[768,128]{1,0:T(8,128)S(1)}, f32[768,128]{1,0:T(8,128)S(1)}, u32[]{:S(2)}, u32[]{:S(2)}) collective-permute-start(f32[768,128]{1,0:T(8,128)S(1)} %get-tuple-element.80), channel_id=1, source_target_pairs={{0,64},{64,0},{1,65},{65,1},{2,66},{66,2},{3,67},{67,3},{4,68},{68... | collective-permute-start | bytes 1179656 | tf_op jit(solution)/shard_map/ppermute | solution.py:281
  179.2 42.4 %collective-permute-start.20 = (f32[16,96,128]{2,1,0:T(8,128)S(1)}, f32[16,96,128]{2,1,0:T(8,128)S(1)}, u32[]{:S(2)}, u32[]{:S(2)}) collective-permute-start(f32[16,96,128]{2,1,0:T(8,128)S(1)} %get-tuple-element.84.af_ref.a0_ref), channel_id=1, source_target_pairs={{1,0},{2,1},{3,2},{4,3},{5,4},{6,5},{7,6},{9,8},{10,9},{11,10},{12... | collective-permute-start | bytes 2359304 | tf_op jit(solution)/shard_map/ppermute | solution.py:258
  188.6 57.9 %collective-permute-start.24 = (f32[16,96,128]{2,1,0:T(8,128)S(1)}, f32[16,96,128]{2,1,0:T(8,128)S(1)}, u32[]{:S(2)}, u32[]{:S(2)}) collective-permute-start(f32[16,96,128]{2,1,0:T(8,128)S(1)} %get-tuple-element.86.a7_ref), channel_id=1, source_target_pairs={{0,1},{1,2},{2,3},{3,4},{4,5},{5,6},{6,7},{8,9},{9,10},{10,11},{11... | collective-permute-start | bytes 2359304 | tf_op jit(solution)/shard_map/ppermute | solution.py:258
  205.6 16.0 %collective-permute-start.21 = (f32[768,128]{1,0:T(8,128)S(1)}, f32[768,128]{1,0:T(8,128)S(1)}, u32[]{:S(2)}, u32[]{:S(2)}) collective-permute-start(f32[768,128]{1,0:T(8,128)S(1)} %get-tuple-element.87), channel_id=1, source_target_pairs={{0,64},{64,0},{1,65},{65,1},{2,66},{66,2},{3,67},{67,3},{4,68},{68... | collective-permute-start | bytes 1179656 | tf_op jit(solution)/shard_map/ppermute | solution.py:281
  229.2 34.4 %collective-permute-start.25 = (f32[16,96,128]{2,1,0:T(8,128)S(1)}, f32[16,96,128]{2,1,0:T(8,128)S(1)}, u32[]{:S(2)}, u32[]{:S(2)}) collective-permute-start(f32[16,96,128]{2,1,0:T(8,128)S(1)} %get-tuple-element.92.af_ref.a7_ref), channel_id=1, source_target_pairs={{0,1},{1,2},{2,3},{3,4},{4,5},{5,6},{6,7},{8,9},{9,10},{10,11},{11... | collective-permute-start | bytes 2359304 | tf_op jit(solution)/shard_map/ppermute | solution.py:258
  247.0 33.4 %collective-permute-start.29 = (f32[16,96,128]{2,1,0:T(8,128)S(1)}, f32[16,96,128]{2,1,0:T(8,128)S(1)}, u32[]{:S(2)}, u32[]{:S(2)}) collective-permute-start(f32[16,96,128]{2,1,0:T(8,128)S(1)} %get-tuple-element.93.a0_ref), channel_id=1, source_target_pairs={{1,0},{2,1},{3,2},{4,3},{5,4},{6,5},{7,6},{9,8},{10,9},{11,10},{12... | collective-permute-start | bytes 2359304 | tf_op jit(solution)/shard_map/ppermute | solution.py:258
  248.3 15.3 %collective-permute-start.26 = (f32[768,128]{1,0:T(8,128)S(1)}, f32[768,128]{1,0:T(8,128)S(1)}, u32[]{:S(2)}, u32[]{:S(2)}) collective-permute-start(f32[768,128]{1,0:T(8,128)S(1)} %get-tuple-element.94), channel_id=1, source_target_pairs={{0,64},{64,0},{1,65},{65,1},{2,66},{66,2},{3,67},{67,3},{4,68},{68... | collective-permute-start | bytes 1179656 | tf_op jit(solution)/shard_map/ppermute | solution.py:281
  (8 other events, 123.8 us)
